TPU v7x, 8 devices: a whole 2x2x1 slice. The times are simulated.
8 devices in a mesh: dp: 2 (over z, y), tp: 4 (over x, core).
Axes of the slice: x: 2, y: 2, z: 1, core: 2. Of those that a mesh axis runs over, the one named last changes fastest.
Arguments:
- patches: bfloat16 [128, 256, 768], P('dp', 'tp'), parts along dimension 0
- patch_w: bfloat16 [768, 768], replicated
- patch_b: bfloat16 [768], replicated
- pos_emb: bfloat16 [256, 768], P('tp')
- ln_scale: bfloat16 [2, 768], replicated
- ln_bias: bfloat16 [2, 768], replicated
- qkv_w: bfloat16 [3, 768, 12, 64], P(None, None, 'tp')
- qkv_b: bfloat16 [3, 12, 64], P(None, 'tp')
- out_w: bfloat16 [12, 64, 768], P('tp')
- out_b: bfloat16 [768], replicated
- fc1_w: bfloat16 [768, 3072], P(None, 'tp')
- fc1_b: bfloat16 [3072], P('tp')
- fc2_w: bfloat16 [3072, 768], P('tp')
- fc2_b: bfloat16 [768], replicated
- d_out: bfloat16 [128, 256, 768], P('dp', 'tp'), parts along dimension 0
Outputs:
- output 1: bfloat16 [128, 256, 768], P('dp', 'tp'), parts along dimension 0
- output 2: bfloat16 [1536, 768], P('dp'), parts along dimension 0
- output 3: bfloat16 [1536], P('dp'), parts along dimension 0
- output 4: bfloat16 [512, 768], P(('dp', 'tp')), parts along dimension 0
- output 5: bfloat16 [4, 768], P('dp'), parts along dimension 0
- output 6: bfloat16 [4, 768], P('dp'), parts along dimension 0
- output 7: bfloat16 [6, 768, 12, 64], P('dp', None, 'tp'), parts along dimension 0
- output 8: bfloat16 [6, 12, 64], P('dp', 'tp'), parts along dimension 0
- output 9: bfloat16 [24, 64, 768], P(('dp', 'tp')), parts along dimension 0
- output 10: bfloat16 [1536], P('dp'), parts along dimension 0
- output 11: bfloat16 [1536, 3072], P('dp', 'tp'), parts along dimension 0
- output 12: bfloat16 [6144], P(('dp', 'tp')), parts along dimension 0
- output 13: bfloat16 [6144, 768], P(('dp', 'tp')), parts along dimension 0
- output 14: bfloat16 [1536], P('dp'), parts along dimension 0
There are 2 independent parts. A program takes and returns all parts, laid end to end along the dimension named above; an argument that names none is the same for every part.
All inputs are finite; a program needn't handle non-finite values.
Results may differ from a plain program's by a relative error of at most 0.0189636.
Values are sent between devices in bfloat16 or wider.
A program may use at most 1 GiB of HBM per device.

v0:
```python
import jax
import jax.numpy as jnp
from jax import lax
from jax.sharding import PartitionSpec as P

LN_EPS = 1e-6


def layer_norm(x_val, scale_f, bias_f):
    row_mean = jnp.mean(x_val, axis=-1, keepdims=True)
    centered = x_val - row_mean
    row_var = jnp.mean(centered * centered, axis=-1, keepdims=True)
    return centered * lax.rsqrt(row_var + LN_EPS) * scale_f + bias_f


def gelu_tanh(pre_act):
    return jax.nn.gelu(pre_act, approximate=True)


def group_step(patches, patch_w, patch_b, pos_emb, ln_scale, ln_bias, qkv_w, qkv_b, out_w, out_b, fc1_w, fc1_b, fc2_w, fc2_b, d_out):
    wide = jnp.float32
    half = jnp.bfloat16
    scale = qkv_w.shape[-1] ** -0.5
    ln_scale_f = ln_scale.astype(wide)
    ln_bias_f = ln_bias.astype(wide)
    emb = jnp.einsum('btp,pd->btd', patches, patch_w, preferred_element_type=wide)
    emb_f = (emb + patch_b.astype(wide) + pos_emb.astype(wide)).astype(half).astype(wide)
    h_one_f, ln_one_vjp = jax.vjp(layer_norm, emb_f, ln_scale_f[0], ln_bias_f[0])
    h_one_all = lax.all_gather(h_one_f.astype(half), 'tp', axis=1, tiled=True)
    qkv = jnp.einsum('btd,sdhc->btshc', h_one_all, qkv_w, preferred_element_type=wide)
    qkv = (qkv + qkv_b.astype(wide)).astype(half)
    query = qkv[:, :, 0]
    keys_all = qkv[:, :, 1]
    values = qkv[:, :, 2]
    scores = jnp.einsum('bqhc,bkhc->bhqk', query, keys_all, preferred_element_type=wide) * scale
    probs = jax.nn.softmax(scores, axis=-1)
    probs_h = probs.astype(half)
    context = jnp.einsum('bhqk,bkhc->bqhc', probs_h, values, preferred_element_type=wide).astype(half)
    attn_part = jnp.einsum('crid,ide->cre', context, out_w, preferred_element_type=wide)
    attn_out = lax.psum_scatter(attn_part, 'tp', scatter_dimension=1, tiled=True)
    x_one_f = (emb_f + (attn_out + out_b.astype(wide))).astype(half).astype(wide)
    h_two_f, ln_two_vjp = jax.vjp(layer_norm, x_one_f, ln_scale_f[1], ln_bias_f[1])
    h_two_all = lax.all_gather(h_two_f.astype(half), 'tp', axis=1, tiled=True)
    pre_act = jnp.einsum('btd,df->btf', h_two_all, fc1_w, preferred_element_type=wide) + fc1_b.astype(wide)
    hidden_f, gelu_vjp = jax.vjp(gelu_tanh, pre_act)
    hidden = hidden_f.astype(half)
    mlp_part = jnp.einsum('btf,fd->btd', hidden, fc2_w, preferred_element_type=wide)
    mlp_out = lax.psum_scatter(mlp_part, 'tp', scatter_dimension=1, tiled=True)
    x_two = (x_one_f + (mlp_out + fc2_b.astype(wide))).astype(half)
    d_two_f = d_out.astype(wide)
    d_fc2_b = jnp.sum(d_two_f, axis=(0, 1))
    d_out_all = lax.all_gather(d_out, 'tp', axis=1, tiled=True)
    d_fc2_w = jnp.einsum('btf,btd->fd', hidden, d_out_all, preferred_element_type=wide)
    d_hidden = jnp.einsum('btd,fd->btf', d_out_all, fc2_w, preferred_element_type=wide).astype(half)
    d_pre = gelu_vjp(d_hidden.astype(wide))[0]
    d_fc1_b = jnp.sum(d_pre, axis=(0, 1))
    d_pre_h = d_pre.astype(half)
    d_fc1_w = jnp.einsum('btd,btf->df', h_two_all, d_pre_h, preferred_element_type=wide)
    d_h_two_part = jnp.einsum('btf,df->btd', d_pre_h, fc1_w, preferred_element_type=wide)
    d_h_two = lax.psum_scatter(d_h_two_part, 'tp', scatter_dimension=1, tiled=True).astype(half)
    d_x_ln, d_ln2_scale, d_ln2_bias = ln_two_vjp(d_h_two.astype(wide))
    d_x_one = (d_two_f + d_x_ln).astype(half)
    d_out_b = jnp.sum(d_x_one, axis=(0, 1), dtype=wide)
    d_x_one_all = lax.all_gather(d_x_one, 'tp', axis=1, tiled=True)
    d_out_w = jnp.einsum('crid,cre->ide', context, d_x_one_all, preferred_element_type=wide)
    d_context = jnp.einsum('cre,ide->crid', d_x_one_all, out_w, preferred_element_type=wide).astype(half)
    d_values = jnp.einsum('bhqk,bqhc->bkhc', probs_h, d_context, preferred_element_type=wide).astype(half)
    d_probs = jnp.einsum('bqhc,bkhc->bhqk', d_context, values, preferred_element_type=wide).astype(half).astype(wide)
    d_scores = probs * (d_probs - jnp.sum(d_probs * probs, axis=-1, keepdims=True))
    d_scores_h = (d_scores * scale).astype(half)
    d_query = jnp.einsum('bhqk,bkhc->bqhc', d_scores_h, keys_all, preferred_element_type=wide).astype(half)
    d_keys = jnp.einsum('bhqk,bqhc->bkhc', d_scores_h, query, preferred_element_type=wide).astype(half)
    d_qkv = jnp.stack([d_query, d_keys, d_values], axis=2)
    d_qkv_b = jnp.sum(d_qkv, axis=(0, 1), dtype=wide)
    d_qkv_w = jnp.einsum('btd,btshc->sdhc', h_one_all, d_qkv, preferred_element_type=wide)
    d_h_one_part = jnp.einsum('btshc,sdhc->btd', d_qkv, qkv_w, preferred_element_type=wide)
    d_h_one = lax.psum_scatter(d_h_one_part, 'tp', scatter_dimension=1, tiled=True).astype(half)
    d_emb_ln, d_ln1_scale, d_ln1_bias = ln_one_vjp(d_h_one.astype(wide))
    d_emb = (d_x_one.astype(wide) + d_emb_ln).astype(half)
    d_pos = jnp.sum(d_emb, axis=0, dtype=wide)
    d_patch_b = jnp.sum(d_emb, axis=(0, 1), dtype=wide)
    d_patch_w = jnp.einsum('btp,btd->pd', patches, d_emb, preferred_element_type=wide)
    d_ln_scale = jnp.stack([d_ln1_scale, d_ln2_scale])
    d_ln_bias = jnp.stack([d_ln1_bias, d_ln2_bias])
    d_patch_w, d_patch_b, d_ln_scale, d_ln_bias, d_out_b, d_fc2_b = lax.psum((d_patch_w, d_patch_b, d_ln_scale, d_ln_bias, d_out_b, d_fc2_b), 'tp')
    return (x_two, d_patch_w.astype(half), d_patch_b.astype(half), d_pos.astype(half), d_ln_scale.astype(half), d_ln_bias.astype(half), d_qkv_w.astype(half), d_qkv_b.astype(half), d_out_w.astype(half), d_out_b.astype(half), d_fc1_w.astype(half), d_fc1_b.astype(half), d_fc2_w.astype(half), d_fc2_b.astype(half))


def solution(mesh):
    in_specs = (P('dp', 'tp', None), P(), P(), P('tp', None), P(), P(), P(None, None, 'tp', None), P(None, 'tp', None), P('tp', None, None), P(), P(None, 'tp'), P('tp'), P('tp', None), P(), P('dp', 'tp', None))
    out_specs = (P('dp', 'tp', None), P('dp', None), P('dp'), P(('dp', 'tp'), None), P('dp', None), P('dp', None), P('dp', None, 'tp', None), P('dp', 'tp', None), P(('dp', 'tp'), None, None), P('dp'), P('dp', 'tp'), P(('dp', 'tp')), P(('dp', 'tp'), None), P('dp'))
    return jax.shard_map(group_step, mesh=mesh, in_specs=in_specs, out_specs=out_specs, check_vma=False)
```

profile of v0, /device:TPU:0, one launch (start us, length us, event | category | flops | bytes accessed | tf_op | source)
XLA Modules:
  0.0 2523.2 jit_solution(10624209444983881440)
XLA Ops:
  27.2 155.5 %all-gather.5.cloned.1.call-done = bf16[64,256,768]{2,1,0:T(8,128)(2,1)} async-done(((bf16[64,64,768]{2,1,0:T(8,128)(2,1)}), bf16[64,256,768]{2,1,0:T(8,128)(2,1)}) %all-gather.5.cloned.1.call-update) | async-done | bytes 25165840 | tf_op jit(solution)/shard_map/all_gather | solution.py:29
  182.7 43.3 %add_convert_fusion = bf16[64,256,3,3,64]{1,4,3,2,0:T(8,128)(2,1)} fusion(f32[3,3,64]{2,1,0:T(4,128)S(1)} %convert_element_type.174, bf16[64,256,768]{2,1,0:T(8,128)(2,1)} %all-gather.5.cloned.1.call-done, bf16[3,768,3,64]{1,3,2,0:T(8,128)(2,1)S(1)} %copy-done.34), kind=kOutput, calls=%fused_computation.24 | convolution fusion | flops 14514388992 | bytes 44927232 | tf_op jit(solution)/shard_map/btd,sdhc->btshc/dot_general | solution.py:30
  247.9 54.1 %fusion.118 = (f32[64,3,256]{2,1,0:T(4,128)S(1)}, f32[64,3,256,256]{2,3,1,0:T(8,128)}) fusion(f32[64,3,256,256]{2,3,1,0:T(8,128)} %fusion.69), kind=kOutput, calls=%fused_computation.150 | output fusion | flops 50331904 | bytes 100859904 | tf_op jit(solution)/shard_map/sub | solution.py:36
  302.0 22.0 fusion.70
  346.2 325.6 %reduce-scatter.5.cloned.1.call-done = f32[64,64,768]{2,1,0:T(8,128)} async-done(((f32[64,256,768]{2,1,0:T(8,128)}), f32[64,64,768]{2,1,0:T(8,128)}) %reduce-scatter.5.cloned.1.call-update) | async-done | bytes 12582928 | tf_op jit(solution)/shard_map/reduce_scatter | solution.py:40
  688.0 152.3 %all-gather.7.cloned.1.call-done = bf16[64,256,768]{2,1,0:T(8,128)(2,1)} async-done(((bf16[64,64,768]{2,1,0:T(8,128)(2,1)}), bf16[64,256,768]{2,1,0:T(8,128)(2,1)}) %all-gather.7.cloned.1.call-update) | async-done | bytes 25165840 | tf_op jit(solution)/shard_map/all_gather | solution.py:43
  840.3 31.5 %fusion.99 = f32[64,256,768]{2,1,0:T(8,128)} fusion(bf16[64,256,768]{2,1,0:T(8,128)(2,1)} %all-gather.7.cloned.1.call-done, bf16[768,768]{1,0:T(8,128)(2,1)S(1)} %copy-done.33), kind=kOutput, calls=%fused_computation.120 | convolution fusion | flops 19327352832 | bytes 76677120 | tf_op jit(solution)/shard_map/btd,df->btf/dot_general | solution.py:44
  871.7 122.7 %all-gather.9.cloned.1.call-done = bf16[64,256,768]{2,1,0:T(8,128)(2,1)} async-done(((bf16[64,64,768]{2,1,0:T(8,128)(2,1)}), bf16[64,256,768]{2,1,0:T(8,128)(2,1)}) %all-gather.9.cloned.1.call-update) | async-done | bytes 25165840 | tf_op jit(solution)/shard_map/all_gather | solution.py:52
  994.5 59.9 %fusion.119 = (bf16[768]{0:T(1024)(128)(2,1)}, bf16[64,256,768]{2,1,0:T(8,128)(2,1)}) fusion(f32[64,256,768]{2,1,0:T(8,128)} %fusion.99, f32[768]{0:T(1024)S(1)} %convert_element_type.183, bf16[64,256,768]{2,1,0:T(8,128)(2,1)} %all-gather.9.cloned.1.call-done, bf16[768,768]{1,0:T(8,128)(2,1)S(1)} %copy-done), kind=kOutput, calls=%fused_computation.151 | convolution fusion | flops 19629342720 | bytes 101847552 | tf_op jit(solution)/shard_map/btd,fd->btf/dot_general | solution.py:54
  1054.3 31.6 %fusion.59 = f32[64,256,768]{2,1,0:T(8,128)} fusion(bf16[64,256,768]{2,1,0:T(8,128)(2,1)} %get-tuple-element.61, bf16[768,768]{1,0:T(8,128)(2,1)S(1)} %copy-done.33), kind=kOutput, calls=%fused_computation.89 | convolution fusion | flops 19327352832 | bytes 76677120 | tf_op jit(solution)/shard_map/btf,df->btd/dot_general | solution.py:59
  1086.1 42.7 %fusion.96 = f32[64,256,768]{2,1,0:T(8,128)} fusion(bf16[768,768]{1,0:T(8,128)(2,1)S(1)} %copy-done, f32[64,256,768]{2,1,0:T(8,128)} %fusion.99, f32[768]{0:T(1024)S(1)} %convert_element_type.183), kind=kOutput, calls=%fused_computation.117 | convolution fusion | flops 19453181952 | bytes 101846016 | tf_op jit(solution)/shard_map/btf,fd->btd/dot_general | solution.py:47
  1129.4 282.9 %reduce-scatter.9.cloned.1.call-done = f32[64,64,768]{2,1,0:T(8,128)} async-done(((f32[64,256,768]{2,1,0:T(8,128)}), f32[64,64,768]{2,1,0:T(8,128)}) %reduce-scatter.9.cloned.1.call-update) | async-done | bytes 12582928 | tf_op jit(solution)/shard_map/reduce_scatter | solution.py:60
  1434.0 306.8 %reduce-scatter.7.cloned.1.call-done = f32[64,64,768]{2,1,0:T(8,128)} async-done(((f32[64,256,768]{2,1,0:T(8,128)}), f32[64,64,768]{2,1,0:T(8,128)}) %reduce-scatter.7.cloned.1.call-update) | async-done | bytes 12582928 | tf_op jit(solution)/shard_map/reduce_scatter | solution.py:48
  1758.1 152.9 %all-gather.11.cloned.1.call-done = bf16[64,256,768]{2,1,0:T(8,128)(2,1)} async-done(((bf16[64,64,768]{2,1,0:T(8,128)(2,1)}), bf16[64,256,768]{2,1,0:T(8,128)(2,1)}) %all-gather.11.cloned.1.call-update) | async-done | bytes 25165840 | tf_op jit(solution)/shard_map/all_gather | solution.py:64
  1911.0 25.6 %fusion.75 = bf16[64,256,3,64]{1,3,2,0:T(8,128)(2,1)} fusion(bf16[64,256,768]{2,1,0:T(8,128)(2,1)} %all-gather.11.cloned.1.call-done, bf16[3,64,768]{2,1,0:T(8,128)(2,1)S(1)} %copy-done.37), kind=kOutput, calls=%fused_computation.108 | convolution fusion | flops 4834983936 | bytes 31752192 | tf_op jit(solution)/shard_map/cre,ide->crid/dot_general | solution.py:66
  1936.6 22.1 convert_bitcast_fusion
  1974.6 52.0 %convert_bitcast_fusion.2 = bf16[64,256,1,3,64]{1,4,3,0,2:T(8,128)(2,1)} fusion(bf16[64,3,256,256]{2,3,1,0:T(8,128)(2,1)} %convolution_convert_fusion, bf16[64,256,3,3,64]{1,4,3,2,0:T(8,128)(2,1)} %add_convert_fusion, f32[64,3,256,256]{2,3,1,0:T(8,128)} %get-tuple-element.59, f32[64,3,256]{2,1,0:T(4,128)S(1)} %copy-done.18), kind=kOutput, calls=%fused_computation.105 | convolution fusion | flops 1727054080 | bytes 164102144 | tf_op jit(solution)/shard_map/bhqk,bkhc->bqhc/dot_general | solution.py:71
  2026.5 52.0 %convert_bitcast_fusion.1 = bf16[64,256,1,3,64]{1,4,3,0,2:T(8,128)(2,1)} fusion(bf16[64,3,256,256]{2,3,1,0:T(8,128)(2,1)} %convolution_convert_fusion, bf16[64,256,3,3,64]{1,4,3,2,0:T(8,128)(2,1)} %add_convert_fusion, f32[64,3,256,256]{2,3,1,0:T(8,128)} %get-tuple-element.59, f32[64,3,256]{2,1,0:T(4,128)S(1)} %copy-done.18), kind=kOutput, calls=%fused_computation.104 | convolution fusion | flops 1727054080 | bytes 164102144 | tf_op jit(solution)/shard_map/bhqk,bqhc->bkhc/dot_general | solution.py:72
  2078.5 28.8 %convolution_bitcast_fusion = f32[64,256,768]{2,1,0:T(8,128)} fusion(bf16[3,768,3,64]{1,3,2,0:T(8,128)(2,1)S(1)} %copy-done.35, bf16[64,256,1,3,64]{1,4,3,0,2:T(8,128)(2,1)} %convert_bitcast_fusion, bf16[64,256,1,3,64]{1,4,3,0,2:T(8,128)(2,1)} %convert_bitcast_fusion.1, bf16[64,256,1,3,64]{1,4,3,0,2:T(8,128)(2,1)} %convert_bitcast_fusion.2), kind=kOutput, calls=%fused_computation.61 | convolution fusion | flops 14514388992 | bytes 70090752 | tf_op jit(solution)/shard_map/btshc,sdhc->btd/dot_general | solution.py:76
  2107.3 26.8 %bitcast_convert_fusion.1 = bf16[768,768]{1,0:T(8,128)(2,1)} fusion(bf16[64,256,768]{2,1,0:T(8,128)(2,1)} %all-gather.7.cloned.1.call-done, bf16[64,256,768]{2,1,0:T(8,128)(2,1)} %get-tuple-element.61), kind=kOutput, calls=%fused_computation.110 | convolution fusion | flops 19327942656 | bytes 51511296 | tf_op jit(solution)/shard_map/btd,btf->df/dot_general | solution.py:58
  2134.2 35.8 %bitcast_convert_fusion = bf16[768,768]{1,0:T(8,128)(2,1)} fusion(bf16[64,256,768]{2,1,0:T(8,128)(2,1)} %all-gather.9.cloned.1.call-done, f32[64,256,768]{2,1,0:T(8,128)} %fusion.99, f32[768]{0:T(1024)S(1)} %copy-done.28), kind=kOutput, calls=%fused_computation.109 | convolution fusion | flops 19453771776 | bytes 76680192 | tf_op jit(solution)/shard_map/btf,btd->fd/dot_general | solution.py:53
  2189.6 26.7 %fusion.82 = bf16[3,768,3,64]{1,3,2,0:T(8,128)(2,1)} fusion(bf16[64,256,768]{2,1,0:T(8,128)(2,1)} %all-gather.5.cloned.1.call-done, bf16[64,256,1,3,64]{1,4,3,0,2:T(8,128)(2,1)} %convert_bitcast_fusion, bf16[64,256,1,3,64]{1,4,3,0,2:T(8,128)(2,1)} %convert_bitcast_fusion.1, bf16[64,256,1,3,64]{1,4,3,0,2:T(8,128)(2,1)} %convert_bitcast_fusion.2), kind=kOutput, calls=%fused_computation.113 | convolution fusion | flops 14514831360 | bytes 44924928 | tf_op jit(solution)/shard_map/btd,btshc->sdhc/dot_general | solution.py:75
  2216.2 217.4 %reduce-scatter.11.cloned.1.call-done = f32[64,64,768]{2,1,0:T(8,128)} async-done(((f32[64,256,768]{2,1,0:T(8,128)}), f32[64,64,768]{2,1,0:T(8,128)}) %reduce-scatter.11.cloned.1.call-update) | async-done | bytes 12582928 | tf_op jit(solution)/shard_map/reduce_scatter | solution.py:77
  2468.2 45.6 %all-reduce.2 = (bf16[768,768]{0,1:T(8,128)(2,1)}, bf16[768]{0:T(1024)(128)(2,1)}, bf16[2,768]{1,0:T(2,128)(2,1)}, bf16[2,768]{1,0:T(2,128)(2,1)}, bf16[768]{0:T(1024)(128)(2,1)}, /*index=5*/bf16[768]{0:T(1024)(128)(2,1)}) all-reduce(f32[768,768]{0,1:T(8,128)S(1)} %convolution_bitcast_fusion.2, ...), channel_id=1, replica_groups=mesh['dp'=2,'tp'=4] {'tp'}, use_global_device_ids=true, to_apply=%region_15.0 | all-reduce | flops 595200 | bytes 3571200 | tf_op jit(solution)/shard_map/psum | solution.py:85
  (160 shorter events, 192.0 us)
Async XLA Ops:
  7.2 987.3 %copy-start = (bf16[768,768]{1,0:T(8,128)(2,1)S(1)}, bf16[768,768]{1,0:T(8,128)(2,1)}, u32[]{:S(2)}) copy-start(bf16[768,768]{1,0:T(8,128)(2,1)} %param.27) | copy-start | bytes 3538948
  7.2 175.5 %all-gather.5.cloned.1.call-start = ((), (), s32[]{:S(2)}) async-start(), calls=%async_computation.4 | async-start | bytes 31457280 | tf_op jit(solution)/shard_map/all_gather | solution.py:29
  18.5 164.3 %copy-start.34 = (bf16[3,768,3,64]{1,3,2,0:T(8,128)(2,1)S(1)}, bf16[3,768,3,64]{1,3,2,0:T(8,128)(2,1)}, u32[]{:S(2)}) copy-start(bf16[3,768,3,64]{1,3,2,0:T(8,128)(2,1)} %param.21) | copy-start | bytes 2654212
  27.0 644.8 %reduce-scatter.5.cloned.1.call-start = ((), (), s32[]{:S(2)}) async-start(), calls=%async_computation.5 | async-start | bytes 62914560 | tf_op jit(solution)/shard_map/reduce_scatter | solution.py:40
  345.5 494.8 %all-gather.7.cloned.1.call-start = ((), (), s32[]{:S(2)}) async-start(), calls=%async_computation.6 | async-start | bytes 31457280 | tf_op jit(solution)/shard_map/all_gather | solution.py:43
  346.2 336.7 %copy-start.19 = (f32[768]{0:T(1024)S(1)}, f32[768]{0:T(1024)}, u32[]{:S(2)}) copy-start(f32[768]{0:T(1024)} %get-tuple-element.63) | copy-start | bytes 9220
  346.2 336.7 %copy-start.23 = (f32[768]{0:T(1024)S(1)}, f32[768]{0:T(1024)}, u32[]{:S(2)}) copy-start(f32[768]{0:T(1024)} %get-tuple-element.38) | copy-start | bytes 9220
  682.9 157.4 %copy-start.33 = (bf16[768,768]{1,0:T(8,128)(2,1)S(1)}, bf16[768,768]{1,0:T(8,128)(2,1)}, u32[]{:S(2)}) copy-start(bf16[768,768]{1,0:T(8,128)(2,1)} %param.25) | copy-start | bytes 3538948
  687.4 307.1 %all-gather.9.cloned.1.call-start = ((), (), s32[]{:S(2)}) async-start(), calls=%async_computation.8 | async-start | bytes 31457280 | tf_op jit(solution)/shard_map/all_gather | solution.py:52
  687.9 724.3 %reduce-scatter.9.cloned.1.call-start = ((), (), s32[]{:S(2)}) async-start(), calls=%async_computation.9 | async-start | bytes 62914560 | tf_op jit(solution)/shard_map/reduce_scatter | solution.py:60
  688.0 398.1 %copy-start.27 = (f32[768]{0:T(1024)}, f32[768]{0:T(1024)S(1)}, u32[]{:S(2)}) copy-start(f32[768]{0:T(1024)S(1)} %convert_element_type.183) | copy-start | bytes 9220
  1086.0 654.8 %reduce-scatter.7.cloned.1.call-start = ((), (), s32[]{:S(2)}) async-start(), calls=%async_computation.7 | async-start | bytes 62914560 | tf_op jit(solution)/shard_map/reduce_scatter | solution.py:48
  1128.7 283.6 %copy-start.8 = (f32[64,64]{1,0:T(8,128)S(1)}, f32[64,64]{1,0:T(8,128)}, u32[]{:S(2)}) copy-start(f32[64,64]{1,0:T(8,128)} %copy-done.7) | copy-start | bytes 49156
  1128.7 283.6 %copy-start.20 = (f32[768]{0:T(1024)S(1)}, f32[768]{0:T(1024)}, u32[]{:S(2)}) copy-start(f32[768]{0:T(1024)} %get-tuple-element.63) | copy-start | bytes 9220
  1128.8 782.2 %all-gather.11.cloned.1.call-start = ((), (), s32[]{:S(2)}) async-start(), calls=%async_computation.10 | async-start | bytes 31457280 | tf_op jit(solution)/shard_map/all_gather | solution.py:64
  1129.4 291.7 %copy-start.16 = (f32[64,64]{1,0:T(8,128)S(1)}, f32[64,64]{1,0:T(8,128)}, u32[]{:S(2)}) copy-start(f32[64,64]{1,0:T(8,128)} %copy-done.15) | copy-start | bytes 49156
  1129.4 294.3 %copy-start.12 = (f32[64,64]{1,0:T(8,128)S(1)}, f32[64,64]{1,0:T(8,128)}, u32[]{:S(2)}) copy-start(f32[64,64]{1,0:T(8,128)} %copy-done.11) | copy-start | bytes 49156
  1434.0 477.0 %copy-start.37 = (bf16[3,64,768]{2,1,0:T(8,128)(2,1)S(1)}, bf16[3,64,768]{2,1,0:T(8,128)(2,1)}, u32[]{:S(2)}) copy-start(bf16[3,64,768]{2,1,0:T(8,128)(2,1)} %param.23) | copy-start | bytes 884740
  1758.1 178.5 %copy-start.18 = (f32[64,3,256]{2,1,0:T(4,128)S(1)}, f32[64,3,256]{2,1,0:T(4,128)}, u32[]{:S(2)}) copy-start(f32[64,3,256]{2,1,0:T(4,128)} %copy-done.17) | copy-start | bytes 589828
  1758.1 675.5 %reduce-scatter.11.cloned.1.call-start = ((), (), s32[]{:S(2)}) async-start(), calls=%async_computation.11 | async-start | bytes 62914560 | tf_op jit(solution)/shard_map/reduce_scatter | solution.py:77
  2189.5 244.0 %copy-start.6 = (f32[64,64]{1,0:T(8,128)S(1)}, f32[64,64]{1,0:T(8,128)}, u32[]{:S(2)}) copy-start(f32[64,64]{1,0:T(8,128)} %copy-done.5) | copy-start | bytes 49156
  2189.6 244.0 %copy-start.22 = (f32[768]{0:T(1024)S(1)}, f32[768]{0:T(1024)}, u32[]{:S(2)}) copy-start(f32[768]{0:T(1024)} %copy-done.21) | copy-start | bytes 9220
  2216.2 225.6 %copy-start.14 = (f32[64,64]{1,0:T(8,128)S(1)}, f32[64,64]{1,0:T(8,128)}, u32[]{:S(2)}) copy-start(f32[64,64]{1,0:T(8,128)} %copy-done.13) | copy-start | bytes 49156
  2216.2 225.7 %copy-start.10 = (f32[64,64]{1,0:T(8,128)S(1)}, f32[64,64]{1,0:T(8,128)}, u32[]{:S(2)}) copy-start(f32[64,64]{1,0:T(8,128)} %copy-done.9) | copy-start | bytes 49156
  (32 other events, 640.8 us)
Sparse Core Ops, SparseCore 0:
  27.1 155.5 all-gather.4
  345.6 326.1 reduce-scatter.4
  687.5 152.7 all-gather.6
  841.7 152.7 all-gather.8
  1086.1 326.1 reduce-scatter.8
  1414.7 326.0 reduce-scatter.6
  1758.2 152.7 all-gather.10
  2107.4 326.1 reduce-scatter.10
where the time goes:
time: 2530 us; the launch traced here: 2520 us
  waiting for transfers between devices  1720 us (68%)
  matrix products  588 us (23%)
  other arithmetic  148 us (6%)
  blocking collectives  45.6 us (2%)
    reduce_scatter x1, waiting for transfers between devices, group_step(): lax.psum_scatter(attn_part, 'tp', scatter_dimension=1, tiled=True)  326 us
    reduce_scatter x1, waiting for transfers between devices, group_step(): mlp_out = lax.psum_scatter(mlp_part, 'tp', scatter_dimension=1, tiled=True)  307 us
    reduce_scatter x1, waiting for transfers between devices, group_step(): lax.psum_scatter(d_h_two_part, 'tp', scatter_dimension=1, tiled=True)  283 us
    reduce_scatter x1, waiting for transfers between devices, group_step(): lax.psum_scatter(d_h_one_part, 'tp', scatter_dimension=1, tiled=True)  217 us
    all_gather x1, waiting for transfers between devices, group_step(): h_one_all = lax.all_gather(h_one_f.astype(half), 'tp', axis=1, tiled=True)  155 us
    all_gather x1, waiting for transfers between devices, group_step(): d_x_one_all = lax.all_gather(d_x_one, 'tp', axis=1, tiled=True)  153 us
    all_gather x1, waiting for transfers between devices, group_step(): h_two_all = lax.all_gather(h_two_f.astype(half), 'tp', axis=1, tiled=True)  152 us
    all_gather x1, waiting for transfers between devices, group_step(): d_out_all = lax.all_gather(d_out, 'tp', axis=1, tiled=True)  123 us
  transfers between devices with their start and end apart: 8, of which 8 were waited for; matrix products, arithmetic and copies ran while one was open for 8% of the time, Pallas kernels for 0%

commit v1 on v0

v1 whole, which is shorter than its diff:
```python
import jax
import jax.numpy as jnp
from jax import lax
from jax.sharding import PartitionSpec as P

LN_EPS = 1e-6
TP = 4


def permute_xor(x, k):
    return lax.ppermute(x, 'tp', [(i, i ^ k) for i in range(TP)])


def exchange(x, me):
    blocks = x.reshape((TP, x.shape[0] // TP) + x.shape[1:])
    out = []
    for k in range(TP):
        block = lax.dynamic_index_in_dim(blocks, me ^ k, 0, keepdims=False)
        out.append(block if k == 0 else permute_xor(block, k))
    return out


def give_back(slots, me):
    out = jnp.zeros((TP,) + slots[0].shape, slots[0].dtype)
    for k in range(TP):
        block = slots[k] if k == 0 else permute_xor(slots[k], k)
        out = lax.dynamic_update_index_in_dim(out, block, me ^ k, 0)
    return out.reshape((-1,) + slots[0].shape[1:])


def gather(w):
    w2 = permute_xor(w, 2)
    w1 = permute_xor(w, 1)
    w3 = permute_xor(w2, 1)
    return [w, w1, w2, w3]


def reduce_slots(g):
    r1 = permute_xor(g[1], 1)
    r3 = permute_xor(g[3], 1)
    a2 = g[2] + r3
    return (g[0] + r1) + permute_xor(a2, 2)


def layer_norm(x_val, scale_f, bias_f):
    row_mean = jnp.mean(x_val, axis=-1, keepdims=True)
    centered = x_val - row_mean
    row_var = jnp.mean(centered * centered, axis=-1, keepdims=True)
    return centered * lax.rsqrt(row_var + LN_EPS) * scale_f + bias_f


def gelu_tanh(pre_act):
    return jax.nn.gelu(pre_act, approximate=True)


def group_step(patches, patch_w, patch_b, pos_emb, ln_scale, ln_bias, qkv_w, qkv_b, out_w, out_b, fc1_w, fc1_b, fc2_w, fc2_b, d_out):
    wide = jnp.float32
    half = jnp.bfloat16
    me = lax.axis_index('tp')
    scale = qkv_w.shape[-1] ** -0.5
    ln_scale_f = ln_scale.astype(wide)
    ln_bias_f = ln_bias.astype(wide)
    patches = jnp.concatenate(exchange(patches, me), axis=1)
    pos_emb = jnp.concatenate(gather(pos_emb), axis=0)
    qkv_w = jnp.concatenate(gather(qkv_w), axis=2)
    qkv_b = jnp.concatenate(gather(qkv_b), axis=1)
    out_w = jnp.concatenate(gather(out_w), axis=0)
    fc1_w = jnp.concatenate(gather(fc1_w), axis=1)
    fc1_b = jnp.concatenate(gather(fc1_b), axis=0)
    fc2_w = jnp.concatenate(gather(fc2_w), axis=0)
    d_out = jnp.concatenate(exchange(d_out, me), axis=1)
    emb = jnp.einsum('btp,pd->btd', patches, patch_w, preferred_element_type=wide)
    emb_f = (emb + patch_b.astype(wide) + pos_emb.astype(wide)).astype(half).astype(wide)
    h_one_f, ln_one_vjp = jax.vjp(layer_norm, emb_f, ln_scale_f[0], ln_bias_f[0])
    h_one_all = h_one_f.astype(half)
    qkv = jnp.einsum('btd,sdhc->btshc', h_one_all, qkv_w, preferred_element_type=wide)
    qkv = (qkv + qkv_b.astype(wide)).astype(half)
    query = qkv[:, :, 0]
    keys_all = qkv[:, :, 1]
    values = qkv[:, :, 2]
    scores = jnp.einsum('bqhc,bkhc->bhqk', query, keys_all, preferred_element_type=wide) * scale
    probs = jax.nn.softmax(scores, axis=-1)
    probs_h = probs.astype(half)
    context = jnp.einsum('bhqk,bkhc->bqhc', probs_h, values, preferred_element_type=wide).astype(half)
    attn_out = jnp.einsum('crid,ide->cre', context, out_w, preferred_element_type=wide)
    x_one_f = (emb_f + (attn_out + out_b.astype(wide))).astype(half).astype(wide)
    h_two_f, ln_two_vjp = jax.vjp(layer_norm, x_one_f, ln_scale_f[1], ln_bias_f[1])
    h_two_all = h_two_f.astype(half)
    pre_act = jnp.einsum('btd,df->btf', h_two_all, fc1_w, preferred_element_type=wide) + fc1_b.astype(wide)
    hidden_f, gelu_vjp = jax.vjp(gelu_tanh, pre_act)
    hidden = hidden_f.astype(half)
    mlp_out = jnp.einsum('btf,fd->btd', hidden, fc2_w, preferred_element_type=wide)
    x_two = (x_one_f + (mlp_out + fc2_b.astype(wide))).astype(half)
    x_two = give_back([x_two[:, 64 * k:64 * k + 64] for k in range(TP)], me)
    d_two_f = d_out.astype(wide)
    d_fc2_b = jnp.sum(d_two_f, axis=(0, 1))
    d_fc2_w = jnp.einsum('btf,btd->fd', hidden, d_out, preferred_element_type=wide)
    d_hidden = jnp.einsum('btd,fd->btf', d_out, fc2_w, preferred_element_type=wide).astype(half)
    d_pre = gelu_vjp(d_hidden.astype(wide))[0]
    d_fc1_b = jnp.sum(d_pre, axis=(0, 1))
    d_pre_h = d_pre.astype(half)
    d_fc1_w = jnp.einsum('btd,btf->df', h_two_all, d_pre_h, preferred_element_type=wide)
    d_h_two = jnp.einsum('btf,df->btd', d_pre_h, fc1_w, preferred_element_type=wide).astype(half)
    d_x_ln, d_ln2_scale, d_ln2_bias = ln_two_vjp(d_h_two.astype(wide))
    d_x_one = (d_two_f + d_x_ln).astype(half)
    d_out_b = jnp.sum(d_x_one, axis=(0, 1), dtype=wide)
    d_out_w = jnp.einsum('crid,cre->ide', context, d_x_one, preferred_element_type=wide)
    d_context = jnp.einsum('cre,ide->crid', d_x_one, out_w, preferred_element_type=wide).astype(half)
    d_values = jnp.einsum('bhqk,bqhc->bkhc', probs_h, d_context, preferred_element_type=wide).astype(half)
    d_probs = jnp.einsum('bqhc,bkhc->bhqk', d_context, values, preferred_element_type=wide).astype(half).astype(wide)
    d_scores = probs * (d_probs - jnp.sum(d_probs * probs, axis=-1, keepdims=True))
    d_scores_h = (d_scores * scale).astype(half)
    d_query = jnp.einsum('bhqk,bkhc->bqhc', d_scores_h, keys_all, preferred_element_type=wide).astype(half)
    d_keys = jnp.einsum('bhqk,bqhc->bkhc', d_scores_h, query, preferred_element_type=wide).astype(half)
    d_qkv = jnp.stack([d_query, d_keys, d_values], axis=2)
    d_qkv_b = jnp.sum(d_qkv, axis=(0, 1), dtype=wide)
    d_qkv_w = jnp.einsum('btd,btshc->sdhc', h_one_all, d_qkv, preferred_element_type=wide)
    d_h_one = jnp.einsum('btshc,sdhc->btd', d_qkv, qkv_w, preferred_element_type=wide).astype(half)
    d_emb_ln, d_ln1_scale, d_ln1_bias = ln_one_vjp(d_h_one.astype(wide))
    d_emb = (d_x_one.astype(wide) + d_emb_ln).astype(half)
    d_pos = jnp.sum(d_emb, axis=0, dtype=wide)
    d_patch_b = jnp.sum(d_emb, axis=(0, 1), dtype=wide)
    d_patch_w = jnp.einsum('btp,btd->pd', patches, d_emb, preferred_element_type=wide)
    d_fc2_w = reduce_slots([d_fc2_w[768 * k:768 * k + 768] for k in range(TP)])
    d_fc1_w = reduce_slots([d_fc1_w[:, 768 * k:768 * k + 768] for k in range(TP)])
    d_out_w = reduce_slots([d_out_w[3 * k:3 * k + 3] for k in range(TP)])
    d_qkv_w = reduce_slots([d_qkv_w[:, :, 3 * k:3 * k + 3] for k in range(TP)])
    d_fc1_b = reduce_slots([d_fc1_b[768 * k:768 * k + 768] for k in range(TP)])
    d_qkv_b = reduce_slots([d_qkv_b[:, 3 * k:3 * k + 3] for k in range(TP)])
    d_pos = reduce_slots([d_pos[64 * k:64 * k + 64] for k in range(TP)])
    vec = jnp.stack([d_patch_b, d_ln1_scale, d_ln2_scale, d_ln1_bias, d_ln2_bias, d_out_b, d_fc2_b, d_fc2_b])
    vec = vec + permute_xor(vec, 1)
    vec = (vec + permute_xor(vec, 2)).astype(half)
    core = me % 2
    halves = d_patch_w.reshape(2, 384, 768)
    mine = lax.dynamic_index_in_dim(halves, core, 0, keepdims=False)
    other = lax.dynamic_index_in_dim(halves, 1 - core, 0, keepdims=False)
    mine = mine + permute_xor(other, 1)
    mine = (mine + permute_xor(mine, 2)).astype(half)
    theirs = permute_xor(mine, 1)
    first = core == 0
    d_patch_w = jnp.concatenate([jnp.where(first, mine, theirs), jnp.where(first, theirs, mine)], axis=0)
    return (x_two, d_patch_w, vec[0], d_pos.astype(half), vec[1:3], vec[3:5], d_qkv_w.astype(half), d_qkv_b.astype(half), d_out_w.astype(half), vec[5], d_fc1_w.astype(half), d_fc1_b.astype(half), d_fc2_w.astype(half), vec[6])


def solution(mesh):
    in_specs = (P('dp', 'tp', None), P(), P(), P('tp', None), P(), P(), P(None, None, 'tp', None), P(None, 'tp', None), P('tp', None, None), P(), P(None, 'tp'), P('tp'), P('tp', None), P(), P('dp', 'tp', None))
    out_specs = (P('dp', 'tp', None), P('dp', None), P('dp'), P(('dp', 'tp'), None), P('dp', None), P('dp', None), P('dp', None, 'tp', None), P('dp', 'tp', None), P(('dp', 'tp'), None, None), P('dp'), P('dp', 'tp'), P(('dp', 'tp')), P(('dp', 'tp'), None), P('dp'))
    return jax.shard_map(group_step, mesh=mesh, in_specs=in_specs, out_specs=out_specs, check_vma=False)
```

time: 2530 us -> 998 us (0.39)
  waiting for transfers between devices: 1720 us -> 315 us
  matrix products: 588 us -> 499 us
  other arithmetic: 148 us -> 86.8 us
  local copies, waits for them, and re-layouts: 9.94 us -> 56.3 us
  blocking collectives: 45.6 us -> 0 us
  starting transfers between devices: 0.5 us -> 32.2 us
    reduce_scatter x4 -> x0, waiting for transfers between devices: 1130 us -> none  [the longest x1 326 us: group_step(): lax.psum_scatter(attn_part, 'tp', scatter_dimension=1, tiled=True)]
    all_gather x4 -> x0, waiting for transfers between devices: 583 us -> none  [the longest x1 155 us: group_step(): h_one_all = lax.all_gather(h_one_f.astype(half), 'tp', axis=1, tiled=True)]
    ppermute x0 -> x56, waiting for transfers between devices: none -> 315 us  [permute_xor(): return lax.ppermute(x, 'tp', [(i, i ^ k) for i in range(TP)])]
    dot_general x5 -> x4, matrix products: 158 us -> 95.1 us  [the longest x1 55.2 us: group_step(): jnp.einsum('btd,fd->btf', d_out, fc2_w, preferred_element_type=wide)]
    sub x1 -> x0, other arithmetic: 54.1 us -> none  [group_step(): probs = jax.nn.softmax(scores, axis=-1)]
    psum x1 -> x0, blocking collectives: 45.6 us -> none  [group_step(): lax.psum((d_patch_w, d_patch_b, d_ln_scale, d_ln_bias, d_out_b, d_fc2_b),...]
    ppermute x0 -> x56, starting transfers between devices: none -> 32.2 us  [permute_xor(): return lax.ppermute(x, 'tp', [(i, i ^ k) for i in range(TP)])]
  transfers between devices with their start and end apart: 8 -> 56, of which waited for: 8 -> 18; matrix products, arithmetic and copies ran while one was open for 8% -> 25% of each run, Pallas kernels for 0% -> 0%
where the time goes in v1:
time: 998 us; the launch traced here: 992 us
  matrix products  499 us (50%)
  waiting for transfers between devices  315 us (32%)
  other arithmetic  86.8 us (9%)
  local copies, waits for them, and re-layouts  56.3 us (6%)
  starting transfers between devices  32.2 us (3%)
    ppermute x56, waiting for transfers between devices, permute_xor(): return lax.ppermute(x, 'tp', [(i, i ^ k) for i in range(TP)])  315 us
    dot_general x1, matrix products, group_step(): jnp.einsum('btd,fd->btf', d_out, fc2_w, preferred_element_type=wide)  55.2 us
    dot_general x1, matrix products, group_step(): jnp.einsum('bhqk,bqhc->bkhc', d_scores_h, query, preferred_element_type=w...  52 us
    dot_general x1, matrix products, group_step(): jnp.einsum('bhqk,bkhc->bqhc', d_scores_h, keys_all, preferred_element_typ...  52 us
    dot_general x1, matrix products, group_step(): jnp.einsum('btd,df->btf', h_two_all, fc1_w, preferred_element_type=wide)  38 us
    dot_general x1, matrix products, group_step(): jnp.einsum('btf,df->btd', d_pre_h, fc1_w, preferred_element_type=wide)  32.5 us
    ppermute x56, starting transfers between devices, permute_xor(): return lax.ppermute(x, 'tp', [(i, i ^ k) for i in range(TP)])  32.2 us
    dot_general x1, matrix products, group_step(): jnp.einsum('btd,btf->df', h_two_all, d_pre_h, preferred_element_type=wide)  27.4 us
  transfers between devices with their start and end apart: 56, of which 18 were waited for; matrix products, arithmetic and copies ran while one was open for 25% of the time, Pallas kernels for 0%

profile of v1, /device:TPU:0, one launch (start us, length us, event | category | flops | bytes accessed | tf_op | source)
XLA Modules:
  0.0 992.0 jit_solution(10182938733180928118)
XLA Ops:
  11.2 67.0 %collective-permute-done.10 = bf16[3,3,64]{2,1,0:T(4,128)(2,1)S(1)} collective-permute-done((bf16[3,3,64]{2,1,0:T(4,128)(2,1)S(1)}, bf16[3,3,64]{2,1,0:T(4,128)(2,1)S(1)}, u32[]{:S(2)}, u32[]{:S(2)}) %collective-permute-start.10) | collective-permute-done | bytes 1184 | tf_op jit(solution)/shard_map/ppermute | solution.py:11
  131.6 22.8 %add_convert_fusion = bf16[16,256,3,12,64]{1,4,3,2,0:T(8,128)(2,1)} fusion(f32[3,12,64]{2,1,0:T(8,128)S(1)} %maximum_convert_fusion.1, bf16[3,768,12,64]{1,3,2,0:T(8,128)(2,1)} %copy-done.28, bf16[16,256,768]{2,1,0:T(8,128)(2,1)} %copy-done.2, f32[768]{0:T(1024)S(1)} %get-tuple-element.30, f32[768]{0:T(1024)S(1)} %get-tuple-element.28, ...), kind=kOutput, calls=%fused_computation.25 | convolution fusion | flops 14533263360 | bytes 28752896 | tf_op jit(solution)/shard_map/btd,sdhc->btshc/dot_general | solution.py:76
  154.4 25.3 %fusion.144 = (f32[16,12,256]{2,1,0:T(8,128)S(1)}, f32[16,12,256,256]{2,3,1,0:T(8,128)}) fusion(bf16[16,256,3,12,64]{1,4,3,2,0:T(8,128)(2,1)} %add_convert_fusion), kind=kOutput, calls=%fused_computation.221 | convolution fusion | flops 1648361728 | bytes 63111168 | tf_op jit(solution)/shard_map/sub | solution.py:82
  179.6 22.0 %fusion.78 = bf16[16,12,64,256]{3,2,1,0:T(8,128)(2,1)} fusion(bf16[16,256,3,12,64]{1,4,3,2,0:T(8,128)(2,1)} %add_convert_fusion, f32[16,12,256,256]{2,3,1,0:T(8,128)} %get-tuple-element.67, f32[16,12,256]{2,1,0:T(8,128)S(1)} %get-tuple-element.66), kind=kOutput, calls=%fused_computation.119 | convolution fusion | flops 1638924288 | bytes 63111168 | tf_op jit(solution)/shard_map/bhqk,bkhc->bqhc/dot_general | solution.py:84
  218.8 38.0 %multiply_convert_fusion = (bf16[16,256,3072]{2,1,0:T(8,128)(2,1)}, f32[16,256,3072]{2,1,0:T(8,128)}) fusion(f32[3072]{0:T(1024)S(1)} %copy-done.48, bf16[16,256,768]{2,1,0:T(8,128)(2,1)} %copy-done.3, f32[768]{0:T(1024)S(1)} %copy-done.51, f32[768]{0:T(1024)S(1)} %copy-done.40, f32[16,256]{1,0:T(8,128)S(1)} %fusion.115, ...), kind=kOutput, calls=%fused_computation.20 | convolution fusion | flops 19472056320 | bytes 86558720 | tf_op jit(solution)/shard_map/btd,df->btf/dot_general | solution.py:89
  263.0 20.0 %collective-permute-done.29 = bf16[16,64,768]{2,1,0:T(8,128)(2,1)} collective-permute-done((bf16[16,64,768]{2,1,0:T(8,128)(2,1)}, bf16[16,64,768]{2,1,0:T(8,128)(2,1)}, u32[]{:S(2)}, u32[]{:S(2)}) %collective-permute-start.29) | collective-permute-done | bytes 1572896 | tf_op jit(solution)/shard_map/ppermute | solution.py:11
  283.0 55.2 %fusion.145 = (f32[3072]{0:T(1024)}, bf16[16,256,3072]{2,1,0:T(8,128)(2,1)}) fusion(f32[16,256,3072]{2,1,0:T(8,128)} %get-tuple-element.71, f32[3072]{0:T(1024)S(1)} %copy-done.48, bf16[16,64,768]{2,1,0:T(8,128)(2,1)} %collective-permute-done.29, bf16[16,64,768]{2,1,0:T(8,128)(2,1)} %collective-permute-done.28, ...), kind=kOutput, calls=%fused_computation.222 | convolution fusion | flops 19654504448 | bytes 86532096 | tf_op jit(solution)/shard_map/btd,fd->btf/dot_general | solution.py:98
  338.2 27.4 %fusion.69 = f32[768,3072]{1,0:T(8,128)} fusion(bf16[16,256,3072]{2,1,0:T(8,128)(2,1)} %get-tuple-element.75, bf16[16,256,768]{2,1,0:T(8,128)(2,1)S(1)} %bitcast.200, f32[768]{0:T(1024)S(1)} %copy-done.51, f32[768]{0:T(1024)S(1)} %copy-done.40, f32[16,256]{1,0:T(8,128)S(1)} %fusion.115, f32[16,256]{1,0:T(8,128)S(1)} %broadcast_multiply_fusion), kind=kOutput, calls=%fused_computation.111 | convolution fusion | flops 19346227200 | bytes 40933376 | tf_op jit(solution)/shard_map/btd,btf->df/dot_general | solution.py:102
  365.6 32.5 %convert_reduce_fusion.2 = (f32[768]{0:T(1024)}, f32[16,256]{1,0:T(8,128)S(1)}, bf16[16,256,768]{2,1,0:T(8,128)(2,1)}) fusion(f32[768]{0:T(1024)S(1)} %copy-done.40, f32[16,256]{1,0:T(8,128)S(1)} %broadcast_multiply_fusion, bf16[16,256,768]{2,1,0:T(8,128)(2,1)} %copy-done.3, bf16[768,768]{1,0:T(8,128)(2,1)S(1)} %copy-done.20, ...), kind=kOutput, calls=%fused_computation.36 | convolution fusion | flops 19371388928 | bytes 42506240 | tf_op jit(solution)/shard_map/btf,df->btd/dot_general | solution.py:103
  398.2 11.2 %fusion.45 = (f32[768]{0:T(1024)}, f32[16,256]{1,0:T(8,128)S(1)}) fusion(bf16[16,256,768]{2,1,0:T(8,128)(2,1)} %get-tuple-element.72, bf16[16,256,768]{2,1,0:T(8,128)(2,1)} %copy-done.3, f32[16,256]{1,0:T(8,128)S(1)} %fusion.115, f32[16,256]{1,0:T(8,128)S(1)} %broadcast_multiply_fusion, f32[16,256]{1,0:T(8,128)S(1)} %multiply_multiply_fusion.3, ...), kind=kLoop, calls=%fused_computation.77 | loop fusion | flops 37743872 | bytes 12654592 | tf_op jit(solution)/shard_map/transpose(jvp())/reduce_sum | solution.py:49
  433.3 15.8 %convolution_convert_fusion = bf16[16,12,256,256]{2,3,1,0:T(8,128)(2,1)} fusion(bf16[16,256,12,64]{1,3,2,0:T(8,128)(2,1)} %fusion.75, bf16[16,256,3,12,64]{1,4,3,2,0:T(8,128)(2,1)} %add_convert_fusion), kind=kOutput, calls=%fused_computation.64 | convolution fusion | flops 1623195648 | bytes 37748736 | tf_op jit(solution)/shard_map/bqhc,bkhc->bhqk/dot_general | solution.py:110
  449.2 52.0 %convert_bitcast_fusion.2 = bf16[16,256,1,12,64]{1,4,3,0,2:T(8,128)(2,1)} fusion(bf16[16,12,256,256]{2,3,1,0:T(8,128)(2,1)} %convolution_convert_fusion, bf16[16,256,3,12,64]{1,4,3,2,0:T(8,128)(2,1)} %add_convert_fusion, f32[16,12,256,256]{2,3,1,0:T(8,128)} %get-tuple-element.67, f32[16,12,256]{2,1,0:T(8,128)S(1)} %copy-done.69), kind=kOutput, calls=%fused_computation.110 | convolution fusion | flops 1727054080 | bytes 164102144 | tf_op jit(solution)/shard_map/bhqk,bkhc->bqhc/dot_general | solution.py:113
  501.1 52.0 %convert_bitcast_fusion.1 = bf16[16,256,1,12,64]{1,4,3,0,2:T(8,128)(2,1)} fusion(bf16[16,12,256,256]{2,3,1,0:T(8,128)(2,1)} %convolution_convert_fusion, bf16[16,256,3,12,64]{1,4,3,2,0:T(8,128)(2,1)} %add_convert_fusion, f32[16,12,256,256]{2,3,1,0:T(8,128)} %get-tuple-element.67, f32[16,12,256]{2,1,0:T(8,128)S(1)} %copy-done.69), kind=kOutput, calls=%fused_computation.109 | convolution fusion | flops 1727054080 | bytes 164102144 | tf_op jit(solution)/shard_map/bhqk,bqhc->bkhc/dot_general | solution.py:114
  553.1 22.1 %convert_bitcast_fusion = bf16[16,256,1,12,64]{1,4,3,0,2:T(8,128)(2,1)} fusion(bf16[16,256,12,64]{1,3,2,0:T(8,128)(2,1)} %fusion.75, f32[16,12,256,256]{2,3,1,0:T(8,128)} %get-tuple-element.67, f32[16,12,256]{2,1,0:T(8,128)S(1)} %copy-done.69), kind=kOutput, calls=%fused_computation.108 | convolution fusion | flops 1638924288 | bytes 63111168 | tf_op jit(solution)/shard_map/bhqk,bqhc->bkhc/dot_general | solution.py:109
  582.5 23.1 %fusion.91 = f32[3,768,12,64]{1,3,2,0:T(8,128)} fusion(f32[768]{0:T(1024)S(1)} %copy-done.50, f32[768]{0:T(1024)S(1)} %copy-done.38, f32[16,256]{1,0:T(8,128)S(1)} %copy-done.31, f32[16,256]{1,0:T(8,128)S(1)} %copy-done.26, bf16[16,256,768]{2,1,0:T(8,128)(2,1)} %copy-done.2, bf16[16,256,1,12,64]{1,4,3,0,2:T(8,128)(2,1)} %convert_bitcast_fusion, ...), kind=kOutput, calls=%fused_computation.122 | convolution fusion | flops 14533263360 | bytes 32282624 | tf_op jit(solution)/shard_map/btd,btshc->sdhc/dot_general | solution.py:117
  605.6 22.1 %convert_reduce_fusion.1 = (f32[768]{0:T(1024)}, f32[16,256]{1,0:T(8,128)S(1)}, bf16[16,256,768]{2,1,0:T(8,128)(2,1)S(1)}) fusion(f32[768]{0:T(1024)S(1)} %copy-done.38, f32[16,256]{1,0:T(8,128)S(1)} %copy-done.26, bf16[16,256,768]{2,1,0:T(8,128)(2,1)} %copy-done.2, bf16[3,768,12,64]{1,3,2,0:T(8,128)(2,1)} %copy-done.28, ...), kind=kOutput, calls=%fused_computation.32 | convolution fusion | flops 14539549696 | bytes 35035136 | tf_op jit(solution)/shard_map/btshc,sdhc->btd/dot_general | solution.py:118
  627.8 25.5 %convolution_bitcast_fusion = f32[3072,768]{1,0:T(8,128)S(1)} fusion(bf16[16,256,3072]{2,1,0:T(8,128)(2,1)} %get-tuple-element.70, bf16[16,64,768]{2,1,0:T(8,128)(2,1)} %collective-permute-done.29, bf16[16,64,768]{2,1,0:T(8,128)(2,1)} %collective-permute-done.28, bf16[16,64,768]{2,1,0:T(8,128)(2,1)} %collective-permute-done.27, ...), kind=kOutput, calls=%fused_computation.112 | convolution fusion | flops 19352518656 | bytes 40894464 | tf_op jit(solution)/shard_map/btf,btd->fd/dot_general | solution.py:97
  683.9 25.2 %fusion.44 = bf16[16,256,768]{2,1,0:T(8,128)(2,1)} fusion(bf16[16,256,768]{2,1,0:T(8,128)(2,1)S(1)} %bitcast.202, f32[768]{0:T(1024)} %convert_element_type.188, bf16[16,256,3072]{2,1,0:T(8,128)(2,1)} %get-tuple-element.70, bf16[768,768]{1,0:T(8,128)(2,1)} %collective-permute-done.23, bf16[768,768]{1,0:T(8,128)(2,1)} %collective-permute-done.22, ...), kind=kOutput, calls=%fused_computation.76 | convolution fusion | flops 19358810112 | bytes 42470400 | tf_op jit(solution)/shard_map/btf,fd->btd/dot_general | solution.py:92
  762.9 21.6 %collective-permute-done.31 = f32[384,768]{1,0:T(8,128)} collective-permute-done((f32[384,768]{1,0:T(8,128)S(1)}, f32[384,768]{1,0:T(8,128)}, u32[]{:S(2)}, u32[]{:S(2)}) %collective-permute-start.31) | collective-permute-done | bytes 1179680 | tf_op jit(solution)/shard_map/ppermute | solution.py:11
  792.3 25.9 %collective-permute-done.25 = bf16[16,64,768]{2,1,0:T(8,128)(2,1)} collective-permute-done((bf16[16,64,768]{2,1,0:T(8,128)(2,1)}, bf16[16,64,768]{2,1,0:T(8,128)(2,1)}, u32[]{:S(2)}, u32[]{:S(2)}) %collective-permute-start.25) | collective-permute-done | bytes 1572896 | tf_op jit(solution)/shard_map/ppermute | solution.py:11
  818.2 28.9 %collective-permute-done.26 = bf16[16,64,768]{2,1,0:T(8,128)(2,1)} collective-permute-done((bf16[16,64,768]{2,1,0:T(8,128)(2,1)}, bf16[16,64,768]{2,1,0:T(8,128)(2,1)}, u32[]{:S(2)}, u32[]{:S(2)}) %collective-permute-start.26) | collective-permute-done | bytes 1572896 | tf_op jit(solution)/shard_map/ppermute | solution.py:11
  861.3 26.5 %collective-permute-done.40 = f32[3,768,3,64]{1,3,2,0:T(8,128)} collective-permute-done((f32[3,768,3,64]{1,3,2,0:T(8,128)}, f32[3,768,3,64]{1,3,2,0:T(8,128)}, u32[]{:S(2)}, u32[]{:S(2)}) %collective-permute-start.40) | collective-permute-done | bytes 1769504 | tf_op jit(solution)/shard_map/ppermute | solution.py:11
  890.7 47.7 %collective-permute-done.55 = f32[768,768]{1,0:T(8,128)} collective-permute-done((f32[768,768]{1,0:T(8,128)S(1)}, f32[768,768]{1,0:T(8,128)}, u32[]{:S(2)}, u32[]{:S(2)}) %collective-permute-start.55) | collective-permute-done | bytes 2359328 | tf_op jit(solution)/shard_map/ppermute | solution.py:11
  942.1 46.5 %collective-permute-done.49 = f32[768,768]{1,0:T(8,128)} collective-permute-done((f32[768,768]{1,0:T(8,128)S(1)}, f32[768,768]{1,0:T(8,128)}, u32[]{:S(2)}, u32[]{:S(2)}) %collective-permute-start.49) | collective-permute-done | bytes 2359328 | tf_op jit(solution)/shard_map/ppermute | solution.py:11
  (369 shorter events, 233.6 us)
Async XLA Ops:
  6.0 108.6 %collective-permute-start = (bf16[16,64,768]{2,1,0:T(8,128)(2,1)}, bf16[16,64,768]{2,1,0:T(8,128)(2,1)}, u32[]{:S(2)}, u32[]{:S(2)}) collective-permute-start(bf16[16,64,768]{2,1,0:T(8,128)(2,1)} %get-tuple-element.51), channel_id=1, source_target_pairs={{0,1},{1,0},{2,3},{3,2},{4,5},{5,4},{6,7},{7,6}} | collective-permute-start | bytes 4718600 | tf_op jit(solution)/shard_map/ppermute | solution.py:11
  6.9 109.5 %collective-permute-start.1 = (bf16[16,64,768]{2,1,0:T(8,128)(2,1)}, bf16[16,64,768]{2,1,0:T(8,128)(2,1)}, u32[]{:S(2)}, u32[]{:S(2)}) collective-permute-start(bf16[16,64,768]{2,1,0:T(8,128)(2,1)} %get-tuple-element.50), channel_id=1, source_target_pairs={{0,2},{1,3},{2,0},{3,1},{4,6},{5,7},{6,4},{7,5}} | collective-permute-start | bytes 4718600 | tf_op jit(solution)/shard_map/ppermute | solution.py:11
  9.4 107.3 %collective-permute-start.2 = (bf16[16,64,768]{2,1,0:T(8,128)(2,1)}, bf16[16,64,768]{2,1,0:T(8,128)(2,1)}, u32[]{:S(2)}, u32[]{:S(2)}) collective-permute-start(bf16[16,64,768]{2,1,0:T(8,128)(2,1)} %get-tuple-element.49), channel_id=1, source_target_pairs={{0,3},{1,2},{2,1},{3,0},{4,7},{5,6},{6,5},{7,4}} | collective-permute-start | bytes 4718600 | tf_op jit(solution)/shard_map/ppermute | solution.py:11
  9.5 68.7 %collective-permute-start.10 = (bf16[3,3,64]{2,1,0:T(4,128)(2,1)S(1)}, bf16[3,3,64]{2,1,0:T(4,128)(2,1)S(1)}, u32[]{:S(2)}, u32[]{:S(2)}) collective-permute-start(bf16[3,3,64]{2,1,0:T(4,128)(2,1)S(1)} %copy-done.55), channel_id=1, source_target_pairs={{0,2},{1,3},{2,0},{3,1},{4,6},{5,7},{6,4},{7,5}} | collective-permute-start | bytes 3464 | tf_op jit(solution)/shard_map/ppermute | solution.py:11
  11.2 68.7 %collective-permute-start.9 = (bf16[3,3,64]{2,1,0:T(4,128)(2,1)S(1)}, bf16[3,3,64]{2,1,0:T(4,128)(2,1)S(1)}, u32[]{:S(2)}, u32[]{:S(2)}) collective-permute-start(bf16[3,3,64]{2,1,0:T(4,128)(2,1)S(1)} %copy-done.55), channel_id=1, source_target_pairs={{0,1},{1,0},{2,3},{3,2},{4,5},{5,4},{6,7},{7,6}} | collective-permute-start | bytes 3464 | tf_op jit(solution)/shard_map/ppermute | solution.py:11
  113.4 88.3 %collective-permute-start.12 = (bf16[3,64,768]{2,1,0:T(8,128)(2,1)S(1)}, bf16[3,64,768]{2,1,0:T(8,128)(2,1)}, u32[]{:S(2)}, u32[]{:S(2)}) collective-permute-start(bf16[3,64,768]{2,1,0:T(8,128)(2,1)S(1)} %copy-done.62), channel_id=1, source_target_pairs={{0,1},{1,0},{2,3},{3,2},{4,5},{5,4},{6,7},{7,6}} | collective-permute-start | bytes 884744 | tf_op jit(solution)/shard_map/ppermute | solution.py:11
  114.6 87.6 %collective-permute-start.16 = (bf16[768,768]{1,0:T(8,128)(2,1)}, bf16[768,768]{1,0:T(8,128)(2,1)}, u32[]{:S(2)}, u32[]{:S(2)}) collective-permute-start(bf16[768,768]{1,0:T(8,128)(2,1)} %param.25), channel_id=1, source_target_pairs={{0,2},{1,3},{2,0},{3,1},{4,6},{5,7},{6,4},{7,5}} | collective-permute-start | bytes 3538952 | tf_op jit(solution)/shard_map/ppermute | solution.py:11
  116.4 97.3 %collective-permute-start.15 = (bf16[768,768]{1,0:T(8,128)(2,1)}, bf16[768,768]{1,0:T(8,128)(2,1)}, u32[]{:S(2)}, u32[]{:S(2)}) collective-permute-start(bf16[768,768]{1,0:T(8,128)(2,1)} %param.25), channel_id=1, source_target_pairs={{0,1},{1,0},{2,3},{3,2},{4,5},{5,4},{6,7},{7,6}} | collective-permute-start | bytes 3538952 | tf_op jit(solution)/shard_map/ppermute | solution.py:11
  129.5 86.0 %collective-permute-start.22 = (bf16[768,768]{1,0:T(8,128)(2,1)S(1)}, bf16[768,768]{1,0:T(8,128)(2,1)}, u32[]{:S(2)}, u32[]{:S(2)}) collective-permute-start(bf16[768,768]{1,0:T(8,128)(2,1)S(1)} %copy-done.17), channel_id=1, source_target_pairs={{0,2},{1,3},{2,0},{3,1},{4,6},{5,7},{6,4},{7,5}} | collective-permute-start | bytes 3538952 | tf_op jit(solution)/shard_map/ppermute | solution.py:11
  129.8 72.4 %collective-permute-start.14 = (bf16[3,64,768]{2,1,0:T(8,128)(2,1)S(1)}, bf16[3,64,768]{2,1,0:T(8,128)(2,1)S(1)}, u32[]{:S(2)}, u32[]{:S(2)}) collective-permute-start(bf16[3,64,768]{2,1,0:T(8,128)(2,1)S(1)} %collective-permute-done.13), channel_id=1, source_target_pairs={{0,1},{1,0},{2,3},{3,2},{4,5},{5,4},{6,7},{7,6}} | collective-permute-start | bytes 884744 | tf_op jit(solution)/shard_map/ppermute | solution.py:11
  202.2 60.8 %collective-permute-start.27 = (bf16[16,64,768]{2,1,0:T(8,128)(2,1)}, bf16[16,64,768]{2,1,0:T(8,128)(2,1)}, u32[]{:S(2)}, u32[]{:S(2)}) collective-permute-start(bf16[16,64,768]{2,1,0:T(8,128)(2,1)} %get-tuple-element.44), channel_id=1, source_target_pairs={{0,1},{1,0},{2,3},{3,2},{4,5},{5,4},{6,7},{7,6}} | collective-permute-start | bytes 4718600 | tf_op jit(solution)/shard_map/ppermute | solution.py:11
  215.4 67.6 %collective-permute-start.29 = (bf16[16,64,768]{2,1,0:T(8,128)(2,1)}, bf16[16,64,768]{2,1,0:T(8,128)(2,1)}, u32[]{:S(2)}, u32[]{:S(2)}) collective-permute-start(bf16[16,64,768]{2,1,0:T(8,128)(2,1)} %get-tuple-element.42), channel_id=1, source_target_pairs={{0,3},{1,2},{2,1},{3,0},{4,7},{5,6},{6,5},{7,4}} | collective-permute-start | bytes 4718600 | tf_op jit(solution)/shard_map/ppermute | solution.py:11
  656.5 69.2 %collective-permute-start.51 = (f32[768]{0:T(1024)}, f32[768]{0:T(1024)}, u32[]{:S(2)}, u32[]{:S(2)}) collective-permute-start(f32[768]{0:T(1024)} %get-tuple-element.61), channel_id=1, source_target_pairs={{0,1},{1,0},{2,3},{3,2},{4,5},{5,4},{6,7},{7,6}} | collective-permute-start | bytes 9224 | tf_op jit(solution)/shard_map/ppermute | solution.py:11
  662.6 70.8 %collective-permute-start.45 = (f32[3,64,768]{2,1,0:T(8,128)}, f32[3,64,768]{2,1,0:T(8,128)}, u32[]{:S(2)}, u32[]{:S(2)}) collective-permute-start(f32[3,64,768]{2,1,0:T(8,128)} %get-tuple-element.53), channel_id=1, source_target_pairs={{0,1},{1,0},{2,3},{3,2},{4,5},{5,4},{6,7},{7,6}} | collective-permute-start | bytes 1769480 | tf_op jit(solution)/shard_map/ppermute | solution.py:11
  663.6 60.8 %collective-permute-start.42 = (f32[3,3,64]{2,1,0:T(4,128)}, f32[3,3,64]{2,1,0:T(4,128)}, u32[]{:S(2)}, u32[]{:S(2)}) collective-permute-start(f32[3,3,64]{2,1,0:T(4,128)} %get-tuple-element.59), channel_id=1, source_target_pairs={{0,1},{1,0},{2,3},{3,2},{4,5},{5,4},{6,7},{7,6}} | collective-permute-start | bytes 6920 | tf_op jit(solution)/shard_map/ppermute | solution.py:11
  663.7 64.0 %collective-permute-start.41 = (f32[3,3,64]{2,1,0:T(4,128)}, f32[3,3,64]{2,1,0:T(4,128)}, u32[]{:S(2)}, u32[]{:S(2)}) collective-permute-start(f32[3,3,64]{2,1,0:T(4,128)} %get-tuple-element.58), channel_id=1, source_target_pairs={{0,1},{1,0},{2,3},{3,2},{4,5},{5,4},{6,7},{7,6}} | collective-permute-start | bytes 6920 | tf_op jit(solution)/shard_map/ppermute | solution.py:11
  746.4 102.5 %collective-permute-start.48 = (f32[768,768]{1,0:T(8,128)}, f32[768,768]{1,0:T(8,128)S(1)}, u32[]{:S(2)}, u32[]{:S(2)}) collective-permute-start(f32[768,768]{1,0:T(8,128)} %get-tuple-element.37), channel_id=1, source_target_pairs={{0,1},{1,0},{2,3},{3,2},{4,5},{5,4},{6,7},{7,6}} | collective-permute-start | bytes 7077896 | tf_op jit(solution)/shard_map/ppermute | solution.py:11
  762.3 84.8 %collective-permute-start.26 = (bf16[16,64,768]{2,1,0:T(8,128)(2,1)}, bf16[16,64,768]{2,1,0:T(8,128)(2,1)}, u32[]{:S(2)}, u32[]{:S(2)}) collective-permute-start(bf16[16,64,768]{2,1,0:T(8,128)(2,1)} %get-tuple-element.45), channel_id=1, source_target_pairs={{0,3},{1,2},{2,1},{3,0},{4,7},{5,6},{6,5},{7,4}} | collective-permute-start | bytes 4718600 | tf_op jit(solution)/shard_map/ppermute | solution.py:11
  784.5 65.0 %collective-permute-start.38 = (f32[3,768,3,64]{1,3,2,0:T(8,128)}, f32[3,768,3,64]{1,3,2,0:T(8,128)S(1)}, u32[]{:S(2)}, u32[]{:S(2)}) collective-permute-start(f32[3,768,3,64]{1,3,2,0:T(8,128)} %get-tuple-element.38), channel_id=1, source_target_pairs={{0,1},{1,0},{2,3},{3,2},{4,5},{5,4},{6,7},{7,6}} | collective-permute-start | bytes 5308424 | tf_op jit(solution)/shard_map/ppermute | solution.py:11
  789.8 61.3 %collective-permute-start.32 = (bf16[384,768]{1,0:T(8,128)(2,1)S(1)}, bf16[384,768]{1,0:T(8,128)(2,1)S(1)}, u32[]{:S(2)}, u32[]{:S(2)}) collective-permute-start(bf16[384,768]{1,0:T(8,128)(2,1)S(1)} %add_convert_fusion.2), channel_id=1, source_target_pairs={{0,1},{1,0},{2,3},{3,2},{4,5},{5,4},{6,7},{7,6}} | collective-permute-start | bytes 1769480 | tf_op jit(solution)/shard_map/ppermute | solution.py:11
  818.2 72.5 %collective-permute-start.53 = (f32[768,768]{1,0:T(8,128)}, f32[768,768]{1,0:T(8,128)}, u32[]{:S(2)}, u32[]{:S(2)}) collective-permute-start(f32[768,768]{1,0:T(8,128)} %get-tuple-element.34), channel_id=1, source_target_pairs={{0,1},{1,0},{2,3},{3,2},{4,5},{5,4},{6,7},{7,6}} | collective-permute-start | bytes 7077896 | tf_op jit(solution)/shard_map/ppermute | solution.py:11
  848.9 89.5 %collective-permute-start.55 = (f32[768,768]{1,0:T(8,128)S(1)}, f32[768,768]{1,0:T(8,128)}, u32[]{:S(2)}, u32[]{:S(2)}) collective-permute-start(f32[768,768]{1,0:T(8,128)S(1)} %slice_add_fusion), channel_id=1, source_target_pairs={{0,2},{1,3},{2,0},{3,1},{4,6},{5,7},{6,4},{7,5}} | collective-permute-start | bytes 7077896 | tf_op jit(solution)/shard_map/ppermute | solution.py:11
  849.6 92.6 %collective-permute-start.47 = (f32[768,768]{1,0:T(8,128)}, f32[768,768]{1,0:T(8,128)S(1)}, u32[]{:S(2)}, u32[]{:S(2)}) collective-permute-start(f32[768,768]{1,0:T(8,128)} %get-tuple-element.36), channel_id=1, source_target_pairs={{0,1},{1,0},{2,3},{3,2},{4,5},{5,4},{6,7},{7,6}} | collective-permute-start | bytes 7077896 | tf_op jit(solution)/shard_map/ppermute | solution.py:11
  851.1 137.6 %collective-permute-start.49 = (f32[768,768]{1,0:T(8,128)S(1)}, f32[768,768]{1,0:T(8,128)}, u32[]{:S(2)}, u32[]{:S(2)}) collective-permute-start(f32[768,768]{1,0:T(8,128)S(1)} %slice_add_fusion.2), channel_id=1, source_target_pairs={{0,2},{1,3},{2,0},{3,1},{4,6},{5,7},{6,4},{7,5}} | collective-permute-start | bytes 7077896 | tf_op jit(solution)/shard_map/ppermute | solution.py:11
  (120 other events, 3110.1 us)

commit v2 on v0

v2 whole, which is shorter than its diff:
```python
import functools
import jax
import jax.numpy as jnp
from jax import lax
from jax.experimental import pallas as pl
from jax.experimental.pallas import tpu as pltpu
from jax.sharding import PartitionSpec as P

LN_EPS = 1e-6
TP = 4
WIDE = jnp.float32
HALF = jnp.bfloat16
IMAGES = 16
TOK = 256
PART = 64
DIM = 768
GROUP = 2
ROWS = GROUP * TOK
STEPS = IMAGES // GROUP
PAIRS = 6
EXP_SCALE = 0.125 * 1.4426950408889634
GELU_C = 0.7978845608028654
GELU_A = 0.044715


def dot_nn(a, b):
    return lax.dot_general(a, b, (((1,), (0,)), ((), ())), preferred_element_type=WIDE)


def dot_nt(a, b):
    return lax.dot_general(a, b, (((1,), (1,)), ((), ())), preferred_element_type=WIDE)


def dot_tn(a, b):
    return lax.dot_general(a, b, (((0,), (0,)), ((), ())), preferred_element_type=WIDE)


def rows_of(slot_refs):
    return jnp.concatenate([r[g] for g in range(GROUP) for r in slot_refs], axis=0)


def stack_rows(refs, s):
    return jnp.concatenate([r[s] for r in refs], axis=0)


def join_rows(refs):
    return jnp.concatenate([r[...] for r in refs], axis=0)


def normalize(x_f):
    mean = jnp.sum(x_f, axis=-1, keepdims=True) * (1.0 / DIM)
    centered = x_f - mean
    var = jnp.sum(centered * centered, axis=-1, keepdims=True) * (1.0 / DIM)
    inv = lax.rsqrt(var + LN_EPS)
    return centered * inv, inv


def norm_back(d_out_f, xhat, inv, scale):
    d_hat = d_out_f * scale
    m1 = jnp.sum(d_hat, axis=-1, keepdims=True) * (1.0 / DIM)
    m2 = jnp.sum(d_hat * xhat, axis=-1, keepdims=True) * (1.0 / DIM)
    return (d_hat - m1 - xhat * m2) * inv


def lane_half(j):
    lane = lax.broadcasted_iota(jnp.int32, (1, 128), 1)
    return (lane < 64) if j == 0 else (lane >= 64)


def mask_half(x, j):
    return jnp.where(lane_half(j), x, jnp.zeros_like(x))


def col_sum(x):
    return jnp.sum(x, axis=0, keepdims=True)


def attn_fwd_kernel(p0, p1, p2, p3, pos, wp, vec, wq0, wq1, wq2, wq3, bqkv, wo0, wo1, wo2, wo3, e_ref, qkv_ref, o_ref, x1_ref):
    x = rows_of((p0, p1, p2, p3))
    posb = pos[...].astype(WIDE) + vec[0:1]
    emb = dot_nn(x, wp[...]) + jnp.concatenate([posb] * GROUP, axis=0)
    e_h = emb.astype(HALF)
    for g in range(GROUP):
        e_ref[g] = e_h[TOK * g:TOK * g + TOK]
    e_f = e_h.astype(WIDE)
    xhat, _ = normalize(e_f)
    h1 = (xhat * vec[1:2] + vec[2:3]).astype(HALF)
    for s in range(3):
        part = (dot_nt(h1, stack_rows((wq0, wq1, wq2, wq3), s)) + bqkv[s:s + 1]).astype(HALF)
        for g in range(GROUP):
            qkv_ref[g, :, DIM * s:DIM * s + DIM] = part[TOK * g:TOK * g + TOK]
    for g in range(GROUP):
        for pr in range(PAIRS):
            q = qkv_ref[g, :, 128 * pr:128 * pr + 128]
            k = qkv_ref[g, :, DIM + 128 * pr:DIM + 128 * pr + 128]
            v = qkv_ref[g, :, 2 * DIM + 128 * pr:2 * DIM + 128 * pr + 128]
            probs = []
            for j in range(2):
                s = dot_nt(mask_half(q, j), k)
                m = jnp.max(s, axis=-1, keepdims=True)
                e = jnp.exp2((s - m) * EXP_SCALE)
                l = jnp.sum(e, axis=-1, keepdims=True)
                probs.append((e * (1.0 / l)).astype(HALF))
            pv = dot_nn(jnp.concatenate(probs, axis=1), jnp.concatenate([mask_half(v, 0), mask_half(v, 1)], axis=0))
            o_ref[g, :, 128 * pr:128 * pr + 128] = pv.astype(HALF)
    o = jnp.concatenate([o_ref[g] for g in range(GROUP)], axis=0)
    e_f = jnp.concatenate([e_ref[g] for g in range(GROUP)], axis=0).astype(WIDE)
    x1 = (e_f + (dot_nn(o, join_rows((wo0, wo1, wo2, wo3))) + vec[3:4])).astype(HALF)
    for g in range(GROUP):
        x1_ref[g] = x1[TOK * g:TOK * g + TOK]


def fixed(shape):
    return pl.BlockSpec(shape, lambda i: (0,) * len(shape), pipeline_mode=pl.Buffered(1))


def slot_spec():
    return pl.BlockSpec((GROUP, PART, DIM), lambda i: (i, 0, 0))


def image_spec(width):
    return pl.BlockSpec((GROUP, TOK, width), lambda i: (i, 0, 0))


def params():
    return pltpu.CompilerParams(dimension_semantics=('arbitrary',), vmem_limit_bytes=63 * 1024 * 1024)


def image_shape(width):
    return jax.ShapeDtypeStruct((IMAGES, TOK, width), HALF)


def attn_fwd(p, pos, wp, vec, wqkv, bqkv, wo):
    return pl.pallas_call(
        attn_fwd_kernel,
        grid=(STEPS,),
        in_specs=[slot_spec()] * 4 + [fixed((TOK, DIM)), fixed((DIM, DIM)), fixed((8, DIM))] + [fixed((3, 192, DIM))] * 4 + [fixed((8, DIM))] + [fixed((192, DIM))] * 4,
        out_specs=[image_spec(DIM), image_spec(3 * DIM), image_spec(DIM), image_spec(DIM)],
        out_shape=[image_shape(DIM), image_shape(3 * DIM), image_shape(DIM), image_shape(DIM)],
        compiler_params=params(),
        cost_estimate=pl.CostEstimate(flops=60_000_000_000, bytes_accessed=50_000_000, transcendentals=12_000_000),
        name='attn_fwd',
    )(*p, pos, wp, vec, *wqkv, bqkv, *wo)


def mlp_kernel(x1_ref, o_ref, d0, d1, d2, d3, w10, w11, w12, w13, b1, w20, w21, w22, w23, wo0, wo1, wo2, wo3, vec, y0, y1, y2, y3, dx1_ref, do_ref, dw1_out, dw2_out, dwo_out, dvec_ref, db1_ref, dw1, dw2, dwo, sems):
    step = pl.program_id(0)
    w1 = (w10, w11, w12, w13)
    w2 = (w20, w21, w22, w23)

    @pl.when(step == 0)
    def _():
        dw1[...] = jnp.zeros_like(dw1)
        dw2[...] = jnp.zeros_like(dw2)
        dwo[...] = jnp.zeros_like(dwo)
        dvec_ref[...] = jnp.zeros_like(dvec_ref)
        db1_ref[...] = jnp.zeros_like(db1_ref)

    x1 = jnp.concatenate([x1_ref[g] for g in range(GROUP)], axis=0)
    dout = rows_of((d0, d1, d2, d3))
    xhat, inv = normalize(x1.astype(WIDE))
    h2 = (xhat * vec[0:1] + vec[1:2]).astype(HALF)
    y = None
    dh2 = None
    for f in range(TP):
        pre = dot_nn(h2, w1[f][...]) + b1[f:f + 1]
        sq = pre * pre
        t = jnp.tanh(pre * (GELU_C + (GELU_C * GELU_A) * sq))
        half_pre = 0.5 * pre
        hid = (half_pre + half_pre * t).astype(HALF)
        slope = (0.5 + 0.5 * t) + (half_pre * (1.0 - t * t)) * (GELU_C + (3.0 * GELU_C * GELU_A) * sq)
        dhid = dot_nt(dout, w2[f][...]).astype(HALF).astype(WIDE)
        dpre = dhid * slope
        db1_ref[f:f + 1] += col_sum(dpre)
        dpre_h = dpre.astype(HALF)
        part_y = dot_nn(hid, w2[f][...])
        part_h = dot_nt(dpre_h, w1[f][...])
        y = part_y if y is None else y + part_y
        dh2 = part_h if dh2 is None else dh2 + part_h
        dw1[f] += dot_tn(h2, dpre_h)
        dw2[f] += dot_tn(dout, hid)
    x2 = (x1.astype(WIDE) + (y + vec[2:3])).astype(HALF)
    for g in range(GROUP):
        for k, ref in enumerate((y0, y1, y2, y3)):
            ref[g] = x2[TOK * g + PART * k:TOK * g + PART * k + PART]
    dh2 = dh2.astype(HALF).astype(WIDE)
    xhat, inv = normalize(x1.astype(WIDE))
    dout_f = dout.astype(WIDE)
    dx1 = (dout_f + norm_back(dh2, xhat, inv, vec[0:1])).astype(HALF)
    dvec_ref[0:1] += col_sum(dh2 * xhat)
    dvec_ref[1:2] += col_sum(dh2)
    dvec_ref[2:3] += col_sum(dout_f)
    dvec_ref[3:4] += col_sum(dx1.astype(WIDE))
    d_o = dot_nt(dx1, join_rows((wo0, wo1, wo2, wo3))).astype(HALF)
    for g in range(GROUP):
        dx1_ref[g] = dx1[TOK * g:TOK * g + TOK]
        do_ref[g] = d_o[TOK * g:TOK * g + TOK]
    o = jnp.concatenate([o_ref[g] for g in range(GROUP)], axis=0)
    dwo[...] += dot_tn(o, dx1)

    @pl.when(step == STEPS - 1)
    def _():
        copies = [pltpu.make_async_copy(src, dst, sems.at[n]) for n, (src, dst) in enumerate(((dw1, dw1_out), (dw2, dw2_out), (dwo, dwo_out)))]
        for c in copies:
            c.start()
        for c in copies:
            c.wait()


def mlp(x1, o, dout, w1, b1, w2, wo, vec):
    any_spec = pl.BlockSpec(memory_space=pl.ANY)
    slot_shape = jax.ShapeDtypeStruct((IMAGES, PART, DIM), HALF)
    return pl.pallas_call(
        mlp_kernel,
        grid=(STEPS,),
        in_specs=[image_spec(DIM), image_spec(DIM)] + [slot_spec()] * 4 + [fixed((DIM, DIM))] * 4 + [fixed((8, DIM))] + [fixed((DIM, DIM))] * 4 + [fixed((192, DIM))] * 4 + [fixed((8, DIM))],
        out_specs=[slot_spec()] * 4 + [image_spec(DIM), image_spec(DIM), any_spec, any_spec, any_spec, pl.BlockSpec((8, DIM), lambda i: (0, 0)), pl.BlockSpec((8, DIM), lambda i: (0, 0))],
        out_shape=[slot_shape] * 4 + [image_shape(DIM), image_shape(DIM), jax.ShapeDtypeStruct((TP, DIM, DIM), WIDE), jax.ShapeDtypeStruct((TP, DIM, DIM), WIDE), jax.ShapeDtypeStruct((DIM, DIM), WIDE), jax.ShapeDtypeStruct((8, DIM), WIDE), jax.ShapeDtypeStruct((8, DIM), WIDE)],
        scratch_shapes=[pltpu.VMEM((TP, DIM, DIM), WIDE), pltpu.VMEM((TP, DIM, DIM), WIDE), pltpu.VMEM((DIM, DIM), WIDE), pltpu.SemaphoreType.DMA((3,))],
        compiler_params=params(),
        cost_estimate=pl.CostEstimate(flops=130_000_000_000, bytes_accessed=80_000_000, transcendentals=12_000_000),
        name='mlp',
    )(x1, o, *dout, *w1, b1, *w2, *wo, vec)


def attn_bwd_kernel(e_ref, qkv_ref, do_ref, dx1_ref, p0, p1, p2, p3, wq0, wq1, wq2, wq3, vec, dwqkv_out, dwp_out, dpos_ref, dvec_ref, dbqkv_ref, dqkv, dwqkv, dwp, sems):
    step = pl.program_id(0)

    @pl.when(step == 0)
    def _():
        dwqkv[...] = jnp.zeros_like(dwqkv)
        dwp[...] = jnp.zeros_like(dwp)
        dpos_ref[...] = jnp.zeros_like(dpos_ref)
        dvec_ref[...] = jnp.zeros_like(dvec_ref)
        dbqkv_ref[...] = jnp.zeros_like(dbqkv_ref)

    for g in range(GROUP):
        rows = slice(TOK * g, TOK * g + TOK)
        for pr in range(PAIRS):
            cols = slice(128 * pr, 128 * pr + 128)
            q = qkv_ref[g, :, 128 * pr:128 * pr + 128]
            k = qkv_ref[g, :, DIM + 128 * pr:DIM + 128 * pr + 128]
            v = qkv_ref[g, :, 2 * DIM + 128 * pr:2 * DIM + 128 * pr + 128]
            d_o = do_ref[g, :, 128 * pr:128 * pr + 128]
            probs = []
            dscores = []
            for j in range(2):
                s = dot_nt(k, mask_half(q, j))
                m = jnp.max(s, axis=0, keepdims=True)
                e = jnp.exp2((s - m) * EXP_SCALE)
                l = jnp.sum(e, axis=0, keepdims=True)
                p = e * (1.0 / l)
                dp = dot_nt(v, mask_half(d_o, j)).astype(HALF).astype(WIDE)
                delta = jnp.sum(dp * p, axis=0, keepdims=True)
                ds = (p * ((dp - delta) * 0.125)).astype(HALF)
                probs.append(p.astype(HALF))
                dscores.append(ds)
            dv = dot_nn(jnp.concatenate(probs, axis=1), jnp.concatenate([mask_half(d_o, 0), mask_half(d_o, 1)], axis=0))
            dk = dot_nn(jnp.concatenate(dscores, axis=1), jnp.concatenate([mask_half(q, 0), mask_half(q, 1)], axis=0))
            dq = dot_tn(jnp.concatenate(dscores, axis=0), jnp.concatenate([mask_half(k, 0), mask_half(k, 1)], axis=0))
            dqkv[rows, 128 * pr:128 * pr + 128] = dq.astype(HALF)
            dqkv[rows, DIM + 128 * pr:DIM + 128 * pr + 128] = dk.astype(HALF)
            dqkv[rows, 2 * DIM + 128 * pr:2 * DIM + 128 * pr + 128] = dv.astype(HALF)
    e_f = jnp.concatenate([e_ref[g] for g in range(GROUP)], axis=0).astype(WIDE)
    xhat, inv = normalize(e_f)
    h1 = (xhat * vec[1:2] + vec[2:3]).astype(HALF)
    dh1 = None
    for s in range(3):
        part = dqkv[:, DIM * s:DIM * s + DIM]
        dbqkv_ref[s:s + 1] += col_sum(part.astype(WIDE))
        dwqkv[s] += dot_tn(part, h1)
        term = dot_nn(part, stack_rows((wq0, wq1, wq2, wq3), s))
        dh1 = term if dh1 is None else dh1 + term
    dh1 = dh1.astype(HALF).astype(WIDE)
    dx1 = jnp.concatenate([dx1_ref[g] for g in range(GROUP)], axis=0).astype(WIDE)
    de = (dx1 + norm_back(dh1, xhat, inv, vec[1:2])).astype(HALF)
    de_f = de.astype(WIDE)
    dvec_ref[0:1] += col_sum(dh1 * xhat)
    dvec_ref[1:2] += col_sum(dh1)
    acc = de_f[0:TOK]
    for g in range(1, GROUP):
        acc = acc + de_f[TOK * g:TOK * g + TOK]
    dpos_ref[...] += acc
    x = rows_of((p0, p1, p2, p3))
    dwp[...] += dot_tn(x, de)

    @pl.when(step == STEPS - 1)
    def _():
        copies = [pltpu.make_async_copy(src, dst, sems.at[n]) for n, (src, dst) in enumerate(((dwqkv, dwqkv_out), (dwp, dwp_out)))]
        for c in copies:
            c.start()
        for c in copies:
            c.wait()


def attn_bwd(e, qkv, d_o, dx1, p, wqkv, vec):
    any_spec = pl.BlockSpec(memory_space=pl.ANY)
    return pl.pallas_call(
        attn_bwd_kernel,
        grid=(STEPS,),
        in_specs=[image_spec(DIM), image_spec(3 * DIM), image_spec(DIM), image_spec(DIM)] + [slot_spec()] * 4 + [fixed((3, 192, DIM))] * 4 + [fixed((8, DIM))],
        out_specs=[any_spec, any_spec, pl.BlockSpec((TOK, DIM), lambda i: (0, 0)), pl.BlockSpec((8, DIM), lambda i: (0, 0)), pl.BlockSpec((8, DIM), lambda i: (0, 0))],
        out_shape=[jax.ShapeDtypeStruct((3, DIM, DIM), WIDE), jax.ShapeDtypeStruct((DIM, DIM), WIDE), jax.ShapeDtypeStruct((TOK, DIM), WIDE), jax.ShapeDtypeStruct((8, DIM), WIDE), jax.ShapeDtypeStruct((8, DIM), WIDE)],
        scratch_shapes=[pltpu.VMEM((ROWS, 3 * DIM), HALF), pltpu.VMEM((3, DIM, DIM), WIDE), pltpu.VMEM((DIM, DIM), WIDE), pltpu.SemaphoreType.DMA((2,))],
        compiler_params=params(),
        cost_estimate=pl.CostEstimate(flops=100_000_000_000, bytes_accessed=80_000_000, transcendentals=12_000_000),
        name='attn_bwd',
    )(e, qkv, d_o, dx1, *p, *wqkv, vec)


def permute_xor(x, k):
    return lax.ppermute(x, 'tp', [(i, i ^ k) for i in range(TP)])


def exchange(x, me):
    blocks = x.reshape(TP, IMAGES, PART, DIM)
    picks = [lax.dynamic_index_in_dim(blocks, me ^ k, 0, keepdims=False) for k in range(TP)]
    return [picks[0]] + [permute_xor(picks[k], k) for k in range(1, TP)]


def give_back(slots, me):
    out = jnp.zeros((TP, IMAGES, PART, DIM), HALF)
    for k in range(TP):
        block = slots[k] if k == 0 else permute_xor(slots[k], k)
        out = lax.dynamic_update_index_in_dim(out, block, me ^ k, 0)
    return out.reshape(TP * IMAGES, PART, DIM)


def gather(w):
    w2 = permute_xor(w, 2)
    return [w, permute_xor(w, 1), w2, permute_xor(w2, 1)]


def reduce_slots(g):
    r1 = permute_xor(g[1], 1)
    r3 = permute_xor(g[3], 1)
    return (g[0] + r1) + permute_xor(g[2] + r3, 2)


def pad_rows(rows):
    rows = [r.astype(WIDE).reshape(-1, DIM) for r in rows]
    n = sum(r.shape[0] for r in rows)
    return jnp.concatenate(rows + [jnp.zeros((8 - n, DIM), WIDE)], axis=0)


def group_step(patches, patch_w, patch_b, pos_emb, ln_scale, ln_bias, qkv_w, qkv_b, out_w, out_b, fc1_w, fc1_b, fc2_w, fc2_b, d_out):
    me = lax.axis_index('tp')
    p = exchange(patches, me)
    wqkv = gather(qkv_w.transpose(0, 2, 3, 1).reshape(3, 192, DIM))
    small = jnp.concatenate([pos_emb, jnp.pad(qkv_b.reshape(3, 192), ((0, 0), (0, DIM - 192))), fc1_b.reshape(1, DIM), jnp.zeros((12, DIM), HALF)], axis=0)
    small = gather(small)
    wo = gather(out_w.reshape(192, DIM))
    w1 = gather(fc1_w)
    w2 = gather(fc2_w)
    dout = exchange(d_out, me)
    pos = jnp.concatenate([s[0:PART] for s in small], axis=0)
    bqkv = pad_rows([jnp.concatenate([s[PART:PART + 3, :192] for s in small], axis=1)])
    b1 = pad_rows([s[PART + 3] for s in small])
    vec1 = pad_rows([patch_b, ln_scale[0], ln_bias[0], out_b])
    vec2 = pad_rows([ln_scale[1], ln_bias[1], fc2_b])
    e, qkv, o, x1 = attn_fwd(p, pos, patch_w, vec1, wqkv, bqkv, wo)
    y0, y1, y2, y3, dx1, d_o, dw1, dw2, dwo, dvec2, db1 = mlp(x1, o, dout, w1, b1, w2, wo, vec2)
    x_two = give_back([y0, y1, y2, y3], me)
    d_fc2_w = reduce_slots([dw2[k] for k in range(TP)]).T
    d_fc1_w = reduce_slots([dw1[k] for k in range(TP)])
    d_out_w = reduce_slots([dwo[192 * k:192 * k + 192] for k in range(TP)])
    dwqkv, dwp, dpos, dvec1, dbqkv = attn_bwd(e, qkv, d_o, dx1, p, wqkv, vec1)
    d_qkv_w = reduce_slots([dwqkv[:, 192 * k:192 * k + 192] for k in range(TP)])
    d_qkv_w = d_qkv_w.astype(HALF).reshape(3, 3, 64, DIM).transpose(0, 3, 1, 2)
    small = reduce_slots([jnp.concatenate([dpos[PART * k:PART * k + PART], jnp.pad(dbqkv[0:3, 192 * k:192 * k + 192], ((0, 0), (0, DIM - 192))), db1[k:k + 1], jnp.zeros((4, DIM), WIDE)], axis=0) for k in range(TP)])
    d_pos = small[0:PART]
    d_qkv_b = small[PART:PART + 3, :192].reshape(3, 3, 64)
    d_fc1_b = small[PART + 3]
    d_patch_b = jnp.sum(dpos, axis=0)
    vec = pad_rows([d_patch_b, dvec1[0], dvec2[0], dvec1[1], dvec2[1], dvec2[3], dvec2[2]])
    vec = vec + permute_xor(vec, 1)
    vec = (vec + permute_xor(vec, 2)).astype(HALF)
    core = me % 2
    halves = dwp.reshape(2, 384, DIM)
    mine = lax.dynamic_index_in_dim(halves, core, 0, keepdims=False)
    other = lax.dynamic_index_in_dim(halves, 1 - core, 0, keepdims=False)
    mine = mine + permute_xor(other, 1)
    mine = (mine + permute_xor(mine, 2)).astype(HALF)
    theirs = permute_xor(mine, 1)
    first = core == 0
    d_patch_w = jnp.concatenate([jnp.where(first, mine, theirs), jnp.where(first, theirs, mine)], axis=0)
    return (x_two, d_patch_w, vec[0], d_pos.astype(HALF), vec[1:3], vec[3:5], d_qkv_w, d_qkv_b.astype(HALF), d_out_w.astype(HALF).reshape(3, 64, DIM), vec[5], d_fc1_w.astype(HALF), d_fc1_b.astype(HALF), d_fc2_w.astype(HALF), vec[6])


def solution(mesh):
    in_specs = (P('dp', 'tp', None), P(), P(), P('tp', None), P(), P(), P(None, None, 'tp', None), P(None, 'tp', None), P('tp', None, None), P(), P(None, 'tp'), P('tp'), P('tp', None), P(), P('dp', 'tp', None))
    out_specs = (P('dp', 'tp', None), P('dp', None), P('dp'), P(('dp', 'tp'), None), P('dp', None), P('dp', None), P('dp', None, 'tp', None), P('dp', 'tp', None), P(('dp', 'tp'), None, None), P('dp'), P('dp', 'tp'), P(('dp', 'tp')), P(('dp', 'tp'), None), P('dp'))
    return jax.shard_map(group_step, mesh=mesh, in_specs=in_specs, out_specs=out_specs, check_vma=False)
```

time: 2530 us -> 790 us (0.31)
  waiting for transfers between devices: 1720 us -> 330 us
  matrix products: 588 us -> 0 us
  Pallas kernels: 0 us -> 344 us
  other arithmetic: 148 us -> 27 us
  blocking collectives: 45.6 us -> 0 us
  local copies, waits for them, and re-layouts: 9.94 us -> 55.3 us
    reduce_scatter x4 -> x0, waiting for transfers between devices: 1130 us -> none  [the longest x1 326 us: group_step(): lax.psum_scatter(attn_part, 'tp', scatter_dimension=1, tiled=True)]
    dot_general x20 -> x0, matrix products: 588 us -> none  [the longest x1 59.9 us: group_step(): jnp.einsum('btd,fd->btf', d_out_all, fc2_w, preferred_element_type=wide)]
    all_gather x4 -> x0, waiting for transfers between devices: 583 us -> none  [the longest x1 155 us: group_step(): h_one_all = lax.all_gather(h_one_f.astype(half), 'tp', axis=1, tiled=True)]
    pallas_call x0 -> x3, Pallas kernels: none -> 344 us  [the longest x1 158 us: mlp(): pl.pallas_call(mlp_kernel, grid=(STEPS,), in_specs=[image_spec(DIM), imag...]
    ppermute x0 -> x44, waiting for transfers between devices: none -> 330 us  [permute_xor(): return lax.ppermute(x, 'tp', [(i, i ^ k) for i in range(TP)])]
    reduce_sum x11 -> x1, other arithmetic: 82 us -> 0.07 us  [group_step(): d_patch_b = jnp.sum(dpos, axis=0)]
    sub x1 -> x0, other arithmetic: 54.1 us -> none  [group_step(): probs = jax.nn.softmax(scores, axis=-1)]
    psum x1 -> x0, blocking collectives: 45.6 us -> none  [group_step(): lax.psum((d_patch_w, d_patch_b, d_ln_scale, d_ln_bias, d_out_b, d_fc2_b),...]
  transfers between devices with their start and end apart: 8 -> 44, of which waited for: 8 -> 14; matrix products, arithmetic and copies ran while one was open for 8% -> 9% of each run, Pallas kernels for 0% -> 24%
where the time goes in v2:
time: 790 us; the launch traced here: 782 us
  Pallas kernels  344 us (44%)
  waiting for transfers between devices  330 us (42%)
  local copies, waits for them, and re-layouts  55.3 us (7%)
  other arithmetic  27 us (3%)
  starting transfers between devices  23.8 us (3%)
    ppermute x44, waiting for transfers between devices, permute_xor(): return lax.ppermute(x, 'tp', [(i, i ^ k) for i in range(TP)])  330 us
    pallas_call x1, Pallas kernels, mlp(): pl.pallas_call(mlp_kernel, grid=(STEPS,), in_specs=[image_spec(DIM), imag...  158 us
    pallas_call x1, Pallas kernels, attn_bwd(): pl.pallas_call(attn_bwd_kernel, grid=(STEPS,), in_specs=[image_spec(DIM),...  112 us
    pallas_call x1, Pallas kernels, attn_fwd(): pl.pallas_call(attn_fwd_kernel, grid=(STEPS,), in_specs=[slot_spec()] * 4...  74.6 us
    ppermute x44, starting transfers between devices, permute_xor(): return lax.ppermute(x, 'tp', [(i, i ^ k) for i in range(TP)])  23.8 us
  transfers between devices with their start and end apart: 44, of which 14 were waited for; matrix products, arithmetic and copies ran while one was open for 9% of the time, Pallas kernels for 24%

profile of v2, /device:TPU:0, one launch (start us, length us, event | category | flops | bytes accessed | tf_op | source)
XLA Modules:
  0.0 781.7 jit_solution(12576296534289581471)
XLA Ops:
  0.6 3.4 collective-permute-start.16
  6.6 26.0 %collective-permute-done.4 = bf16[80,768]{1,0:T(8,128)(2,1)S(1)} collective-permute-done((bf16[80,768]{1,0:T(8,128)(2,1)S(1)}, bf16[80,768]{1,0:T(8,128)(2,1)S(1)}, u32[]{:S(2)}, u32[]{:S(2)}) %collective-permute-start.4) | collective-permute-done | bytes 122912 | tf_op jit(solution)/shard_map/ppermute | solution.py:312
  35.6 6.9 collective-permute-done.10.wo2
  45.7 5.2 dynamic-slice_bitcast_fusion.4
  50.9 10.6 %collective-permute-done.7.wq2 = bf16[3,192,768]{2,1,0:T(8,128)(2,1)} collective-permute-done((bf16[3,192,768]{2,1,0:T(8,128)(2,1)}, bf16[3,192,768]{2,1,0:T(8,128)(2,1)}, u32[]{:S(2)}, u32[]{:S(2)}) %collective-permute-start.7) | collective-permute-done | bytes 884768 | tf_op jit(solution)/shard_map/ppermute | solution.py:312
  64.9 21.9 %collective-permute-done.19.w22 = bf16[768,768]{1,0:T(8,128)(2,1)} collective-permute-done((bf16[768,768]{1,0:T(8,128)(2,1)}, bf16[768,768]{1,0:T(8,128)(2,1)}, u32[]{:S(2)}, u32[]{:S(2)}) %collective-permute-start.19) | collective-permute-done | bytes 1179680 | tf_op jit(solution)/shard_map/ppermute | solution.py:312
  86.7 5.7 dynamic-slice_bitcast_fusion
  100.0 20.5 %collective-permute-done.1.p2 = bf16[16,64,768]{2,1,0:T(8,128)(2,1)} collective-permute-done((bf16[16,64,768]{2,1,0:T(8,128)(2,1)S(1)}, bf16[16,64,768]{2,1,0:T(8,128)(2,1)}, u32[]{:S(2)}, u32[]{:S(2)}) %collective-permute-start.1) | collective-permute-done | bytes 1572896 | tf_op jit(solution)/shard_map/ppermute | solution.py:312
  121.1 32.3 %collective-permute-done.2.p3 = bf16[16,64,768]{2,1,0:T(8,128)(2,1)} collective-permute-done((bf16[16,64,768]{2,1,0:T(8,128)(2,1)S(1)}, bf16[16,64,768]{2,1,0:T(8,128)(2,1)}, u32[]{:S(2)}, u32[]{:S(2)}) %collective-permute-start.2) | collective-permute-done | bytes 1572896 | tf_op jit(solution)/shard_map/ppermute | solution.py:312
  154.0 74.6 %attn_fwd.1 = (bf16[16,256,768]{2,1,0:T(8,128)(2,1)}, bf16[16,256,2304]{2,1,0:T(8,128)(2,1)}, bf16[16,256,768]{2,1,0:T(8,128)(2,1)}, bf16[16,256,768]{2,1,0:T(8,128)(2,1)}) custom-call(bf16[16,64,768]{2,1,0:T(8,128)(2,1)} %get-tuple-element.84.p0, bf16[16,64,768]{2,1,0:T(8,128)(2,1)} %collective-permute-done.p1, ...), custom_call_target="tpu_custom_call" | custom-call | flops 60000002048 | bytes 50000000 | tf_op jit(solution)/shard_map/attn_fwd/pallas_call | solution.py:134
  228.6 158.0 %mlp.1 = (bf16[16,64,768]{2,1,0:T(8,128)(2,1)}, bf16[16,64,768]{2,1,0:T(8,128)(2,1)}, bf16[16,64,768]{2,1,0:T(8,128)(2,1)}, bf16[16,64,768]{2,1,0:T(8,128)(2,1)}...) custom-call(bf16[16,256,768]{2,1,0:T(8,128)(2,1)} %get-tuple-element, ...), custom_call_target="tpu_custom_call" | custom-call | flops 130000003072 | bytes 80000000 | tf_op jit(solution)/shard_map/mlp/pallas_call | solution.py:213
  389.5 111.6 %attn_bwd.1 = (f32[3,768,768]{2,1,0:T(8,128)}, f32[768,768]{1,0:T(8,128)}, f32[256,768]{1,0:T(8,128)}, f32[8,768]{1,0:T(8,128)}, f32[8,768]{1,0:T(8,128)}) custom-call(bf16[16,256,768]{2,1,0:T(8,128)(2,1)} %get-tuple-element.40.e_ref, bf16[16,256,2304]{2,1,0:T(8,128)(2,1)} %get-tuple-element.41.qkv_ref, bf16[16,256,768]{2,1,0:T(8,128)(2,1)} %get-tuple-element.42.do_ref, ...), custom_call_target="tpu_custom_call" | custom-call | flops 99999997952 | bytes 80000000 | tf_op jit(solution)/shard_map/attn_bwd/pallas_call | solution.py:298
  509.4 4.4 fusion.27
  514.3 5.1 slice_bitcast_fusion.1
  520.9 6.3 collective-permute-done.31
  531.9 11.5 %collective-permute-done.37 = f32[192,768]{1,0:T(8,128)S(1)} collective-permute-done((f32[192,768]{1,0:T(8,128)S(1)}, f32[192,768]{1,0:T(8,128)S(1)}, u32[]{:S(2)}, u32[]{:S(2)}) %collective-permute-start.37) | collective-permute-done | bytes 589856 | tf_op jit(solution)/shard_map/ppermute | solution.py:312
  544.3 3.5 broadcast_in_dim.22
  552.1 16.6 %collective-permute-done.25 = f32[384,768]{1,0:T(8,128)S(1)} collective-permute-done((f32[384,768]{1,0:T(8,128)S(1)}, f32[384,768]{1,0:T(8,128)S(1)}, u32[]{:S(2)}, u32[]{:S(2)}) %collective-permute-start.25) | collective-permute-done | bytes 1179680 | tf_op jit(solution)/shard_map/ppermute | solution.py:312
  576.5 26.0 %collective-permute-done.22 = bf16[16,64,768]{2,1,0:T(8,128)(2,1)} collective-permute-done((bf16[16,64,768]{2,1,0:T(8,128)(2,1)}, bf16[16,64,768]{2,1,0:T(8,128)(2,1)}, u32[]{:S(2)}, u32[]{:S(2)}) %collective-permute-start.22) | collective-permute-done | bytes 1572896 | tf_op jit(solution)/shard_map/ppermute | solution.py:312
  602.4 32.7 %collective-permute-done.23 = bf16[16,64,768]{2,1,0:T(8,128)(2,1)} collective-permute-done((bf16[16,64,768]{2,1,0:T(8,128)(2,1)}, bf16[16,64,768]{2,1,0:T(8,128)(2,1)}, u32[]{:S(2)}, u32[]{:S(2)}) %collective-permute-start.23) | collective-permute-done | bytes 1572896 | tf_op jit(solution)/shard_map/ppermute | solution.py:312
  651.5 25.1 %collective-permute-done.34 = f32[3,192,768]{2,1,0:T(8,128)S(1)} collective-permute-done((f32[3,192,768]{2,1,0:T(8,128)S(1)}, f32[3,192,768]{2,1,0:T(8,128)S(1)}, u32[]{:S(2)}, u32[]{:S(2)}) %collective-permute-start.34) | collective-permute-done | bytes 1769504 | tf_op jit(solution)/shard_map/ppermute | solution.py:312
  679.9 47.3 %collective-permute-done.43 = f32[768,768]{1,0:T(8,128)S(1)} collective-permute-done((f32[768,768]{1,0:T(8,128)S(1)}, f32[768,768]{1,0:T(8,128)S(1)}, u32[]{:S(2)}, u32[]{:S(2)}) %collective-permute-start.43) | collective-permute-done | bytes 2359328 | tf_op jit(solution)/shard_map/ppermute | solution.py:312
  730.8 46.3 %collective-permute-done.40 = f32[768,768]{1,0:T(8,128)} collective-permute-done((f32[768,768]{1,0:T(8,128)S(1)}, f32[768,768]{1,0:T(8,128)}, u32[]{:S(2)}, u32[]{:S(2)}) %collective-permute-start.40) | collective-permute-done | bytes 2359328 | tf_op jit(solution)/shard_map/ppermute | solution.py:312
  777.1 4.5 fusion.3
  (204 shorter events, 74.4 us)
Async XLA Ops:
  0.6 62.6 %collective-permute-start.16 = (bf16[768,768]{1,0:T(8,128)(2,1)}, bf16[768,768]{1,0:T(8,128)(2,1)}, u32[]{:S(2)}, u32[]{:S(2)}) collective-permute-start(bf16[768,768]{1,0:T(8,128)(2,1)} %w10.1), channel_id=1, source_target_pairs={{0,2},{1,3},{2,0},{3,1},{4,6},{5,7},{6,4},{7,5}} | collective-permute-start | bytes 3538952 | tf_op jit(solution)/shard_map/ppermute | solution.py:312
  43.2 43.5 %collective-permute-start.19 = (bf16[768,768]{1,0:T(8,128)(2,1)}, bf16[768,768]{1,0:T(8,128)(2,1)}, u32[]{:S(2)}, u32[]{:S(2)}) collective-permute-start(bf16[768,768]{1,0:T(8,128)(2,1)} %w20.1), channel_id=1, source_target_pairs={{0,2},{1,3},{2,0},{3,1},{4,6},{5,7},{6,4},{7,5}} | collective-permute-start | bytes 3538952 | tf_op jit(solution)/shard_map/ppermute | solution.py:312
  45.0 47.5 %collective-permute-start.15 = (bf16[768,768]{1,0:T(8,128)(2,1)}, bf16[768,768]{1,0:T(8,128)(2,1)}, u32[]{:S(2)}, u32[]{:S(2)}) collective-permute-start(bf16[768,768]{1,0:T(8,128)(2,1)} %w10.1), channel_id=1, source_target_pairs={{0,1},{1,0},{2,3},{3,2},{4,5},{5,4},{6,7},{7,6}} | collective-permute-start | bytes 3538952 | tf_op jit(solution)/shard_map/ppermute | solution.py:312
  61.5 59.0 %collective-permute-start.1 = (bf16[16,64,768]{2,1,0:T(8,128)(2,1)S(1)}, bf16[16,64,768]{2,1,0:T(8,128)(2,1)}, u32[]{:S(2)}, u32[]{:S(2)}) collective-permute-start(bf16[16,64,768]{2,1,0:T(8,128)(2,1)S(1)} %get-tuple-element.82), channel_id=1, source_target_pairs={{0,2},{1,3},{2,0},{3,1},{4,6},{5,7},{6,4},{7,5}} | collective-permute-start | bytes 4718600 | tf_op jit(solution)/shard_map/ppermute | solution.py:312
  63.2 90.2 %collective-permute-start.2 = (bf16[16,64,768]{2,1,0:T(8,128)(2,1)S(1)}, bf16[16,64,768]{2,1,0:T(8,128)(2,1)}, u32[]{:S(2)}, u32[]{:S(2)}) collective-permute-start(bf16[16,64,768]{2,1,0:T(8,128)(2,1)S(1)} %get-tuple-element.81), channel_id=1, source_target_pairs={{0,3},{1,2},{2,1},{3,0},{4,7},{5,6},{6,5},{7,4}} | collective-permute-start | bytes 4718600 | tf_op jit(solution)/shard_map/ppermute | solution.py:312
  92.5 61.4 %collective-permute-start.8 = (bf16[3,192,768]{2,1,0:T(8,128)(2,1)}, bf16[3,192,768]{2,1,0:T(8,128)(2,1)}, u32[]{:S(2)}, u32[]{:S(2)}) collective-permute-start(bf16[3,192,768]{2,1,0:T(8,128)(2,1)} %collective-permute-done.7.wq2), channel_id=1, source_target_pairs={{0,1},{1,0},{2,3},{3,2},{4,5},{5,4},{6,7},{7,6}} | collective-permute-start | bytes 2654216 | tf_op jit(solution)/shard_map/ppermute | solution.py:312
  98.2 130.4 %collective-permute-start.12 = (bf16[16,64,768]{2,1,0:T(8,128)(2,1)}, bf16[16,64,768]{2,1,0:T(8,128)(2,1)}, u32[]{:S(2)}, u32[]{:S(2)}) collective-permute-start(bf16[16,64,768]{2,1,0:T(8,128)(2,1)} %get-tuple-element.79), channel_id=1, source_target_pairs={{0,1},{1,0},{2,3},{3,2},{4,5},{5,4},{6,7},{7,6}} | collective-permute-start | bytes 4718600 | tf_op jit(solution)/shard_map/ppermute | solution.py:312
  98.2 130.4 %collective-permute-start.13 = (bf16[16,64,768]{2,1,0:T(8,128)(2,1)}, bf16[16,64,768]{2,1,0:T(8,128)(2,1)}, u32[]{:S(2)}, u32[]{:S(2)}) collective-permute-start(bf16[16,64,768]{2,1,0:T(8,128)(2,1)} %get-tuple-element.78), channel_id=1, source_target_pairs={{0,2},{1,3},{2,0},{3,1},{4,6},{5,7},{6,4},{7,5}} | collective-permute-start | bytes 4718600 | tf_op jit(solution)/shard_map/ppermute | solution.py:312
  120.4 108.1 %collective-permute-start.14 = (bf16[16,64,768]{2,1,0:T(8,128)(2,1)}, bf16[16,64,768]{2,1,0:T(8,128)(2,1)}, u32[]{:S(2)}, u32[]{:S(2)}) collective-permute-start(bf16[16,64,768]{2,1,0:T(8,128)(2,1)} %get-tuple-element.77), channel_id=1, source_target_pairs={{0,3},{1,2},{2,1},{3,0},{4,7},{5,6},{6,5},{7,4}} | collective-permute-start | bytes 4718600 | tf_op jit(solution)/shard_map/ppermute | solution.py:312
  153.4 75.2 %collective-permute-start.17 = (bf16[768,768]{1,0:T(8,128)(2,1)}, bf16[768,768]{1,0:T(8,128)(2,1)}, u32[]{:S(2)}, u32[]{:S(2)}) collective-permute-start(bf16[768,768]{1,0:T(8,128)(2,1)} %collective-permute-done.16.w12), channel_id=1, source_target_pairs={{0,1},{1,0},{2,3},{3,2},{4,5},{5,4},{6,7},{7,6}} | collective-permute-start | bytes 3538952 | tf_op jit(solution)/shard_map/ppermute | solution.py:312
  154.0 74.6 %collective-permute-start.20 = (bf16[768,768]{1,0:T(8,128)(2,1)}, bf16[768,768]{1,0:T(8,128)(2,1)}, u32[]{:S(2)}, u32[]{:S(2)}) collective-permute-start(bf16[768,768]{1,0:T(8,128)(2,1)} %collective-permute-done.19.w22), channel_id=1, source_target_pairs={{0,1},{1,0},{2,3},{3,2},{4,5},{5,4},{6,7},{7,6}} | collective-permute-start | bytes 3538952 | tf_op jit(solution)/shard_map/ppermute | solution.py:312
  389.0 130.5 %collective-permute-start.36 = (f32[192,768]{1,0:T(8,128)}, f32[192,768]{1,0:T(8,128)S(1)}, u32[]{:S(2)}, u32[]{:S(2)}) collective-permute-start(f32[192,768]{1,0:T(8,128)} %get-tuple-element.86), channel_id=1, source_target_pairs={{0,1},{1,0},{2,3},{3,2},{4,5},{5,4},{6,7},{7,6}} | collective-permute-start | bytes 1769480 | tf_op jit(solution)/shard_map/ppermute | solution.py:312
  389.5 138.4 %collective-permute-start.35 = (f32[192,768]{1,0:T(8,128)}, f32[192,768]{1,0:T(8,128)}, u32[]{:S(2)}, u32[]{:S(2)}) collective-permute-start(f32[192,768]{1,0:T(8,128)} %get-tuple-element.85), channel_id=1, source_target_pairs={{0,1},{1,0},{2,3},{3,2},{4,5},{5,4},{6,7},{7,6}} | collective-permute-start | bytes 1769480 | tf_op jit(solution)/shard_map/ppermute | solution.py:312
  527.2 45.9 %collective-permute-start.42 = (f32[768,768]{1,0:T(8,128)}, f32[768,768]{1,0:T(8,128)}, u32[]{:S(2)}, u32[]{:S(2)}) collective-permute-start(f32[768,768]{1,0:T(8,128)} %get-tuple-element.72), channel_id=1, source_target_pairs={{0,1},{1,0},{2,3},{3,2},{4,5},{5,4},{6,7},{7,6}} | collective-permute-start | bytes 7077896 | tf_op jit(solution)/shard_map/ppermute | solution.py:312
  544.2 91.2 %collective-permute-start.39 = (f32[768,768]{1,0:T(8,128)}, f32[768,768]{1,0:T(8,128)}, u32[]{:S(2)}, u32[]{:S(2)}) collective-permute-start(f32[768,768]{1,0:T(8,128)} %get-tuple-element.74), channel_id=1, source_target_pairs={{0,1},{1,0},{2,3},{3,2},{4,5},{5,4},{6,7},{7,6}} | collective-permute-start | bytes 7077896 | tf_op jit(solution)/shard_map/ppermute | solution.py:312
  549.0 53.4 %collective-permute-start.22 = (bf16[16,64,768]{2,1,0:T(8,128)(2,1)}, bf16[16,64,768]{2,1,0:T(8,128)(2,1)}, u32[]{:S(2)}, u32[]{:S(2)}) collective-permute-start(bf16[16,64,768]{2,1,0:T(8,128)(2,1)} %get-tuple-element.38), channel_id=1, source_target_pairs={{0,2},{1,3},{2,0},{3,1},{4,6},{5,7},{6,4},{7,5}} | collective-permute-start | bytes 4718600 | tf_op jit(solution)/shard_map/ppermute | solution.py:312
  549.3 85.9 %collective-permute-start.23 = (bf16[16,64,768]{2,1,0:T(8,128)(2,1)}, bf16[16,64,768]{2,1,0:T(8,128)(2,1)}, u32[]{:S(2)}, u32[]{:S(2)}) collective-permute-start(bf16[16,64,768]{2,1,0:T(8,128)(2,1)} %get-tuple-element.39), channel_id=1, source_target_pairs={{0,3},{1,2},{2,1},{3,0},{4,7},{5,6},{6,5},{7,4}} | collective-permute-start | bytes 4718600 | tf_op jit(solution)/shard_map/ppermute | solution.py:312
  568.7 71.1 %collective-permute-start.32 = (f32[3,192,768]{2,1,0:T(8,128)}, f32[3,192,768]{2,1,0:T(8,128)}, u32[]{:S(2)}, u32[]{:S(2)}) collective-permute-start(f32[3,192,768]{2,1,0:T(8,128)} %get-tuple-element.75), channel_id=1, source_target_pairs={{0,1},{1,0},{2,3},{3,2},{4,5},{5,4},{6,7},{7,6}} | collective-permute-start | bytes 5308424 | tf_op jit(solution)/shard_map/ppermute | solution.py:312
  573.1 66.8 %collective-permute-start.26 = (bf16[384,768]{1,0:T(8,128)(2,1)S(1)}, bf16[384,768]{1,0:T(8,128)(2,1)S(1)}, u32[]{:S(2)}, u32[]{:S(2)}) collective-permute-start(bf16[384,768]{1,0:T(8,128)(2,1)S(1)} %add_convert_fusion.1), channel_id=1, source_target_pairs={{0,1},{1,0},{2,3},{3,2},{4,5},{5,4},{6,7},{7,6}} | collective-permute-start | bytes 1769480 | tf_op jit(solution)/shard_map/ppermute | solution.py:312
  602.4 77.5 %collective-permute-start.41 = (f32[768,768]{1,0:T(8,128)S(1)}, f32[768,768]{1,0:T(8,128)S(1)}, u32[]{:S(2)}, u32[]{:S(2)}) collective-permute-start(f32[768,768]{1,0:T(8,128)S(1)} %copy-done.2), channel_id=1, source_target_pairs={{0,1},{1,0},{2,3},{3,2},{4,5},{5,4},{6,7},{7,6}} | collective-permute-start | bytes 7077896 | tf_op jit(solution)/shard_map/ppermute | solution.py:312
  635.1 41.5 %collective-permute-start.34 = (f32[3,192,768]{2,1,0:T(8,128)S(1)}, f32[3,192,768]{2,1,0:T(8,128)S(1)}, u32[]{:S(2)}, u32[]{:S(2)}) collective-permute-start(f32[3,192,768]{2,1,0:T(8,128)S(1)} %slice_add_fusion), channel_id=1, source_target_pairs={{0,2},{1,3},{2,0},{3,1},{4,6},{5,7},{6,4},{7,5}} | collective-permute-start | bytes 5308424 | tf_op jit(solution)/shard_map/ppermute | solution.py:312
  635.4 91.7 %collective-permute-start.43 = (f32[768,768]{1,0:T(8,128)S(1)}, f32[768,768]{1,0:T(8,128)S(1)}, u32[]{:S(2)}, u32[]{:S(2)}) collective-permute-start(f32[768,768]{1,0:T(8,128)S(1)} %bitcast_add_fusion), channel_id=1, source_target_pairs={{0,2},{1,3},{2,0},{3,1},{4,6},{5,7},{6,4},{7,5}} | collective-permute-start | bytes 7077896 | tf_op jit(solution)/shard_map/ppermute | solution.py:312
  639.9 90.9 %collective-permute-start.38 = (f32[768,768]{1,0:T(8,128)}, f32[768,768]{1,0:T(8,128)}, u32[]{:S(2)}, u32[]{:S(2)}) collective-permute-start(f32[768,768]{1,0:T(8,128)} %get-tuple-element.73), channel_id=1, source_target_pairs={{0,1},{1,0},{2,3},{3,2},{4,5},{5,4},{6,7},{7,6}} | collective-permute-start | bytes 7077896 | tf_op jit(solution)/shard_map/ppermute | solution.py:312
  639.9 137.2 %collective-permute-start.40 = (f32[768,768]{1,0:T(8,128)S(1)}, f32[768,768]{1,0:T(8,128)}, u32[]{:S(2)}, u32[]{:S(2)}) collective-permute-start(f32[768,768]{1,0:T(8,128)S(1)} %bitcast_add_fusion.2), channel_id=1, source_target_pairs={{0,2},{1,3},{2,0},{3,1},{4,6},{5,7},{6,4},{7,5}} | collective-permute-start | bytes 7077896 | tf_op jit(solution)/shard_map/ppermute | solution.py:312
  (52 other events, 1019.7 us)

commit v3 on v2

v3 whole, which is shorter than its diff:
```python
import functools
import jax
import jax.numpy as jnp
from jax import lax
from jax.experimental import pallas as pl
from jax.experimental.pallas import tpu as pltpu
from jax.sharding import PartitionSpec as P

LN_EPS = 1e-6
TP = 4
WIDE = jnp.float32
HALF = jnp.bfloat16
IMAGES = 16
TOK = 256
PART = 64
DIM = 768
GROUP = 2
ROWS = GROUP * TOK
STEPS = IMAGES // GROUP
PAIRS = 6
EXP_SCALE = 0.125 * 1.4426950408889634
GELU_C = 0.7978845608028654
GELU_A = 0.044715
AHEAD = 3
PACK = 2 * DIM + 192


def dot_nn(a, b):
    return lax.dot_general(a, b, (((1,), (0,)), ((), ())), preferred_element_type=WIDE)


def dot_nt(a, b):
    return lax.dot_general(a, b, (((1,), (1,)), ((), ())), preferred_element_type=WIDE)


def dot_tn(a, b):
    return lax.dot_general(a, b, (((0,), (0,)), ((), ())), preferred_element_type=WIDE)


def normalize(x_f):
    mean = jnp.sum(x_f, axis=-1, keepdims=True) * (1.0 / DIM)
    centered = x_f - mean
    var = jnp.sum(centered * centered, axis=-1, keepdims=True) * (1.0 / DIM)
    inv = lax.rsqrt(var + LN_EPS)
    return centered * inv, inv


def norm_back(d_out_f, xhat, inv, scale):
    d_hat = d_out_f * scale
    m1 = jnp.sum(d_hat, axis=-1, keepdims=True) * (1.0 / DIM)
    m2 = jnp.sum(d_hat * xhat, axis=-1, keepdims=True) * (1.0 / DIM)
    return (d_hat - m1 - xhat * m2) * inv


def lane_half(j):
    lane = lax.broadcasted_iota(jnp.int32, (1, 128), 1)
    return (lane < 64) if j == 0 else (lane >= 64)


def mask_half(x, j):
    return jnp.where(lane_half(j), x, jnp.zeros_like(x))


def col_sum(x):
    return jnp.sum(x, axis=0, keepdims=True)


def peers():
    me = lax.axis_index('tp')
    core = lax.rem(me, 2)
    chip = lax.div(me, 2)
    return me, core, (me, me + 1 - 2 * core, me + 2 - 4 * chip, 3 - me)


def meet(others):
    barrier = pltpu.get_barrier_semaphore()
    for k in range(1, TP):
        pl.semaphore_signal(barrier, inc=1, device_id={'tp': others[k]}, device_id_type=pl.DeviceIdType.MESH)
    pl.semaphore_wait(barrier, TP - 1)


def push(src, dst, send, recv, peer):
    return pltpu.make_async_remote_copy(src_ref=src, dst_ref=dst, send_sem=send, recv_sem=recv, device_id={'tp': peer}, device_id_type=pl.DeviceIdType.MESH)


def image_rows(owner, group):
    return pl.ds(owner * IMAGES + group * GROUP, GROUP)


def group_sends(src, buf, send, recv, others, group):
    return [push(src.at[image_rows(others[k], group)], buf.at[k, pl.ds(group * GROUP, GROUP)], send.at[k - 1, group], recv.at[k - 1, group], others[k]) for k in (2, 3, 1)]


def slot_rows(buf, group):
    base = group * GROUP
    return jnp.concatenate([buf[k, base + g] for g in range(GROUP) for k in range(TP)], axis=0)


def attn_fwd_kernel(patches, wq_own, wop_own, bias_own, w1_own, w2_own, wp, vec, e_ref, qkv_ref, o_ref, x1_ref, x_ref, wq_out, wop_out, bias_out, w1_out, w2_out, xbuf, wq, wop, bias, x_send, x_recv, w_send, w_recv, local):
    step = pl.program_id(0)
    me, core, others = peers()
    small = []
    for n, (src, buf) in enumerate(((wq_own, wq), (wop_own, wop))):
        small.append((push(src, buf.at[2], w_send.at[n, 1], w_recv.at[n, 1], others[2]), push(src, buf.at[1], w_send.at[n, 0], w_recv.at[n, 0], others[1]), push(buf.at[2], buf.at[3], w_send.at[n, 2], w_recv.at[n, 2], others[1])))
    large = []
    for n, (src, out) in enumerate(((w1_own, w1_out), (w2_own, w2_out))):
        large.append((push(src, out.at[1], w_send.at[n + 2, 1], w_recv.at[n + 2, 1], others[2]), push(src, out.at[0], w_send.at[n + 2, 0], w_recv.at[n + 2, 0], others[1]), push(out.at[1], out.at[2], w_send.at[n + 2, 2], w_recv.at[n + 2, 2], others[1])))
    biases = [push(bias_own.at[k], bias.at[k], w_send.at[4, k - 1], w_recv.at[4, k - 1], others[k]) for k in range(1, TP)]
    own = [pltpu.make_async_copy(wq_own, wq.at[0], local.at[0]), pltpu.make_async_copy(wop_own, wop.at[0], local.at[1]), pltpu.make_async_copy(bias_own.at[0], bias.at[0], local.at[2]), pltpu.make_async_copy(patches.at[pl.ds(me * IMAGES, IMAGES)], xbuf.at[0], local.at[3])]
    flush = [pltpu.make_async_copy(wq, wq_out, local.at[4]), pltpu.make_async_copy(wop, wop_out, local.at[5]), pltpu.make_async_copy(bias, bias_out, local.at[6])]

    @pl.when(step == 0)
    def _():
        meet(others)
        small[0][0].start()
        small[1][0].start()
        for c in biases:
            c.start()
        small[0][1].start()
        small[1][1].start()
        for g in range(AHEAD):
            for c in group_sends(patches, xbuf, x_send, x_recv, others, g):
                c.start()
        for c in own:
            c.start()
        for n in range(2):
            small[n][0].wait_recv()
            small[n][2].start()
        for n in range(2):
            large[n][1].start()
        for c in own:
            c.wait()
        for n in range(2):
            small[n][1].wait_recv()
            small[n][2].wait_recv()
        for c in biases:
            c.wait_recv()
        for c in flush:
            c.start()

    @pl.when(step + AHEAD < STEPS)
    def _():
        for c in group_sends(patches, xbuf, x_send, x_recv, others, step + AHEAD):
            c.start()

    @pl.when(step == STEPS - AHEAD)
    def _():
        large[0][0].start()
        large[1][0].start()

    for c in group_sends(patches, xbuf, x_send, x_recv, others, step):
        c.wait_recv()
    x = slot_rows(xbuf, step)
    posb = jnp.concatenate([wop[k, 192:192 + PART] for k in range(TP)], axis=0).astype(WIDE) + vec[0:1]
    emb = dot_nn(x, wp[...]) + jnp.concatenate([posb] * GROUP, axis=0)
    e_h = emb.astype(HALF)
    for g in range(GROUP):
        x_ref[g] = x[TOK * g:TOK * g + TOK]
        e_ref[g] = e_h[TOK * g:TOK * g + TOK]
    e_f = e_h.astype(WIDE)
    xhat, _ = normalize(e_f)
    h1 = (xhat * vec[1:2] + vec[2:3]).astype(HALF)
    bqkv = bias[0].astype(WIDE) + bias[1].astype(WIDE) + bias[2].astype(WIDE) + bias[3].astype(WIDE)
    for s in range(3):
        part = (dot_nt(h1, jnp.concatenate([wq[k, s] for k in range(TP)], axis=0)) + bqkv[s:s + 1]).astype(HALF)
        for g in range(GROUP):
            qkv_ref[g, :, DIM * s:DIM * s + DIM] = part[TOK * g:TOK * g + TOK]
    for g in range(GROUP):
        for pr in range(PAIRS):
            q = qkv_ref[g, :, 128 * pr:128 * pr + 128]
            k = qkv_ref[g, :, DIM + 128 * pr:DIM + 128 * pr + 128]
            v = qkv_ref[g, :, 2 * DIM + 128 * pr:2 * DIM + 128 * pr + 128]
            probs = []
            for j in range(2):
                s = dot_nt(mask_half(q, j), k)
                m = jnp.max(s, axis=-1, keepdims=True)
                e = jnp.exp2((s - m) * EXP_SCALE)
                l = jnp.sum(e, axis=-1, keepdims=True)
                probs.append((e * (1.0 / l)).astype(HALF))
            pv = dot_nn(jnp.concatenate(probs, axis=1), jnp.concatenate([mask_half(v, 0), mask_half(v, 1)], axis=0))
            o_ref[g, :, 128 * pr:128 * pr + 128] = pv.astype(HALF)
    o = jnp.concatenate([o_ref[g] for g in range(GROUP)], axis=0)
    e_f = jnp.concatenate([e_ref[g] for g in range(GROUP)], axis=0).astype(WIDE)
    x1 = (e_f + (dot_nn(o, jnp.concatenate([wop[k, 0:192] for k in range(TP)], axis=0)) + vec[3:4])).astype(HALF)
    for g in range(GROUP):
        x1_ref[g] = x1[TOK * g:TOK * g + TOK]

    @pl.when(step == STEPS - 1)
    def _():
        for n in range(2):
            large[n][0].wait_recv()
            large[n][2].start()
        for n in range(2):
            large[n][1].wait_recv()
            large[n][2].wait_recv()
            for c in small[n] + large[n]:
                c.wait_send()
        for c in biases:
            c.wait_send()
        for c in flush:
            c.wait()
        for g in range(STEPS):
            for c in group_sends(patches, xbuf, x_send, x_recv, others, g):
                c.wait_send()


def fixed(shape):
    return pl.BlockSpec(shape, lambda i: (0,) * len(shape), pipeline_mode=pl.Buffered(1))


def image_spec(width):
    return pl.BlockSpec((GROUP, TOK, width), lambda i: (i, 0, 0))


def any_spec():
    return pl.BlockSpec(memory_space=pl.ANY)


def params(cid):
    return pltpu.CompilerParams(dimension_semantics=('arbitrary',), vmem_limit_bytes=67043328, collective_id=cid, has_side_effects=True)


def image_shape(width):
    return jax.ShapeDtypeStruct((IMAGES, TOK, width), HALF)


def half_shape(*shape):
    return jax.ShapeDtypeStruct(shape, HALF)


def wide_shape(*shape):
    return jax.ShapeDtypeStruct(shape, WIDE)


def attn_fwd(patches, wq, wop, bias, w1, w2, wp, vec):
    dma = pltpu.SemaphoreType.DMA
    return pl.pallas_call(
        attn_fwd_kernel,
        grid=(STEPS,),
        in_specs=[any_spec()] * 6 + [fixed((DIM, DIM)), fixed((8, DIM))],
        out_specs=[image_spec(DIM), image_spec(3 * DIM), image_spec(DIM), image_spec(DIM), image_spec(DIM)] + [any_spec()] * 5,
        out_shape=[image_shape(DIM), image_shape(3 * DIM), image_shape(DIM), image_shape(DIM), image_shape(DIM), half_shape(TP, 3, 192, DIM), half_shape(TP, 256, DIM), half_shape(TP, 16, DIM), half_shape(3, DIM, DIM), half_shape(3, DIM, DIM)],
        scratch_shapes=[pltpu.VMEM((TP, IMAGES, PART, DIM), HALF), pltpu.VMEM((TP, 3, 192, DIM), HALF), pltpu.VMEM((TP, 256, DIM), HALF), pltpu.VMEM((TP, 16, DIM), HALF), dma((3, STEPS)), dma((3, STEPS)), dma((5, 3)), dma((5, 3)), dma((7,))],
        compiler_params=params(0),
        cost_estimate=pl.CostEstimate(flops=60_000_000_000, bytes_accessed=50_000_000, transcendentals=12_000_000),
        name='attn_fwd',
    )(patches, wq, wop, bias, w1, w2, wp, vec)


def mlp_kernel(d_out, x1_ref, o_ref, w1_own, w1_rest, w2_own, w2_rest, wop, bias, vec, x2_out, dx1_ref, do_ref, keep_out, recv_out, dvec_ref, db1_ref, dbuf, ybuf, dw1, dw2, dwo, d_send, d_recv, y_send, y_recv, y_own, g_send, g_recv, local):
    step = pl.program_id(0)
    me, core, others = peers()
    slot = lax.rem(step, 2)

    def y_sends(at, group):
        return [push(ybuf.at[at, k], x2_out.at[image_rows(me, group)], y_send.at[k - 1, at], y_recv.at[k - 1, group], others[k]) for k in (2, 3, 1)]

    def y_keep(at, group):
        return pltpu.make_async_copy(ybuf.at[at, 0], x2_out.at[image_rows(me, group)], y_own.at[at])

    def y_wait(at, group):
        for c in y_sends(at, group):
            c.wait_send()
        y_keep(at, group).wait()

    own = pltpu.make_async_copy(d_out.at[pl.ds(me * IMAGES, IMAGES)], dbuf.at[0], local.at[6])
    grads = []
    for n in range(2):
        grads.append(push(dw1.at[2 * n + 1], recv_out.at[n, 0:DIM], g_send.at[n, 0], g_recv.at[n, 0], others[1]))
        grads.append(push(dw2.at[2 * n + 1], recv_out.at[n, DIM:2 * DIM], g_send.at[n, 1], g_recv.at[n, 1], others[1]))
        grads.append(push(dwo.at[192 * (2 * n + 1):192 * (2 * n + 2)], recv_out.at[n, 2 * DIM:PACK], g_send.at[n, 2], g_recv.at[n, 2], others[1]))
    keeps = []
    for n in range(2):
        keeps.append(pltpu.make_async_copy(dw1.at[2 * n], keep_out.at[n, 0:DIM], local.at[3 * n]))
        keeps.append(pltpu.make_async_copy(dw2.at[2 * n], keep_out.at[n, DIM:2 * DIM], local.at[3 * n + 1]))
        keeps.append(pltpu.make_async_copy(dwo.at[192 * (2 * n):192 * (2 * n + 1)], keep_out.at[n, 2 * DIM:PACK], local.at[3 * n + 2]))

    @pl.when(step == 0)
    def _():
        meet(others)
        for g in range(AHEAD):
            for c in group_sends(d_out, dbuf, d_send, d_recv, others, g):
                c.start()
        own.start()
        dw1[...] = jnp.zeros_like(dw1)
        dw2[...] = jnp.zeros_like(dw2)
        dwo[...] = jnp.zeros_like(dwo)
        dvec_ref[...] = jnp.zeros_like(dvec_ref)
        db1_ref[...] = jnp.zeros_like(db1_ref)
        own.wait()

    @pl.when(step + AHEAD < STEPS)
    def _():
        for c in group_sends(d_out, dbuf, d_send, d_recv, others, step + AHEAD):
            c.start()

    x1 = jnp.concatenate([x1_ref[g] for g in range(GROUP)], axis=0)
    xhat, inv = normalize(x1.astype(WIDE))
    h2 = (xhat * vec[0:1] + vec[1:2]).astype(HALF)
    for c in group_sends(d_out, dbuf, d_send, d_recv, others, step):
        c.wait_recv()
    dout = slot_rows(dbuf, step)
    y = None
    dh2 = None
    for f in range(TP):
        w1 = w1_own[...] if f == 0 else w1_rest[f - 1]
        w2 = w2_own[...] if f == 0 else w2_rest[f - 1]
        pre = dot_nn(h2, w1) + bias[f, 3:4].astype(WIDE)
        sq = pre * pre
        t = jnp.tanh(pre * (GELU_C + (GELU_C * GELU_A) * sq))
        half_pre = 0.5 * pre
        hid = (half_pre + half_pre * t).astype(HALF)
        slope = (0.5 + 0.5 * t) + (half_pre * (1.0 - t * t)) * (GELU_C + (3.0 * GELU_C * GELU_A) * sq)
        dhid = dot_nt(dout, w2).astype(HALF).astype(WIDE)
        dpre = dhid * slope
        db1_ref[f:f + 1] += col_sum(dpre)
        dpre_h = dpre.astype(HALF)
        part_y = dot_nn(hid, w2)
        part_h = dot_nt(dpre_h, w1)
        y = part_y if y is None else y + part_y
        dh2 = part_h if dh2 is None else dh2 + part_h
        dw1[f] += dot_tn(h2, dpre_h)
        dw2[f] += dot_tn(dout, hid)
    x2 = (x1.astype(WIDE) + (y + vec[2:3])).astype(HALF)

    @pl.when(step >= 2)
    def _():
        y_wait(slot, step - 2)

    for g in range(GROUP):
        for k in range(TP):
            ybuf[slot, k, g] = x2[TOK * g + PART * k:TOK * g + PART * k + PART]
    dh2 = dh2.astype(HALF).astype(WIDE)
    xhat, inv = normalize(x1.astype(WIDE))
    dout_f = dout.astype(WIDE)
    dx1 = (dout_f + norm_back(dh2, xhat, inv, vec[0:1])).astype(HALF)
    dvec_ref[0:1] += col_sum(dh2 * xhat)
    dvec_ref[1:2] += col_sum(dh2)
    dvec_ref[2:3] += col_sum(dout_f)
    dvec_ref[3:4] += col_sum(dx1.astype(WIDE))
    d_o = dot_nt(dx1, jnp.concatenate([wop[k, 0:192] for k in range(TP)], axis=0)).astype(HALF)
    for g in range(GROUP):
        dx1_ref[g] = dx1[TOK * g:TOK * g + TOK]
        do_ref[g] = d_o[TOK * g:TOK * g + TOK]
    o = jnp.concatenate([o_ref[g] for g in range(GROUP)], axis=0)
    dwo[...] += dot_tn(o, dx1)

    for c in y_sends(slot, step):
        c.start()
    y_keep(slot, step).start()

    @pl.when(step == STEPS - 1)
    def _():
        for c in grads + keeps:
            c.start()
        for c in keeps:
            c.wait()
        for c in grads:
            c.wait()
        for g in range(STEPS):
            for c in group_sends(d_out, dbuf, d_send, d_recv, others, g):
                c.wait_send()
            for c in y_sends(g % 2, g):
                c.wait_recv()
        for g in (STEPS - 2, STEPS - 1):
            y_wait(g % 2, g)


def mlp(d_out, x1, o, w1, w1_rest, w2, w2_rest, wop, bias, vec):
    dma = pltpu.SemaphoreType.DMA
    vec_spec = pl.BlockSpec((8, DIM), lambda i: (0, 0))
    return pl.pallas_call(
        mlp_kernel,
        grid=(STEPS,),
        in_specs=[any_spec(), image_spec(DIM), image_spec(DIM), fixed((DIM, DIM)), fixed((3, DIM, DIM)), fixed((DIM, DIM)), fixed((3, DIM, DIM)), fixed((TP, 256, DIM)), fixed((TP, 16, DIM)), fixed((8, DIM))],
        out_specs=[any_spec(), image_spec(DIM), image_spec(DIM), any_spec(), any_spec(), vec_spec, vec_spec],
        out_shape=[half_shape(TP * IMAGES, PART, DIM), image_shape(DIM), image_shape(DIM), wide_shape(2, PACK, DIM), wide_shape(2, PACK, DIM), wide_shape(8, DIM), wide_shape(8, DIM)],
        scratch_shapes=[pltpu.VMEM((TP, IMAGES, PART, DIM), HALF), pltpu.VMEM((2, TP, GROUP, PART, DIM), HALF), pltpu.VMEM((TP, DIM, DIM), WIDE), pltpu.VMEM((TP, DIM, DIM), WIDE), pltpu.VMEM((DIM, DIM), WIDE), dma((3, STEPS)), dma((3, STEPS)), dma((3, 2)), dma((3, STEPS)), dma((2,)), dma((2, 3)), dma((2, 3)), dma((7,))],
        compiler_params=params(1),
        cost_estimate=pl.CostEstimate(flops=130_000_000_000, bytes_accessed=80_000_000, transcendentals=12_000_000),
        name='mlp',
    )(d_out, x1, o, w1, w1_rest, w2, w2_rest, wop, bias, vec)


def attn_bwd_kernel(pair, e_ref, qkv_ref, do_ref, dx1_ref, x_ref, wq, vec, dvec2_ref, db1_ref, cross_out, dqkv_out, dwp_out, dpos_out, tiny_out, dqkv, dwq, dwp, dpos, tiny, near_q, near_p, near_pos, far_q, far_p, far_pos, half_q, half_p, half_pos, p_send, p_recv, t_send, t_recv, n_send, n_recv, f_send, f_recv, h_send, h_recv, local):
    step = pl.program_id(0)
    me, core, others = peers()
    cuts = (0, DIM, 2 * DIM, PACK)
    pairs = [push(pair.at[cuts[n]:cuts[n + 1]], cross_out.at[cuts[n]:cuts[n + 1]], p_send.at[n], p_recv.at[n], others[2]) for n in range(3)]

    @pl.when(step == 0)
    def _():
        meet(others)
        for c in pairs:
            c.start()
        dwq[...] = jnp.zeros_like(dwq)
        dwp[...] = jnp.zeros_like(dwp)
        dpos[...] = jnp.zeros_like(dpos)
        tiny[...] = jnp.zeros_like(tiny)

    for g in range(GROUP):
        rows = slice(TOK * g, TOK * g + TOK)
        for pr in range(PAIRS):
            cols = slice(128 * pr, 128 * pr + 128)
            q = qkv_ref[g, :, 128 * pr:128 * pr + 128]
            k = qkv_ref[g, :, DIM + 128 * pr:DIM + 128 * pr + 128]
            v = qkv_ref[g, :, 2 * DIM + 128 * pr:2 * DIM + 128 * pr + 128]
            d_o = do_ref[g, :, 128 * pr:128 * pr + 128]
            probs = []
            dscores = []
            for j in range(2):
                s = dot_nt(k, mask_half(q, j))
                m = jnp.max(s, axis=0, keepdims=True)
                e = jnp.exp2((s - m) * EXP_SCALE)
                l = jnp.sum(e, axis=0, keepdims=True)
                p = e * (1.0 / l)
                dp = dot_nt(v, mask_half(d_o, j)).astype(HALF).astype(WIDE)
                delta = jnp.sum(dp * p, axis=0, keepdims=True)
                ds = (p * ((dp - delta) * 0.125)).astype(HALF)
                probs.append(p.astype(HALF))
                dscores.append(ds)
            dv = dot_nn(jnp.concatenate(probs, axis=1), jnp.concatenate([mask_half(d_o, 0), mask_half(d_o, 1)], axis=0))
            dk = dot_nn(jnp.concatenate(dscores, axis=1), jnp.concatenate([mask_half(q, 0), mask_half(q, 1)], axis=0))
            dq = dot_tn(jnp.concatenate(dscores, axis=0), jnp.concatenate([mask_half(k, 0), mask_half(k, 1)], axis=0))
            dqkv[rows, 128 * pr:128 * pr + 128] = dq.astype(HALF)
            dqkv[rows, DIM + 128 * pr:DIM + 128 * pr + 128] = dk.astype(HALF)
            dqkv[rows, 2 * DIM + 128 * pr:2 * DIM + 128 * pr + 128] = dv.astype(HALF)
    e_f = jnp.concatenate([e_ref[g] for g in range(GROUP)], axis=0).astype(WIDE)
    xhat, inv = normalize(e_f)
    h1 = (xhat * vec[1:2] + vec[2:3]).astype(HALF)
    dh1 = None
    for s in range(3):
        part = dqkv[:, DIM * s:DIM * s + DIM]
        tiny[s:s + 1] += col_sum(part.astype(WIDE))
        grad = dot_tn(part, h1)
        for k in range(TP):
            dwq[k, s] += grad[192 * k:192 * k + 192]
        term = dot_nn(part, jnp.concatenate([wq[k, s] for k in range(TP)], axis=0))
        dh1 = term if dh1 is None else dh1 + term
    dh1 = dh1.astype(HALF).astype(WIDE)
    dx1 = jnp.concatenate([dx1_ref[g] for g in range(GROUP)], axis=0).astype(WIDE)
    de = (dx1 + norm_back(dh1, xhat, inv, vec[1:2])).astype(HALF)
    de_f = de.astype(WIDE)
    tiny[16:17] += col_sum(dh1 * xhat)
    tiny[17:18] += col_sum(dh1)
    acc = de_f[0:TOK]
    for g in range(1, GROUP):
        acc = acc + de_f[TOK * g:TOK * g + TOK]
    dpos[...] += acc
    x = jnp.concatenate([x_ref[g] for g in range(GROUP)], axis=0)
    dwp[...] += dot_tn(x, de)

    @pl.when(step == STEPS - 1)
    def _():
        tiny[8:16] = db1_ref[...]
        tiny[18:19] = col_sum(dpos[...])
        tiny[24:32] = dvec2_ref[...]
        other_half = pl.ds(384 * (1 - core), 384)
        my_half = pl.ds(384 * core, 384)
        near = [push(dwq.at[3], near_q.at[1], n_send.at[0], n_recv.at[0], others[1]), push(dwq.at[1], near_q.at[0], n_send.at[1], n_recv.at[1], others[1]), push(dpos.at[3 * PART:4 * PART], near_pos.at[1], n_send.at[2], n_recv.at[2], others[1]), push(dpos.at[PART:2 * PART], near_pos.at[0], n_send.at[3], n_recv.at[3], others[1]), push(dwp.at[other_half], near_p, n_send.at[4], n_recv.at[4], others[1])]
        tinies = [push(tiny, tiny_out.at[k - 1], t_send.at[k - 1], t_recv.at[k - 1], others[k]) for k in range(1, TP)]
        far = [push(dwq.at[2], far_q, f_send.at[0], f_recv.at[0], others[2]), push(dwp.at[my_half], far_p, f_send.at[1], f_recv.at[1], others[2]), push(dpos.at[2 * PART:3 * PART], far_pos, f_send.at[2], f_recv.at[2], others[2])]
        for c in near + tinies:
            c.start()
        near[0].wait_recv()
        for s in range(3):
            dwq[2, s] += near_q[1, s]
        far[0].start()
        near[4].wait_recv()
        dwp[my_half] += near_p[...]
        far[1].start()
        near[2].wait_recv()
        dpos[2 * PART:3 * PART] += near_pos[1]
        far[2].start()
        near[1].wait_recv()
        near[3].wait_recv()
        for c in pairs:
            c.wait()
        far[0].wait_recv()
        for s in range(3):
            half_q[s] = ((dwq[0, s] + near_q[0, s]) + far_q[s]).astype(HALF)
        q_copy = pltpu.make_async_copy(half_q, dqkv_out, local.at[0])
        q_copy.start()
        far[1].wait()
        half_p[...] = (dwp[my_half] + far_p[...]).astype(HALF)
        swap = push(half_p, dwp_out.at[my_half], h_send, h_recv, others[1])
        swap.start()
        p_copy = pltpu.make_async_copy(half_p, dwp_out.at[my_half], local.at[1])
        p_copy.start()
        far[2].wait_recv()
        half_pos[...] = ((dpos[0:PART] + near_pos[0]) + far_pos[...]).astype(HALF)
        pos_copy = pltpu.make_async_copy(half_pos, dpos_out, local.at[2])
        pos_copy.start()
        for c in near:
            c.wait_send()
        for c in tinies:
            c.wait()
        far[0].wait_send()
        far[2].wait_send()
        tiny_copy = pltpu.make_async_copy(tiny, tiny_out.at[3], local.at[3])
        tiny_copy.start()
        q_copy.wait()
        p_copy.wait()
        pos_copy.wait()
        tiny_copy.wait()
        swap.wait()


def attn_bwd(pair, e, qkv, d_o, dx1, x, wq, vec, dvec2, db1):
    dma = pltpu.SemaphoreType.DMA
    return pl.pallas_call(
        attn_bwd_kernel,
        grid=(STEPS,),
        in_specs=[any_spec(), image_spec(DIM), image_spec(3 * DIM), image_spec(DIM), image_spec(DIM), image_spec(DIM), fixed((TP, 3, 192, DIM)), fixed((8, DIM)), fixed((8, DIM)), fixed((8, DIM))],
        out_specs=[any_spec()] * 5,
        out_shape=[wide_shape(PACK, DIM), half_shape(3, 192, DIM), half_shape(DIM, DIM), half_shape(PART, DIM), wide_shape(TP, 32, DIM)],
        scratch_shapes=[pltpu.VMEM((ROWS, 3 * DIM), HALF), pltpu.VMEM((TP, 3, 192, DIM), WIDE), pltpu.VMEM((DIM, DIM), WIDE), pltpu.VMEM((TOK, DIM), WIDE), pltpu.VMEM((32, DIM), WIDE), pltpu.VMEM((2, 3, 192, DIM), WIDE), pltpu.VMEM((384, DIM), WIDE), pltpu.VMEM((2, PART, DIM), WIDE), pltpu.VMEM((3, 192, DIM), WIDE), pltpu.VMEM((384, DIM), WIDE), pltpu.VMEM((PART, DIM), WIDE), pltpu.VMEM((3, 192, DIM), HALF), pltpu.VMEM((384, DIM), HALF), pltpu.VMEM((PART, DIM), HALF), dma((3,)), dma((3,)), dma((3,)), dma((3,)), dma((5,)), dma((5,)), dma((3,)), dma((3,)), dma, dma, dma((4,))],
        compiler_params=params(2),
        cost_estimate=pl.CostEstimate(flops=100_000_000_000, bytes_accessed=80_000_000, transcendentals=12_000_000),
        name='attn_bwd',
    )(pair, e, qkv, d_o, dx1, x, wq, vec, dvec2, db1)


def pad_rows(rows):
    rows = [r.astype(WIDE).reshape(-1, DIM) for r in rows]
    n = sum(r.shape[0] for r in rows)
    return jnp.concatenate(rows + [jnp.zeros((8 - n, DIM), WIDE)], axis=0)


def group_step(patches, patch_w, patch_b, pos_emb, ln_scale, ln_bias, qkv_w, qkv_b, out_w, out_b, fc1_w, fc1_b, fc2_w, fc2_b, d_out):
    wq = qkv_w.transpose(0, 2, 3, 1).reshape(3, 192, DIM)
    wop = jnp.concatenate([out_w.reshape(192, DIM), pos_emb], axis=0)
    qb = qkv_b.reshape(3, 192)
    bias = jnp.stack([jnp.concatenate([jnp.pad(qb, ((0, 0), (192 * k, DIM - 192 - 192 * k))), fc1_b.reshape(1, DIM), jnp.zeros((12, DIM), HALF)], axis=0) for k in range(TP)])
    vec1 = pad_rows([patch_b, ln_scale[0], ln_bias[0], out_b])
    vec2 = pad_rows([ln_scale[1], ln_bias[1], fc2_b])
    e, qkv, o, x1, x, wq_all, wop_all, bias_all, w1_rest, w2_rest = attn_fwd(patches, wq, wop, bias, fc1_w, fc2_w, patch_w, vec1)
    x_two, dx1, d_o, keep, near, dvec2, db1 = mlp(d_out, x1, o, fc1_w, w1_rest, fc2_w, w2_rest, wop_all, bias_all, vec2)
    pair = keep[1] + near[1]
    cross, d_qkv, d_patch_w, d_pos, tiny = attn_bwd(pair, e, qkv, d_o, dx1, x, wq_all, vec1, dvec2, db1)
    total = ((keep[0] + near[0]) + cross).astype(HALF)
    d_fc1_w = total[0:DIM]
    d_fc2_w = total[DIM:2 * DIM].T
    d_out_w = total[2 * DIM:].reshape(3, 64, DIM)
    d_qkv_w = d_qkv.reshape(3, 3, 64, DIM).transpose(0, 3, 1, 2)
    vec = ((tiny[3] + tiny[0]) + (tiny[1] + tiny[2])).astype(HALF)
    d_qkv_b = (tiny[3, 0:3, 0:192] + tiny[0, 0:3, 192:384]) + (tiny[1, 0:3, 384:576] + tiny[2, 0:3, 576:768])
    d_fc1_b = (tiny[3, 8] + tiny[0, 9]) + (tiny[1, 10] + tiny[2, 11])
    d_ln_scale = jnp.stack([vec[16], vec[24]])
    d_ln_bias = jnp.stack([vec[17], vec[25]])
    return (x_two, d_patch_w, vec[18], d_pos, d_ln_scale, d_ln_bias, d_qkv_w, d_qkv_b.astype(HALF).reshape(3, 3, 64), d_out_w, vec[27], d_fc1_w, d_fc1_b.astype(HALF), d_fc2_w, vec[26])


def solution(mesh):
    in_specs = (P('dp', 'tp', None), P(), P(), P('tp', None), P(), P(), P(None, None, 'tp', None), P(None, 'tp', None), P('tp', None, None), P(), P(None, 'tp'), P('tp'), P('tp', None), P(), P('dp', 'tp', None))
    out_specs = (P('dp', 'tp', None), P('dp', None), P('dp'), P(('dp', 'tp'), None), P('dp', None), P('dp', None), P('dp', None, 'tp', None), P('dp', 'tp', None), P(('dp', 'tp'), None, None), P('dp'), P('dp', 'tp'), P(('dp', 'tp')), P(('dp', 'tp'), None), P('dp'))
    return jax.shard_map(group_step, mesh=mesh, in_specs=in_specs, out_specs=out_specs, check_vma=False)
```

time: 790 us -> 595 us (0.75)
  waiting for transfers between devices: 330 us -> 0 us
  Pallas kernels: 344 us -> 550 us
  local copies, waits for them, and re-layouts: 55.3 us -> 19.2 us
  starting transfers between devices: 23.8 us -> 0 us
    ppermute x44 -> x0, waiting for transfers between devices: 330 us -> none  [permute_xor(): return lax.ppermute(x, 'tp', [(i, i ^ k) for i in range(TP)])]
    pallas_call x3, Pallas kernels: 344 us -> 550 us  [the longest x1 198 us: mlp(): pl.pallas_call(mlp_kernel, grid=(STEPS,), in_specs=[any_spec(), image_spe...]
    ppermute x44 -> x0, starting transfers between devices: 23.8 us -> none  [permute_xor(): return lax.ppermute(x, 'tp', [(i, i ^ k) for i in range(TP)])]
    squeeze x5 -> x0, local copies, waits for them, and re-layouts: 19.9 us -> none  [the longest x2 10.9 us: exchange(): lax.dynamic_index_in_dim(blocks, me ^ k, 0, keepdims=False)]
    slice x18 -> x2, local copies, waits for them, and re-layouts: 14.5 us -> 1.36 us  [the longest x1 0.73 us: group_step(): d_out_w = total[2 * DIM:].reshape(3, 64, DIM)]
    dynamic_update_slice x4 -> x0, local copies, waits for them, and re-layouts: 9.32 us -> none  [give_back(): out = lax.dynamic_update_index_in_dim(out, block, me ^ k, 0)]
  transfers between devices with their start and end apart: 44 -> 0, of which waited for: 14 -> 0; matrix products, arithmetic and copies ran while one was open for 9% -> 0% of each run, Pallas kernels for 24% -> 0%
where the time goes in v3:
time: 595 us; the launch traced here: 590 us
  Pallas kernels  550 us (92%)
  other arithmetic  19.5 us (3%)
  local copies, waits for them, and re-layouts  19.2 us (3%)
    pallas_call x1, Pallas kernels, mlp(): pl.pallas_call(mlp_kernel, grid=(STEPS,), in_specs=[any_spec(), image_spe...  198 us
    pallas_call x1, Pallas kernels, attn_bwd(): pl.pallas_call(attn_bwd_kernel, grid=(STEPS,), in_specs=[any_spec(), imag...  194 us
    pallas_call x1, Pallas kernels, attn_fwd(): pl.pallas_call(attn_fwd_kernel, grid=(STEPS,), in_specs=[any_spec()] * 6...  158 us

profile of v3, /device:TPU:0, one launch (start us, length us, event | category | flops | bytes accessed | tf_op | source)
XLA Modules:
  0.0 589.5 jit_solution(14285271035770341310)
XLA Ops:
  0.8 0.8 reshape.102
  1.6 0.7 reshape.113
  2.3 0.7 reshape.115
  2.9 0.7 reshape.103
  3.6 0.7 reshape.117
  4.3 0.8 slice_convert_fusion
  5.1 0.6 concatenate.26.vec
  5.7 0.7 maximum_maximum_fusion.vec
  6.5 0.7 pad_maximum_fusion.1.bias_own
  7.2 1.8 pad_maximum_fusion.wop_own
  9.0 158.2 %attn_fwd.1 = (bf16[16,256,768]{2,1,0:T(8,128)(2,1)}, bf16[16,256,2304]{2,1,0:T(8,128)(2,1)}, bf16[16,256,768]{2,1,0:T(8,128)(2,1)}, bf16[16,256,768]{2,1,0:T(8,...) custom-call(bf16[64,64,768]{2,1,0:T(8,128)(2,1)} %patches.1, ...), custom_call_target="tpu_custom_call" | custom-call | flops 60000002048 | bytes 50000000 | tf_op jit(solution)/shard_map/attn_fwd/pallas_call | solution.py:237
  167.1 197.6 %mlp.1 = (bf16[64,64,768]{2,1,0:T(8,128)(2,1)}, bf16[16,256,768]{2,1,0:T(8,128)(2,1)}, bf16[16,256,768]{2,1,0:T(8,128)(2,1)}, f32[2,1728,768]{2,1,0:T(8,128)}, f...) custom-call(bf16[64,64,768]{2,1,0:T(8,128)(2,1)} %d_out.1, ...), custom_call_target="tpu_custom_call" | custom-call | flops 130000003072 | bytes 80000000 | tf_op jit(solution)/shard_map/mlp/pallas_call | solution.py:372
  364.8 7.1 %add_bitcast_fusion.pair = f32[1728,768]{1,0:T(8,128)} fusion(f32[2,1728,768]{2,1,0:T(8,128)} %get-tuple-element.44, f32[2,1728,768]{2,1,0:T(8,128)} %get-tuple-element.43), kind=kLoop, calls=%fused_computation.2 | loop fusion | flops 1327104 | bytes 15925248 | tf_op jit(solution)/shard_map/add | solution.py:539
  371.9 194.0 %attn_bwd.1 = (f32[1728,768]{1,0:T(8,128)}, bf16[3,192,768]{2,1,0:T(8,128)(2,1)}, bf16[768,768]{1,0:T(8,128)(2,1)}, bf16[64,768]{1,0:T(8,128)(2,1)}, f32[4,32,768]{2,1,0:T(8,128)}) custom-call(f32[1728,768]{1,0:T(8,128)} %add_bitcast_fusion.pair, bf16[16,256,768]{2,1,0:T(8,128)(2,1)} %get-tuple-element.45.e_ref, ...), custom_call_target="tpu_custom_call" | custom-call | flops 99999997952 | bytes 80000000 | tf_op jit(solution)/shard_map/attn_bwd/pallas_call | solution.py:511
  565.9 6.5 %fusion = bf16[1728,768]{1,0:T(8,128)(2,1)S(1)} fusion(f32[1728,768]{1,0:T(8,128)} %get-tuple-element.57, f32[2,1728,768]{2,1,0:T(8,128)} %get-tuple-element.44, f32[2,1728,768]{2,1,0:T(8,128)} %get-tuple-element.43), kind=kLoop, calls=%fused_computation.1 | loop fusion | flops 3981312 | bytes 18579456 | tf_op jit(solution)/shard_map/convert_element_type | solution.py:541
  573.1 0.6 slice_bitcast_fusion.2
  574.3 0.7 convert_element_type.53
  575.5 0.7 slice.144
  576.3 1.6 slice_bitcast_fusion
  577.8 2.4 copy.29
  580.2 6.4 %copy.34 = bf16[64,64,768]{2,1,0:T(8,128)(2,1)} copy(bf16[64,64,768]{2,1,0:T(8,128)(2,1)} %get-tuple-element.108) | data formatting | bytes 12582912
  586.6 1.0 copy.35
  587.6 0.6 copy.36
  588.2 0.9 copy.37
  (19 shorter events, 2.1 us)
Async XLA Ops:
  565.9 6.5 %copy-start.2 = (f32[4,32,768]{2,1,0:T(8,128)S(1)}, f32[4,32,768]{2,1,0:T(8,128)}, u32[]{:S(2)}) copy-start(f32[4,32,768]{2,1,0:T(8,128)} %get-tuple-element.54) | copy-start | bytes 1179652
  580.2 6.4 %copy-start = (bf16[768,768]{1,0:T(8,128)(2,1)S(1)}, bf16[768,768]{1,0:T(8,128)(2,1)}, u32[]{:S(2)}) copy-start(bf16[768,768]{1,0:T(8,128)(2,1)} %get-tuple-element.109) | copy-start | bytes 3538948
  580.2 7.4 %copy-start.3 = (bf16[64,768]{1,0:T(8,128)(2,1)S(1)}, bf16[64,768]{1,0:T(8,128)(2,1)}, u32[]{:S(2)}) copy-start(bf16[64,768]{1,0:T(8,128)(2,1)} %get-tuple-element.111) | copy-start | bytes 294916
  580.2 8.0 %copy-start.1 = (bf16[3,192,768]{2,1,0:T(8,128)(2,1)S(1)}, bf16[3,192,768]{2,1,0:T(8,128)(2,1)}, u32[]{:S(2)}) copy-start(bf16[3,192,768]{2,1,0:T(8,128)(2,1)} %get-tuple-element.56) | copy-start | bytes 2654212

commit v4 on v3

v4 whole, which is shorter than its diff:
```python
import functools
import jax
import jax.numpy as jnp
from jax import lax
from jax.experimental import pallas as pl
from jax.experimental.pallas import tpu as pltpu
from jax.sharding import PartitionSpec as P

LN_EPS = 1e-6
TP = 4
WIDE = jnp.float32
HALF = jnp.bfloat16
IMAGES = 16
TOK = 256
PART = 64
DIM = 768
GROUP = 2
ROWS = GROUP * TOK
STEPS = IMAGES // GROUP
PAIRS = 6
EXP_SCALE = 0.125 * 1.4426950408889634
GELU_C = 0.7978845608028654
GELU_A = 0.044715
AHEAD = 3
PACK = 2 * DIM + 192
CHUNKS = 6
CHUNK = PACK // CHUNKS


def dot_nn(a, b):
    return lax.dot_general(a, b, (((1,), (0,)), ((), ())), preferred_element_type=WIDE)


def dot_nt(a, b):
    return lax.dot_general(a, b, (((1,), (1,)), ((), ())), preferred_element_type=WIDE)


def dot_tn(a, b):
    return lax.dot_general(a, b, (((0,), (0,)), ((), ())), preferred_element_type=WIDE)


def normalize(x_f):
    mean = jnp.sum(x_f, axis=-1, keepdims=True) * (1.0 / DIM)
    centered = x_f - mean
    var = jnp.sum(centered * centered, axis=-1, keepdims=True) * (1.0 / DIM)
    inv = lax.rsqrt(var + LN_EPS)
    return centered * inv, inv


def norm_back(d_out_f, xhat, inv, scale):
    d_hat = d_out_f * scale
    m1 = jnp.sum(d_hat, axis=-1, keepdims=True) * (1.0 / DIM)
    m2 = jnp.sum(d_hat * xhat, axis=-1, keepdims=True) * (1.0 / DIM)
    return (d_hat - m1 - xhat * m2) * inv


def lane_half(j):
    lane = lax.broadcasted_iota(jnp.int32, (1, 128), 1)
    return (lane < 64) if j == 0 else (lane >= 64)


def mask_half(x, j):
    return jnp.where(lane_half(j), x, jnp.zeros_like(x))


def col_sum(x):
    return jnp.sum(x, axis=0, keepdims=True)


def row(ref):
    return ref[...].reshape(1, DIM).astype(WIDE)


def peers():
    me = lax.axis_index('tp')
    core = lax.rem(me, 2)
    chip = lax.div(me, 2)
    return me, core, (me, me + 1 - 2 * core, me + 2 - 4 * chip, 3 - me)


def meet(others):
    barrier = pltpu.get_barrier_semaphore()
    for k in range(1, TP):
        pl.semaphore_signal(barrier, inc=1, device_id={'tp': others[k]}, device_id_type=pl.DeviceIdType.MESH)
    pl.semaphore_wait(barrier, TP - 1)


def push(src, dst, send, recv, peer):
    return pltpu.make_async_remote_copy(src_ref=src, dst_ref=dst, send_sem=send, recv_sem=recv, device_id={'tp': peer}, device_id_type=pl.DeviceIdType.MESH)


def image_rows(owner, group):
    return pl.ds(owner * IMAGES + group * GROUP, GROUP)


def group_sends(src, buf, send, recv, others, group):
    return [push(src.at[image_rows(others[k], group)], buf.at[k, pl.ds(group * GROUP, GROUP)], send.at[k - 1, group], recv.at[k - 1, group], others[k]) for k in (2, 3, 1)]


def slot_rows(buf, group):
    base = group * GROUP
    return jnp.concatenate([buf[k, base + g] for g in range(GROUP) for k in range(TP)], axis=0)


def attn_fwd_kernel(patches, wq_own, wo_own, pos_own, w1_own, w2_own, wp, patch_b, qkv_b, fc1_b, out_b, ln_scale, ln_bias, e_ref, qkv_ref, o_ref, x1_ref, x_ref, wq_out, wop_out, bias_out, w1_out, w2_near, xbuf, wq, wop, bias, bias_own, bqkv, x_send, x_recv, w_send, w_recv, local):
    step = pl.program_id(0)
    me, core, others = peers()
    small = []
    for n, (src, cut) in enumerate(((wq_own, None), (wo_own, (0, 192)), (pos_own, (192, 256)))):
        at = [wq.at[k] if cut is None else wop.at[k, cut[0]:cut[1]] for k in range(TP)]
        small.append((push(src, at[2], w_send.at[n, 1], w_recv.at[n, 1], others[2]), push(src, at[1], w_send.at[n, 0], w_recv.at[n, 0], others[1]), push(at[2], at[3], w_send.at[n, 2], w_recv.at[n, 2], others[1])))
    large = (push(w1_own, w1_out.at[1], w_send.at[3, 1], w_recv.at[3, 1], others[2]), push(w1_own, w1_out.at[0], w_send.at[3, 0], w_recv.at[3, 0], others[1]), push(w1_out.at[1], w1_out.at[2], w_send.at[3, 2], w_recv.at[3, 2], others[1]), push(w2_own, w2_near, w_send.at[4, 0], w_recv.at[4, 0], others[1]))
    biases = [push(bias_own, bias.at[k], w_send.at[5, k - 1], w_recv.at[5, k - 1], others[k]) for k in range(1, TP)]
    own = [pltpu.make_async_copy(wq_own, wq.at[0], local.at[0]), pltpu.make_async_copy(wo_own, wop.at[0, 0:192], local.at[1]), pltpu.make_async_copy(pos_own, wop.at[0, 192:256], local.at[2]), pltpu.make_async_copy(patches.at[pl.ds(me * IMAGES, IMAGES)], xbuf.at[0], local.at[3])]
    flush = [pltpu.make_async_copy(wq, wq_out, local.at[4]), pltpu.make_async_copy(wop, wop_out, local.at[5]), pltpu.make_async_copy(bias, bias_out, local.at[6])]

    @pl.when(step == 0)
    def _():
        bias_own[...] = jnp.zeros_like(bias_own)
        for s in range(3):
            for h in range(3):
                bias_own[s:s + 1, 64 * h:64 * h + 64] = qkv_b[s, h:h + 1]
        bias_own[3:4] = fc1_b[...].reshape(1, DIM)
        bias[0] = bias_own[...]
        meet(others)
        for n in range(3):
            small[n][0].start()
        for c in biases:
            c.start()
        for n in range(3):
            small[n][1].start()
        for g in range(AHEAD):
            for c in group_sends(patches, xbuf, x_send, x_recv, others, g):
                c.start()
        for c in own:
            c.start()
        for n in range(3):
            small[n][0].wait_recv()
            small[n][2].start()
        large[1].start()
        large[3].start()
        for c in own:
            c.wait()
        for n in range(3):
            small[n][1].wait_recv()
            small[n][2].wait_recv()
        for c in biases:
            c.wait_recv()
        for s in range(3):
            for k in range(TP):
                bqkv[s:s + 1, 192 * k:192 * k + 192] = bias[k, s:s + 1, 0:192].astype(WIDE)
        for c in flush:
            c.start()

    @pl.when(step + AHEAD < STEPS)
    def _():
        for c in group_sends(patches, xbuf, x_send, x_recv, others, step + AHEAD):
            c.start()

    @pl.when(step == STEPS - AHEAD)
    def _():
        large[0].start()

    for c in group_sends(patches, xbuf, x_send, x_recv, others, step):
        c.wait_recv()
    x = slot_rows(xbuf, step)
    posb = jnp.concatenate([wop[k, 192:192 + PART] for k in range(TP)], axis=0).astype(WIDE) + row(patch_b)
    emb = dot_nn(x, wp[...]) + jnp.concatenate([posb] * GROUP, axis=0)
    e_h = emb.astype(HALF)
    for g in range(GROUP):
        x_ref[g] = x[TOK * g:TOK * g + TOK]
        e_ref[g] = e_h[TOK * g:TOK * g + TOK]
    e_f = e_h.astype(WIDE)
    xhat, _ = normalize(e_f)
    h1 = (xhat * ln_scale[0:1].astype(WIDE) + ln_bias[0:1].astype(WIDE)).astype(HALF)
    for s in range(3):
        part = (dot_nt(h1, jnp.concatenate([wq[k, s] for k in range(TP)], axis=0)) + bqkv[s:s + 1]).astype(HALF)
        for g in range(GROUP):
            qkv_ref[g, :, DIM * s:DIM * s + DIM] = part[TOK * g:TOK * g + TOK]
    for g in range(GROUP):
        for pr in range(PAIRS):
            q = qkv_ref[g, :, 128 * pr:128 * pr + 128]
            k = qkv_ref[g, :, DIM + 128 * pr:DIM + 128 * pr + 128]
            v = qkv_ref[g, :, 2 * DIM + 128 * pr:2 * DIM + 128 * pr + 128]
            probs = []
            for j in range(2):
                s = dot_nt(mask_half(q, j), k)
                m = jnp.max(s, axis=-1, keepdims=True)
                e = jnp.exp2((s - m) * EXP_SCALE)
                l = jnp.sum(e, axis=-1, keepdims=True)
                probs.append((e * (1.0 / l)).astype(HALF))
            pv = dot_nn(jnp.concatenate(probs, axis=1), jnp.concatenate([mask_half(v, 0), mask_half(v, 1)], axis=0))
            o_ref[g, :, 128 * pr:128 * pr + 128] = pv.astype(HALF)
    o = jnp.concatenate([o_ref[g] for g in range(GROUP)], axis=0)
    e_f = jnp.concatenate([e_ref[g] for g in range(GROUP)], axis=0).astype(WIDE)
    x1 = (e_f + (dot_nn(o, jnp.concatenate([wop[k, 0:192] for k in range(TP)], axis=0)) + row(out_b))).astype(HALF)
    for g in range(GROUP):
        x1_ref[g] = x1[TOK * g:TOK * g + TOK]

    @pl.when(step == STEPS - 1)
    def _():
        large[0].wait_recv()
        large[2].start()
        for c in large[1:]:
            c.wait_recv()
        for c in small[0] + small[1] + small[2] + large:
            c.wait_send()
        for c in biases:
            c.wait_send()
        for c in flush:
            c.wait()
        for g in range(STEPS):
            for c in group_sends(patches, xbuf, x_send, x_recv, others, g):
                c.wait_send()


def fixed(shape):
    return pl.BlockSpec(shape, lambda i: (0,) * len(shape), pipeline_mode=pl.Buffered(1))


def image_spec(width):
    return pl.BlockSpec((GROUP, TOK, width), lambda i: (i, 0, 0))


def any_spec():
    return pl.BlockSpec(memory_space=pl.ANY)


def params(cid):
    return pltpu.CompilerParams(dimension_semantics=('arbitrary',), vmem_limit_bytes=67043328, collective_id=cid, has_side_effects=True)


def image_shape(width):
    return jax.ShapeDtypeStruct((IMAGES, TOK, width), HALF)


def half_shape(*shape):
    return jax.ShapeDtypeStruct(shape, HALF)


def wide_shape(*shape):
    return jax.ShapeDtypeStruct(shape, WIDE)


def vec_spec(*shape):
    return pl.BlockSpec(shape, lambda i: (0,) * len(shape))


def attn_fwd(patches, wq, wo, pos, w1, w2, wp, patch_b, qkv_b, fc1_b, out_b, ln_scale, ln_bias):
    dma = pltpu.SemaphoreType.DMA
    return pl.pallas_call(
        attn_fwd_kernel,
        grid=(STEPS,),
        in_specs=[any_spec()] * 6 + [fixed((DIM, DIM)), vec_spec(DIM), vec_spec(3, 3, 64), vec_spec(DIM), vec_spec(DIM), vec_spec(2, DIM), vec_spec(2, DIM)],
        out_specs=[image_spec(DIM), image_spec(3 * DIM), image_spec(DIM), image_spec(DIM), image_spec(DIM)] + [any_spec()] * 5,
        out_shape=[image_shape(DIM), image_shape(3 * DIM), image_shape(DIM), image_shape(DIM), image_shape(DIM), half_shape(TP, 3, 192, DIM), half_shape(TP, 256, DIM), half_shape(TP, 16, DIM), half_shape(3, DIM, DIM), half_shape(DIM, DIM)],
        scratch_shapes=[pltpu.VMEM((TP, IMAGES, PART, DIM), HALF), pltpu.VMEM((TP, 3, 192, DIM), HALF), pltpu.VMEM((TP, 256, DIM), HALF), pltpu.VMEM((TP, 16, DIM), HALF), pltpu.VMEM((16, DIM), HALF), pltpu.VMEM((8, DIM), WIDE), dma((3, STEPS)), dma((3, STEPS)), dma((6, 3)), dma((6, 3)), dma((7,))],
        compiler_params=params(0),
        cost_estimate=pl.CostEstimate(flops=60_000_000_000, bytes_accessed=50_000_000, transcendentals=12_000_000),
        name='attn_fwd',
    )(patches, wq, wo, pos, w1, w2, wp, patch_b, qkv_b, fc1_b, out_b, ln_scale, ln_bias)


def mlp_slot(n, f, h2, dout, w1, w2, b1, y, dh2, dw1, dw2, db1_ref):
    pre = dot_nn(h2, w1) + b1
    sq = pre * pre
    t = jnp.tanh(pre * (GELU_C + (GELU_C * GELU_A) * sq))
    half_pre = 0.5 * pre
    hid = (half_pre + half_pre * t).astype(HALF)
    slope = (0.5 + 0.5 * t) + (half_pre * (1.0 - t * t)) * (GELU_C + (3.0 * GELU_C * GELU_A) * sq)
    dhid = dot_nt(dout, w2).astype(HALF).astype(WIDE)
    dpre = dhid * slope
    db1_ref[f:f + 1] += col_sum(dpre)
    dpre_h = dpre.astype(HALF)
    part_y = dot_nn(hid, w2)
    part_h = dot_nt(dpre_h, w1)
    y = part_y if y is None else y + part_y
    dh2 = part_h if dh2 is None else dh2 + part_h
    dw1[n] += dot_tn(h2, dpre_h)
    dw2[n] += dot_tn(dout, hid)
    return y, dh2


def mlp_near_kernel(d_out, w2_push, x1_ref, w1_own, w1_near, w2_own, w2_near, bias, ln_scale, ln_bias, dout_ref, y_ref, dh_ref, w2_far, keep_out, give_out, dvec_ref, db1_ref, dbuf, dw1, dw2, d_send, d_recv, w_send, w_recv, local):
    step = pl.program_id(0)
    me, core, others = peers()
    own = pltpu.make_async_copy(d_out.at[pl.ds(me * IMAGES, IMAGES)], dbuf.at[0], local.at[4])
    far = push(w2_push, w2_far.at[0], w_send.at[0], w_recv.at[0], others[2])
    relay = push(w2_far.at[0], w2_far.at[1], w_send.at[1], w_recv.at[1], others[1])

    @pl.when(step == 0)
    def _():
        meet(others)
        for g in range(AHEAD):
            for c in group_sends(d_out, dbuf, d_send, d_recv, others, g):
                c.start()
        own.start()
        dw1[...] = jnp.zeros_like(dw1)
        dw2[...] = jnp.zeros_like(dw2)
        dvec_ref[...] = jnp.zeros_like(dvec_ref)
        db1_ref[...] = jnp.zeros_like(db1_ref)
        own.wait()

    @pl.when(step + AHEAD < STEPS)
    def _():
        for c in group_sends(d_out, dbuf, d_send, d_recv, others, step + AHEAD):
            c.start()

    @pl.when(step == STEPS - AHEAD)
    def _():
        far.start()

    x1 = jnp.concatenate([x1_ref[g] for g in range(GROUP)], axis=0)
    xhat, inv = normalize(x1.astype(WIDE))
    h2 = (xhat * ln_scale[1:2].astype(WIDE) + ln_bias[1:2].astype(WIDE)).astype(HALF)
    for c in group_sends(d_out, dbuf, d_send, d_recv, others, step):
        c.wait_recv()
    dout = slot_rows(dbuf, step)
    dvec_ref[2:3] += col_sum(dout.astype(WIDE))
    y = None
    dh2 = None
    for f, (w1, w2) in enumerate(((w1_own, w2_own), (w1_near, w2_near))):
        y, dh2 = mlp_slot(f, f, h2, dout, w1[...], w2[...], bias[f, 3:4].astype(WIDE), y, dh2, dw1, dw2, db1_ref)
    for g in range(GROUP):
        rows = slice(TOK * g, TOK * g + TOK)
        dout_ref[g] = dout[rows]
        y_ref[g] = y[rows]
        dh_ref[g] = dh2[rows]

    @pl.when(step == STEPS - 1)
    def _():
        copies = []
        for n, out in enumerate((keep_out, give_out)):
            copies.append(pltpu.make_async_copy(dw1.at[n], out.at[0:DIM], local.at[2 * n]))
            copies.append(pltpu.make_async_copy(dw2.at[n], out.at[DIM:2 * DIM], local.at[2 * n + 1]))
        for c in copies:
            c.start()
        far.wait_recv()
        relay.start()
        for g in range(STEPS):
            for c in group_sends(d_out, dbuf, d_send, d_recv, others, g):
                c.wait_send()
        for c in copies:
            c.wait()
        far.wait_send()
        relay.wait()


def mlp_near(d_out, x1, w1, w1_near, w2, w2_near, bias, ln_scale, ln_bias):
    dma = pltpu.SemaphoreType.DMA
    wide_image = jax.ShapeDtypeStruct((IMAGES, TOK, DIM), WIDE)
    return pl.pallas_call(
        mlp_near_kernel,
        grid=(STEPS,),
        in_specs=[any_spec(), any_spec(), image_spec(DIM), fixed((DIM, DIM)), pl.BlockSpec((None, DIM, DIM), lambda i: (0, 0, 0), pipeline_mode=pl.Buffered(1)), fixed((DIM, DIM)), fixed((DIM, DIM)), fixed((TP, 16, DIM)), vec_spec(2, DIM), vec_spec(2, DIM)],
        out_specs=[image_spec(DIM)] * 3 + [any_spec()] * 3 + [vec_spec(8, DIM), vec_spec(8, DIM)],
        out_shape=[image_shape(DIM), wide_image, wide_image, half_shape(2, DIM, DIM), wide_shape(2 * DIM, DIM), wide_shape(2 * DIM, DIM), wide_shape(8, DIM), wide_shape(8, DIM)],
        scratch_shapes=[pltpu.VMEM((TP, IMAGES, PART, DIM), HALF), pltpu.VMEM((2, DIM, DIM), WIDE), pltpu.VMEM((2, DIM, DIM), WIDE), dma((3, STEPS)), dma((3, STEPS)), dma((2,)), dma((2,)), dma((5,))],
        compiler_params=params(1),
        cost_estimate=pl.CostEstimate(flops=60_000_000_000, bytes_accessed=80_000_000, transcendentals=6_000_000),
        name='mlp_near',
    )(d_out, w2, x1, w1, w1_near, w2, w2_near, bias, ln_scale, ln_bias)


def mlp_far_kernel(give, x1_ref, o_ref, dout_ref, y_ref, dh_ref, w1_rest, w2_far, wop, bias, ln_scale, ln_bias, fc2_b, dvec_near, db1_near, x2_out, dx1_ref, do_ref, near_a, keep_o, near_o, keep_b, near_b, dvec_ref, db1_ref, ybuf, dw1, dw2, dwo, y_send, y_recv, y_own, g_send, g_recv, local):
    step = pl.program_id(0)
    me, core, others = peers()
    slot = lax.rem(step, 2)

    def y_sends(at, group):
        return [push(ybuf.at[at, k], x2_out.at[image_rows(me, group)], y_send.at[k - 1, at], y_recv.at[k - 1, group], others[k]) for k in (2, 3, 1)]

    def y_keep(at, group):
        return pltpu.make_async_copy(ybuf.at[at, 0], x2_out.at[image_rows(me, group)], y_own.at[at])

    def y_wait(at, group):
        for c in y_sends(at, group):
            c.wait_send()
        y_keep(at, group).wait()

    early = push(give, near_a, g_send.at[0], g_recv.at[0], others[1])
    grads = [push(dw1.at[1], near_b.at[0:DIM], g_send.at[1], g_recv.at[1], others[1]), push(dw2.at[1], near_b.at[DIM:2 * DIM], g_send.at[2], g_recv.at[2], others[1]), push(dwo.at[576:768], near_b.at[2 * DIM:PACK], g_send.at[3], g_recv.at[3], others[1]), push(dwo.at[192:384], near_o, g_send.at[4], g_recv.at[4], others[1])]
    keeps = [pltpu.make_async_copy(dw1.at[0], keep_b.at[0:DIM], local.at[0]), pltpu.make_async_copy(dw2.at[0], keep_b.at[DIM:2 * DIM], local.at[1]), pltpu.make_async_copy(dwo.at[384:576], keep_b.at[2 * DIM:PACK], local.at[2]), pltpu.make_async_copy(dwo.at[0:192], keep_o, local.at[3])]

    @pl.when(step == 0)
    def _():
        meet(others)
        early.start()
        dw1[...] = jnp.zeros_like(dw1)
        dw2[...] = jnp.zeros_like(dw2)
        dwo[...] = jnp.zeros_like(dwo)
        dvec_ref[...] = dvec_near[...]
        db1_ref[...] = db1_near[...]

    x1 = jnp.concatenate([x1_ref[g] for g in range(GROUP)], axis=0)
    dout = jnp.concatenate([dout_ref[g] for g in range(GROUP)], axis=0)
    xhat, inv = normalize(x1.astype(WIDE))
    h2 = (xhat * ln_scale[1:2].astype(WIDE) + ln_bias[1:2].astype(WIDE)).astype(HALF)
    y = jnp.concatenate([y_ref[g] for g in range(GROUP)], axis=0)
    dh2 = jnp.concatenate([dh_ref[g] for g in range(GROUP)], axis=0)
    for f in range(2):
        y, dh2 = mlp_slot(f, f + 2, h2, dout, w1_rest[f + 1], w2_far[f], bias[f + 2, 3:4].astype(WIDE), y, dh2, dw1, dw2, db1_ref)
    x2 = (x1.astype(WIDE) + (y + row(fc2_b))).astype(HALF)

    @pl.when(step >= 2)
    def _():
        y_wait(slot, step - 2)

    for g in range(GROUP):
        for k in range(TP):
            ybuf[slot, k, g] = x2[TOK * g + PART * k:TOK * g + PART * k + PART]
    dh2 = dh2.astype(HALF).astype(WIDE)
    xhat, inv = normalize(x1.astype(WIDE))
    dout_f = dout.astype(WIDE)
    dx1 = (dout_f + norm_back(dh2, xhat, inv, ln_scale[1:2].astype(WIDE))).astype(HALF)
    dvec_ref[0:1] += col_sum(dh2 * xhat)
    dvec_ref[1:2] += col_sum(dh2)
    dvec_ref[3:4] += col_sum(dx1.astype(WIDE))
    d_o = dot_nt(dx1, jnp.concatenate([wop[k, 0:192] for k in range(TP)], axis=0)).astype(HALF)
    for g in range(GROUP):
        dx1_ref[g] = dx1[TOK * g:TOK * g + TOK]
        do_ref[g] = d_o[TOK * g:TOK * g + TOK]
    o = jnp.concatenate([o_ref[g] for g in range(GROUP)], axis=0)
    dwo[...] += dot_tn(o, dx1)

    for c in y_sends(slot, step):
        c.start()
    y_keep(slot, step).start()

    @pl.when(step == STEPS - 1)
    def _():
        for c in grads + keeps:
            c.start()
        for c in keeps:
            c.wait()
        early.wait()
        for c in grads:
            c.wait()
        for g in range(STEPS):
            for c in y_sends(g % 2, g):
                c.wait_recv()
        for g in (STEPS - 2, STEPS - 1):
            y_wait(g % 2, g)


def mlp_far(give, x1, o, dout, y, dh, w1_rest, w2_far, wop, bias, ln_scale, ln_bias, fc2_b, dvec_near, db1_near):
    dma = pltpu.SemaphoreType.DMA
    return pl.pallas_call(
        mlp_far_kernel,
        grid=(STEPS,),
        in_specs=[any_spec()] + [image_spec(DIM)] * 5 + [fixed((3, DIM, DIM)), fixed((2, DIM, DIM)), fixed((TP, 256, DIM)), fixed((TP, 16, DIM)), vec_spec(2, DIM), vec_spec(2, DIM), vec_spec(DIM), vec_spec(8, DIM), vec_spec(8, DIM)],
        out_specs=[any_spec(), image_spec(DIM), image_spec(DIM)] + [any_spec()] * 5 + [vec_spec(8, DIM), vec_spec(8, DIM)],
        out_shape=[half_shape(TP * IMAGES, PART, DIM), image_shape(DIM), image_shape(DIM), wide_shape(2 * DIM, DIM), wide_shape(192, DIM), wide_shape(192, DIM), wide_shape(PACK, DIM), wide_shape(PACK, DIM), wide_shape(8, DIM), wide_shape(8, DIM)],
        scratch_shapes=[pltpu.VMEM((2, TP, GROUP, PART, DIM), HALF), pltpu.VMEM((2, DIM, DIM), WIDE), pltpu.VMEM((2, DIM, DIM), WIDE), pltpu.VMEM((DIM, DIM), WIDE), dma((3, 2)), dma((3, STEPS)), dma((2,)), dma((5,)), dma((5,)), dma((4,))],
        compiler_params=params(2),
        cost_estimate=pl.CostEstimate(flops=70_000_000_000, bytes_accessed=80_000_000, transcendentals=6_000_000),
        name='mlp_far',
    )(give, x1, o, dout, y, dh, w1_rest, w2_far, wop, bias, ln_scale, ln_bias, fc2_b, dvec_near, db1_near)


def attn_bwd_kernel(keep_b, near_b, keep_a, near_a, keep_o, near_o, e_ref, qkv_ref, do_ref, dx1_ref, x_ref, wq, ln_scale, ln_bias, dvec2_ref, db1_ref, cross_out, dfc1_out, dfc2_out, dwo_out, dqkv_out, dwp_out, dpos_out, tiny_out, fetch_k, fetch_n, sums, dqkv, dwq, dwp, dpos, tiny, near_q, near_p, near_pos, far_q, far_p, far_pos, half_q, half_p, half_pos, p_send, p_recv, t_send, t_recv, n_send, n_recv, f_send, f_recv, h_send, h_recv, c_sem, o_sem, total1, total2, total3, local):
    step = pl.program_id(0)
    me, core, others = peers()
    pairs = [push(sums.at[n], cross_out.at[CHUNK * n:CHUNK * n + CHUNK], p_send.at[n], p_recv.at[n], others[2]) for n in range(CHUNKS)]

    def fetch(n):
        rows = pl.ds(n * CHUNK, CHUNK)
        at = lax.rem(n, 2)
        return (pltpu.make_async_copy(keep_b.at[rows], fetch_k.at[at], c_sem.at[0, at]), pltpu.make_async_copy(near_b.at[rows], fetch_n.at[at], c_sem.at[1, at]))

    @pl.when(step == 0)
    def _():
        meet(others)
        for c in fetch(0):
            c.start()

    @pl.when(step < CHUNKS)
    def _():
        @pl.when(step + 1 < CHUNKS)
        def _():
            for c in fetch(step + 1):
                c.start()
        for c in fetch(step):
            c.wait()
        at = lax.rem(step, 2)
        sums[step] = fetch_k[at] + fetch_n[at]

    @pl.when(step == 0)
    def _():
        dwq[...] = jnp.zeros_like(dwq)
        dwp[...] = jnp.zeros_like(dwp)
        dpos[...] = jnp.zeros_like(dpos)
        tiny[...] = jnp.zeros_like(tiny)

    @pl.when(step < CHUNKS)
    def _():
        push(sums.at[step], cross_out.at[pl.ds(step * CHUNK, CHUNK)], p_send.at[step], p_recv.at[step], others[2]).start()

    for g in range(GROUP):
        rows = slice(TOK * g, TOK * g + TOK)
        for pr in range(PAIRS):
            cols = slice(128 * pr, 128 * pr + 128)
            q = qkv_ref[g, :, 128 * pr:128 * pr + 128]
            k = qkv_ref[g, :, DIM + 128 * pr:DIM + 128 * pr + 128]
            v = qkv_ref[g, :, 2 * DIM + 128 * pr:2 * DIM + 128 * pr + 128]
            d_o = do_ref[g, :, 128 * pr:128 * pr + 128]
            probs = []
            dscores = []
            for j in range(2):
                s = dot_nt(k, mask_half(q, j))
                m = jnp.max(s, axis=0, keepdims=True)
                e = jnp.exp2((s - m) * EXP_SCALE)
                l = jnp.sum(e, axis=0, keepdims=True)
                p = e * (1.0 / l)
                dp = dot_nt(v, mask_half(d_o, j)).astype(HALF).astype(WIDE)
                delta = jnp.sum(dp * p, axis=0, keepdims=True)
                ds = (p * ((dp - delta) * 0.125)).astype(HALF)
                probs.append(p.astype(HALF))
                dscores.append(ds)
            dv = dot_nn(jnp.concatenate(probs, axis=1), jnp.concatenate([mask_half(d_o, 0), mask_half(d_o, 1)], axis=0))
            dk = dot_nn(jnp.concatenate(dscores, axis=1), jnp.concatenate([mask_half(q, 0), mask_half(q, 1)], axis=0))
            dq = dot_tn(jnp.concatenate(dscores, axis=0), jnp.concatenate([mask_half(k, 0), mask_half(k, 1)], axis=0))
            dqkv[rows, 128 * pr:128 * pr + 128] = dq.astype(HALF)
            dqkv[rows, DIM + 128 * pr:DIM + 128 * pr + 128] = dk.astype(HALF)
            dqkv[rows, 2 * DIM + 128 * pr:2 * DIM + 128 * pr + 128] = dv.astype(HALF)
    e_f = jnp.concatenate([e_ref[g] for g in range(GROUP)], axis=0).astype(WIDE)
    xhat, inv = normalize(e_f)
    h1 = (xhat * ln_scale[0:1].astype(WIDE) + ln_bias[0:1].astype(WIDE)).astype(HALF)
    dh1 = None
    for s in range(3):
        part = dqkv[:, DIM * s:DIM * s + DIM]
        tiny[s:s + 1] += col_sum(part.astype(WIDE))
        grad = dot_tn(part, h1)
        for k in range(TP):
            dwq[k, s] += grad[192 * k:192 * k + 192]
        term = dot_nn(part, jnp.concatenate([wq[k, s] for k in range(TP)], axis=0))
        dh1 = term if dh1 is None else dh1 + term
    dh1 = dh1.astype(HALF).astype(WIDE)
    dx1 = jnp.concatenate([dx1_ref[g] for g in range(GROUP)], axis=0).astype(WIDE)
    de = (dx1 + norm_back(dh1, xhat, inv, ln_scale[0:1].astype(WIDE))).astype(HALF)
    de_f = de.astype(WIDE)
    tiny[8:9] += col_sum(dh1 * xhat)
    tiny[9:10] += col_sum(dh1)
    acc = de_f[0:TOK]
    for g in range(1, GROUP):
        acc = acc + de_f[TOK * g:TOK * g + TOK]
    dpos[...] += acc
    x = jnp.concatenate([x_ref[g] for g in range(GROUP)], axis=0)
    dwp[...] += dot_tn(x, de)

    @pl.when(step == STEPS - 1)
    def _():
        tiny[4:8] = db1_ref[0:4]
        tiny[10:11] = col_sum(dpos[...])
        tiny[12:16] = dvec2_ref[0:4]
        chip = lax.div(me, 2)
        my_quarter = pl.ds(384 * core + 192 * chip, 192)
        far_quarter = pl.ds(384 * core + 192 * (1 - chip), 192)
        my_part = pl.ds(192 * chip, 192)
        other_half = pl.ds(384 * (1 - core), 384)
        my_half = pl.ds(384 * core, 384)
        near = [push(dwq.at[3], near_q.at[1], n_send.at[0], n_recv.at[0], others[1]), push(dwq.at[1], near_q.at[0], n_send.at[1], n_recv.at[1], others[1]), push(dpos.at[3 * PART:4 * PART], near_pos.at[1], n_send.at[2], n_recv.at[2], others[1]), push(dpos.at[PART:2 * PART], near_pos.at[0], n_send.at[3], n_recv.at[3], others[1]), push(dwp.at[other_half], near_p, n_send.at[4], n_recv.at[4], others[1])]
        tinies = [push(tiny, tiny_out.at[k - 1], t_send.at[k - 1], t_recv.at[k - 1], others[k]) for k in range(1, TP)]
        far = [push(dwq.at[2], far_q, f_send.at[0], f_recv.at[0], others[2]), push(dwp.at[far_quarter], far_p, f_send.at[1], f_recv.at[1], others[2]), push(dpos.at[2 * PART:3 * PART], far_pos, f_send.at[2], f_recv.at[2], others[2])]
        near[4].start()
        near[0].start()
        for c in near[1:4] + tinies:
            c.start()
        near[4].wait_recv()
        dwp[my_half] += near_p[...]
        far[1].start()
        near[0].wait_recv()
        for s in range(3):
            dwq[2, s] += near_q[1, s]
        far[0].start()
        near[2].wait_recv()
        dpos[2 * PART:3 * PART] += near_pos[1]
        far[2].start()
        near[1].wait_recv()
        near[3].wait_recv()
        far[1].wait()
        half_p[my_part] = (dwp[my_quarter] + far_p[...]).astype(HALF)
        spread = push(half_p.at[my_part], half_p.at[my_part], h_send.at[1], h_recv.at[1], others[2])
        spread.start()
        for c in pairs:
            c.wait()
        outs = []

        def total(keep_ref, near_ref, cross_ref, rows):
            copies = [pltpu.make_async_copy(r, sums.at[n, 0:rows], c_sem.at[n, 0]) for n, r in enumerate((keep_ref, near_ref, cross_ref))]
            for c in copies:
                c.start()
            for c in copies:
                c.wait()
            return (sums[0, 0:rows] + sums[1, 0:rows]) + sums[2, 0:rows]

        for n in range(3):
            rows = slice(256 * n, 256 * n + 256)
            total1[rows] = total(keep_a.at[rows], near_a.at[rows], cross_out.at[rows], 256).astype(HALF)
        outs.append(pltpu.make_async_copy(total1, dfc1_out, o_sem.at[0]))
        outs[0].start()
        for n in range(3):
            rows = slice(DIM + 256 * n, DIM + 256 * n + 256)
            part = total(keep_a.at[rows], near_a.at[rows], cross_out.at[rows], 256)
            total2[:, 256 * n:256 * n + 256] = part.T.astype(HALF)
        outs.append(pltpu.make_async_copy(total2, dfc2_out, o_sem.at[1]))
        outs[1].start()
        total3[...] = total(keep_o, near_o, cross_out.at[2 * DIM:PACK], 192).astype(HALF)
        outs.append(pltpu.make_async_copy(total3, dwo_out, o_sem.at[2]))
        outs[2].start()
        far[0].wait_recv()
        for s in range(3):
            half_q[s] = ((dwq[0, s] + near_q[0, s]) + far_q[s]).astype(HALF)
        q_copy = pltpu.make_async_copy(half_q, dqkv_out, local.at[0])
        q_copy.start()
        spread.wait()
        swap = push(half_p, dwp_out.at[my_half], h_send.at[0], h_recv.at[0], others[1])
        swap.start()
        p_copy = pltpu.make_async_copy(half_p, dwp_out.at[my_half], local.at[1])
        p_copy.start()
        far[2].wait_recv()
        half_pos[...] = ((dpos[0:PART] + near_pos[0]) + far_pos[...]).astype(HALF)
        pos_copy = pltpu.make_async_copy(half_pos, dpos_out, local.at[2])
        pos_copy.start()
        for c in near:
            c.wait_send()
        for c in tinies:
            c.wait()
        far[0].wait_send()
        far[2].wait_send()
        tiny_copy = pltpu.make_async_copy(tiny, tiny_out.at[3], local.at[3])
        tiny_copy.start()
        for c in outs:
            c.wait()
        q_copy.wait()
        p_copy.wait()
        pos_copy.wait()
        tiny_copy.wait()
        swap.wait()


def attn_bwd(keep_b, near_b, keep_a, near_a, keep_o, near_o, e, qkv, d_o, dx1, x, wq, ln_scale, ln_bias, dvec2, db1):
    dma = pltpu.SemaphoreType.DMA
    return pl.pallas_call(
        attn_bwd_kernel,
        grid=(STEPS,),
        in_specs=[any_spec()] * 6 + [image_spec(DIM), image_spec(3 * DIM), image_spec(DIM), image_spec(DIM), image_spec(DIM), fixed((TP, 3, 192, DIM)), vec_spec(2, DIM), vec_spec(2, DIM), vec_spec(8, DIM), vec_spec(8, DIM)],
        out_specs=[any_spec()] * 8,
        out_shape=[wide_shape(PACK, DIM), half_shape(DIM, DIM), half_shape(DIM, DIM), half_shape(192, DIM), half_shape(3, 192, DIM), half_shape(DIM, DIM), half_shape(PART, DIM), wide_shape(TP, 16, DIM)],
        scratch_shapes=[pltpu.VMEM((2, CHUNK, DIM), WIDE), pltpu.VMEM((2, CHUNK, DIM), WIDE), pltpu.VMEM((CHUNKS, CHUNK, DIM), WIDE), pltpu.VMEM((ROWS, 3 * DIM), HALF), pltpu.VMEM((TP, 3, 192, DIM), WIDE), pltpu.VMEM((DIM, DIM), WIDE), pltpu.VMEM((TOK, DIM), WIDE), pltpu.VMEM((16, DIM), WIDE), pltpu.VMEM((2, 3, 192, DIM), WIDE), pltpu.VMEM((384, DIM), WIDE), pltpu.VMEM((2, PART, DIM), WIDE), pltpu.VMEM((3, 192, DIM), WIDE), pltpu.VMEM((192, DIM), WIDE), pltpu.VMEM((PART, DIM), WIDE), pltpu.VMEM((3, 192, DIM), HALF), pltpu.VMEM((384, DIM), HALF), pltpu.VMEM((PART, DIM), HALF), dma((CHUNKS,)), dma((CHUNKS,)), dma((3,)), dma((3,)), dma((5,)), dma((5,)), dma((3,)), dma((3,)), dma((2,)), dma((2,)), dma((3, 2)), dma((3,)), pltpu.VMEM((DIM, DIM), HALF), pltpu.VMEM((DIM, DIM), HALF), pltpu.VMEM((192, DIM), HALF), dma((4,))],
        compiler_params=params(3),
        cost_estimate=pl.CostEstimate(flops=100_000_000_000, bytes_accessed=80_000_000, transcendentals=12_000_000),
        name='attn_bwd',
    )(keep_b, near_b, keep_a, near_a, keep_o, near_o, e, qkv, d_o, dx1, x, wq, ln_scale, ln_bias, dvec2, db1)


def finish_kernel(x2, fc1, fc2, wo, qkv, wp, pos, tiny, x2_out, fc1_out, fc2_out, wo_out, qkv_out, wp_out, pos_out, patch_b, ln_scale, ln_bias, qkv_b, out_b, fc1_b, fc2_b):
    for src, dst in ((x2, x2_out), (fc1, fc1_out), (fc2, fc2_out), (wo, wo_out), (qkv, qkv_out), (wp, wp_out), (pos, pos_out)):
        dst[...] = src[...]

    @pl.when(pl.program_id(0) == 0)
    def _():
        vec = ((tiny[3] + tiny[0]) + (tiny[1] + tiny[2])).astype(HALF)
        patch_b[...] = vec[10:11].reshape(DIM)
        ln_scale[0:1] = vec[8:9]
        ln_scale[1:2] = vec[12:13]
        ln_bias[0:1] = vec[9:10]
        ln_bias[1:2] = vec[13:14]
        fc2_b[...] = vec[14:15].reshape(DIM)
        out_b[...] = vec[15:16].reshape(DIM)
        fc1_b[...] = ((tiny[3, 4:5] + tiny[0, 5:6]) + (tiny[1, 6:7] + tiny[2, 7:8])).astype(HALF).reshape(DIM)
        for s in range(3):
            for h in range(3):
                at = [tiny[j, s:s + 1, 192 * k + 64 * h:192 * k + 64 * h + 64] for k, j in enumerate((3, 0, 1, 2))]
                qkv_b[s, h:h + 1] = ((at[0] + at[1]) + (at[2] + at[3])).astype(HALF)


def finish(x2, fc1, fc2, wo, qkv, wp, pos, tiny):
    arrays = (x2, fc1, fc2, wo, qkv, wp, pos)
    specs = [pl.BlockSpec((a.shape[0] // 4,) + a.shape[1:], lambda i, n=a.ndim: (i,) + (0,) * (n - 1)) for a in arrays]
    smalls = [(DIM,), (2, DIM), (2, DIM), (3, 3, 64), (DIM,), (DIM,), (DIM,)]
    return pl.pallas_call(
        finish_kernel,
        grid=(4,),
        in_specs=specs + [vec_spec(TP, 16, DIM)],
        out_specs=specs + [vec_spec(*shape) for shape in smalls],
        out_shape=[jax.ShapeDtypeStruct(a.shape, a.dtype) for a in arrays] + [half_shape(*shape) for shape in smalls],
        compiler_params=pltpu.CompilerParams(dimension_semantics=('arbitrary',), vmem_limit_bytes=67043328),
        name='finish',
    )(*arrays, tiny)


def group_step(patches, patch_w, patch_b, pos_emb, ln_scale, ln_bias, qkv_w, qkv_b, out_w, out_b, fc1_w, fc1_b, fc2_w, fc2_b, d_out):
    wq = qkv_w.transpose(0, 2, 3, 1).reshape(3, 192, DIM)
    wo = out_w.reshape(192, DIM)
    e, qkv, o, x1, x, wq_all, wop_all, bias_all, w1_rest, w2_near = attn_fwd(patches, wq, wo, pos_emb, fc1_w, fc2_w, patch_w, patch_b, qkv_b, fc1_b, out_b, ln_scale, ln_bias)
    dout, y, dh, w2_far, keep_a, give_a, dvec_n, db1_n = mlp_near(d_out, x1, fc1_w, w1_rest, fc2_w, w2_near, bias_all, ln_scale, ln_bias)
    x_two, dx1, d_o, near_a, keep_o, near_o, keep_b, near_b, dvec2, db1 = mlp_far(give_a, x1, o, dout, y, dh, w1_rest, w2_far, wop_all, bias_all, ln_scale, ln_bias, fc2_b, dvec_n, db1_n)
    _, d_fc1_w, d_fc2_w, d_out_w, d_qkv, d_patch_w, d_pos, tiny = attn_bwd(keep_b, near_b, keep_a, near_a, keep_o, near_o, e, qkv, d_o, dx1, x, wq_all, ln_scale, ln_bias, dvec2, db1)
    x_two, d_fc1_w, d_fc2_w, d_out_w, d_qkv, d_patch_w, d_pos, d_patch_b, d_ln_scale, d_ln_bias, d_qkv_b, d_out_b, d_fc1_b, d_fc2_b = finish(x_two, d_fc1_w, d_fc2_w, d_out_w, d_qkv.reshape(576, DIM), d_patch_w, d_pos, tiny)
    d_qkv_w = d_qkv.reshape(3, 3, 64, DIM).transpose(0, 3, 1, 2)
    return (x_two, d_patch_w, d_patch_b, d_pos, d_ln_scale, d_ln_bias, d_qkv_w, d_qkv_b, d_out_w.reshape(3, 64, DIM), d_out_b, d_fc1_w, d_fc1_b, d_fc2_w, d_fc2_b)


def solution(mesh):
    in_specs = (P('dp', 'tp', None), P(), P(), P('tp', None), P(), P(), P(None, None, 'tp', None), P(None, 'tp', None), P('tp', None, None), P(), P(None, 'tp'), P('tp'), P('tp', None), P(), P('dp', 'tp', None))
    out_specs = (P('dp', 'tp', None), P('dp', None), P('dp'), P(('dp', 'tp'), None), P('dp', None), P('dp', None), P('dp', None, 'tp', None), P('dp', 'tp', None), P(('dp', 'tp'), None, None), P('dp'), P('dp', 'tp'), P(('dp', 'tp')), P(('dp', 'tp'), None), P('dp'))
    return jax.shard_map(group_step, mesh=mesh, in_specs=in_specs, out_specs=out_specs, check_vma=False)
```

time: 595 us -> 547 us (0.919)
  other arithmetic: 19.5 us -> 0 us
  local copies, waits for them, and re-layouts: 19.2 us -> 0 us
  Pallas kernels: 550 us -> 539 us
    pallas_call x1, Pallas kernels: 158 us -> 133 us  [attn_fwd(): pl.pallas_call(attn_fwd_kernel, grid=(STEPS,), in_specs=[any_spec()] * 6...]
    pallas_call x2 -> x4, Pallas kernels: 392 us -> 406 us  [the longest x1 189 us: attn_bwd(): pl.pallas_call(attn_bwd_kernel, grid=(STEPS,), in_specs=[any_spec()] * 6...]
    unnamed x13 -> x0, local copies, waits for them, and re-layouts: 11.3 us -> none
    convert_element_type x5 -> x0, other arithmetic: 7.94 us -> none  [the longest x1 6.46 us: group_step(): total = (keep[0] + near[0] + cross).astype(HALF)]
    add x1 -> x0, other arithmetic: 7.14 us -> none  [group_step(): pair = keep[1] + near[1]]
where the time goes in v4:
time: 547 us; the launch traced here: 540 us
  Pallas kernels  539 us (99%)
    pallas_call x1, Pallas kernels, attn_bwd(): pl.pallas_call(attn_bwd_kernel, grid=(STEPS,), in_specs=[any_spec()] * 6...  189 us
    pallas_call x1, Pallas kernels, attn_fwd(): pl.pallas_call(attn_fwd_kernel, grid=(STEPS,), in_specs=[any_spec()] * 6...  133 us
    pallas_call x1, Pallas kernels, mlp_far(): pl.pallas_call(mlp_far_kernel, grid=(STEPS,), in_specs=[any_spec()] + [im...  105 us
    pallas_call x1, Pallas kernels, mlp_near(): pl.pallas_call(mlp_near_kernel, grid=(STEPS,), in_specs=[any_spec(), any_...  104 us

profile of v4, /device:TPU:0, one launch (start us, length us, event | category | flops | bytes accessed | tf_op | source)
XLA Modules:
  0.0 540.3 jit_solution(8696113315608620242)
XLA Ops:
  0.6 133.1 %attn_fwd.1 = (bf16[16,256,768]{2,1,0:T(8,128)(2,1)}, bf16[16,256,2304]{2,1,0:T(8,128)(2,1)}, bf16[16,256,768]{2,1,0:T(8,128)(2,1)}, bf16[16,256,768]{2,1,0:T(8,...) custom-call(bf16[64,64,768]{2,1,0:T(8,128)(2,1)} %patches.1, ...), custom_call_target="tpu_custom_call" | custom-call | flops 60000002048 | bytes 50000000 | tf_op jit(solution)/shard_map/attn_fwd/pallas_call | solution.py:251
  133.8 103.5 %mlp_near.1 = (bf16[16,256,768]{2,1,0:T(8,128)(2,1)}, f32[16,256,768]{2,1,0:T(8,128)}, f32[16,256,768]{2,1,0:T(8,128)}, bf16[2,768,768]{2,1,0:T(8,128)(2,1)}, f3...) custom-call(bf16[64,64,768]{2,1,0:T(8,128)(2,1)} %d_out.1, ...), custom_call_target="tpu_custom_call" | custom-call | flops 60000002048 | bytes 80000000 | tf_op jit(solution)/shard_map/mlp_near/pallas_call | solution.py:352
  237.3 104.5 %mlp_far.1 = (bf16[64,64,768]{2,1,0:T(8,128)(2,1)}, bf16[16,256,768]{2,1,0:T(8,128)(2,1)}, bf16[16,256,768]{2,1,0:T(8,128)(2,1)}, f32[1536,768]{1,0:T(8,128)}, f...) custom-call(f32[1536,768]{1,0:T(8,128)} %get-tuple-element.67.give, ...), custom_call_target="tpu_custom_call" | custom-call | flops 70000001024 | bytes 80000000 | tf_op jit(solution)/shard_map/mlp_far/pallas_call | solution.py:448
  341.8 189.2 %attn_bwd.1 = (f32[1728,768]{1,0:T(8,128)}, bf16[768,768]{1,0:T(8,128)(2,1)}, bf16[768,768]{1,0:T(8,128)(2,1)}, bf16[192,768]{1,0:T(8,128)(2,1)}, bf16[3,192,768...) custom-call(f32[1728,768]{1,0:T(8,128)} %get-tuple-element.77.keep_b, ...), custom_call_target="tpu_custom_call" | custom-call | flops 99999997952 | bytes 80000000 | tf_op jit(solution)/shard_map/attn_bwd/pallas_call | solution.py:644
  531.0 8.8 %finish.1 = (bf16[64,64,768]{2,1,0:T(8,128)(2,1)}, bf16[768,768]{1,0:T(8,128)(2,1)}, bf16[768,768]{1,0:T(8,128)(2,1)}, bf16[192,768]{1,0:T(8,128)(2,1)}, bf16[57...) custom-call(bf16[64,64,768]{2,1,0:T(8,128)(2,1)} %get-tuple-element., ...), custom_call_target="tpu_custom_call" | custom-call | tf_op jit(solution)/shard_map/finish/pallas_call | solution.py:682

commit v5 on v4

--- a/solution.py
+++ b/solution.py
@@ -14,15 +14,19 @@
 TOK = 256
 PART = 64
 DIM = 768
-GROUP = 2
+GROUP = 1
 ROWS = GROUP * TOK
 STEPS = IMAGES // GROUP
+FRONT = 2
+FRONT_STEPS = IMAGES // FRONT
 PAIRS = 6
 EXP_SCALE = 0.125 * 1.4426950408889634
 GELU_C = 0.7978845608028654
 GELU_A = 0.044715
-AHEAD = 3
+AHEAD = 6 // FRONT
 PACK = 2 * DIM + 192
+EARLY = 256
+LATE = DIM - EARLY
 CHUNKS = 6
 CHUNK = PACK // CHUNKS
 
@@ -89,30 +93,63 @@
     return pltpu.make_async_remote_copy(src_ref=src, dst_ref=dst, send_sem=send, recv_sem=recv, device_id={'tp': peer}, device_id_type=pl.DeviceIdType.MESH)
 
 
-def image_rows(owner, group):
-    return pl.ds(owner * IMAGES + group * GROUP, GROUP)
+def image_rows(owner, group, size):
+    return pl.ds(owner * IMAGES + group * size, size)
 
 
 def group_sends(src, buf, send, recv, others, group):
-    return [push(src.at[image_rows(others[k], group)], buf.at[k, pl.ds(group * GROUP, GROUP)], send.at[k - 1, group], recv.at[k - 1, group], others[k]) for k in (2, 3, 1)]
+    return [push(src.at[image_rows(others[k], group, FRONT)], buf.at[k, pl.ds(group * FRONT, FRONT)], send.at[k - 1, group], recv.at[k - 1, group], others[k]) for k in (2, 3, 1)]
 
 
 def slot_rows(buf, group):
-    base = group * GROUP
-    return jnp.concatenate([buf[k, base + g] for g in range(GROUP) for k in range(TP)], axis=0)
-
-
-def attn_fwd_kernel(patches, wq_own, wo_own, pos_own, w1_own, w2_own, wp, patch_b, qkv_b, fc1_b, out_b, ln_scale, ln_bias, e_ref, qkv_ref, o_ref, x1_ref, x_ref, wq_out, wop_out, bias_out, w1_out, w2_near, xbuf, wq, wop, bias, bias_own, bqkv, x_send, x_recv, w_send, w_recv, local):
+    base = group * FRONT
+    return jnp.concatenate([buf[k, base + g] for g in range(FRONT) for k in range(TP)], axis=0)
+
+
+def mlp_slot(f, base, h2, dout, w1, w2, bias, y, dh2, dw1, dw2, db1_ref):
+    hids = []
+    dpres = []
+    for c in range(w1.shape[1] // 256):
+        cols = slice(256 * c, 256 * c + 256)
+        units = slice(base + 256 * c, base + 256 * c + 256)
+        pre = dot_nn(h2, w1[:, cols]) + bias[f, 3:4, units].astype(WIDE)
+        sq = pre * pre
+        t = jnp.tanh(pre * (GELU_C + (GELU_C * GELU_A) * sq))
+        half_pre = 0.5 * pre
+        hids.append((half_pre + half_pre * t).astype(HALF))
+        slope = (0.5 + 0.5 * t) + (half_pre * (1.0 - t * t)) * (GELU_C + (3.0 * GELU_C * GELU_A) * sq)
+        dpre = dot_nt(dout, w2[cols]).astype(HALF).astype(WIDE) * slope
+        db1_ref[f:f + 1, units] += col_sum(dpre)
+        dpres.append(dpre.astype(HALF))
+    hid = jnp.concatenate(hids, axis=1)
+    dpre_h = jnp.concatenate(dpres, axis=1)
+    part_y = dot_nn(hid, w2)
+    part_h = dot_nt(dpre_h, w1)
+    y = part_y if y is None else y + part_y
+    dh2 = part_h if dh2 is None else dh2 + part_h
+    dw1[...] += dot_tn(h2, dpre_h)
+    dw2[...] += dot_tn(dout, hid)
+    return y, dh2
+
+
+def front_kernel(patches, d_out, wq_own, wo_own, pos_own, w1_own, w2_own, wp, patch_b, qkv_b, fc1_b, out_b, ln_scale, ln_bias, e_ref, qkv_ref, o_ref, x1_ref, x_ref, dout_ref, y_ref, dh_ref, wq_out, wop_out, bias_out, w1_far, w2_far, keep_out, give_out, part1_out, part2_out, dvec_ref, db1_ref, xbuf, dbuf, wq, wop, w1, w2, wa1, wa2, bias, bias_own, bqkv, dw1, dw2, dwa1, dwa2, x_send, x_recv, d_send, d_recv, w_send, w_recv, local, done):
     step = pl.program_id(0)
     me, core, others = peers()
     small = []
     for n, (src, cut) in enumerate(((wq_own, None), (wo_own, (0, 192)), (pos_own, (192, 256)))):
         at = [wq.at[k] if cut is None else wop.at[k, cut[0]:cut[1]] for k in range(TP)]
         small.append((push(src, at[2], w_send.at[n, 1], w_recv.at[n, 1], others[2]), push(src, at[1], w_send.at[n, 0], w_recv.at[n, 0], others[1]), push(at[2], at[3], w_send.at[n, 2], w_recv.at[n, 2], others[1])))
-    large = (push(w1_own, w1_out.at[1], w_send.at[3, 1], w_recv.at[3, 1], others[2]), push(w1_own, w1_out.at[0], w_send.at[3, 0], w_recv.at[3, 0], others[1]), push(w1_out.at[1], w1_out.at[2], w_send.at[3, 2], w_recv.at[3, 2], others[1]), push(w2_own, w2_near, w_send.at[4, 0], w_recv.at[4, 0], others[1]))
+    near = [push(w1_own, w1.at[1], w_send.at[3, 0], w_recv.at[3, 0], others[1]), push(w2_own, w2.at[1], w_send.at[4, 0], w_recv.at[4, 0], others[1])]
+    early = [push(w1_own.at[:, 0:EARLY], wa1.at[0], w_send.at[6, 0], w_recv.at[6, 0], others[2]), push(w2_own.at[0:EARLY], wa2.at[0], w_send.at[7, 0], w_recv.at[7, 0], others[2])]
+    early_relay = [push(wa1.at[0], wa1.at[1], w_send.at[6, 1], w_recv.at[6, 1], others[1]), push(wa2.at[0], wa2.at[1], w_send.at[7, 1], w_recv.at[7, 1], others[1])]
+    far = [push(w1_own.at[:, EARLY:DIM], w1_far.at[0], w_send.at[3, 1], w_recv.at[3, 1], others[2]), push(w2_own.at[EARLY:DIM], w2_far.at[0], w_send.at[4, 1], w_recv.at[4, 1], others[2])]
+    relay = [push(w1_far.at[0], w1_far.at[1], w_send.at[3, 2], w_recv.at[3, 2], others[1]), push(w2_far.at[0], w2_far.at[1], w_send.at[4, 2], w_recv.at[4, 2], others[1])]
     biases = [push(bias_own, bias.at[k], w_send.at[5, k - 1], w_recv.at[5, k - 1], others[k]) for k in range(1, TP)]
-    own = [pltpu.make_async_copy(wq_own, wq.at[0], local.at[0]), pltpu.make_async_copy(wo_own, wop.at[0, 0:192], local.at[1]), pltpu.make_async_copy(pos_own, wop.at[0, 192:256], local.at[2]), pltpu.make_async_copy(patches.at[pl.ds(me * IMAGES, IMAGES)], xbuf.at[0], local.at[3])]
+    own = [pltpu.make_async_copy(wq_own, wq.at[0], local.at[0]), pltpu.make_async_copy(wo_own, wop.at[0, 0:192], local.at[1]), pltpu.make_async_copy(pos_own, wop.at[0, 192:256], local.at[2]), pltpu.make_async_copy(patches.at[pl.ds(me * IMAGES, IMAGES)], xbuf.at[0], local.at[3]), pltpu.make_async_copy(d_out.at[pl.ds(me * IMAGES, IMAGES)], dbuf.at[0], local.at[7]), pltpu.make_async_copy(w1_own, w1.at[0], local.at[8]), pltpu.make_async_copy(w2_own, w2.at[0], local.at[9])]
     flush = [pltpu.make_async_copy(wq, wq_out, local.at[4]), pltpu.make_async_copy(wop, wop_out, local.at[5]), pltpu.make_async_copy(bias, bias_out, local.at[6])]
+
+    def arrivals(group):
+        return group_sends(patches, xbuf, x_send, x_recv, others, group) + group_sends(d_out, dbuf, d_send, d_recv, others, group)
 
     @pl.when(step == 0)
     def _():
@@ -130,21 +167,25 @@
         for n in range(3):
             small[n][1].start()
         for g in range(AHEAD):
-            for c in group_sends(patches, xbuf, x_send, x_recv, others, g):
+            for c in arrivals(g) + (early if g == 0 else []):
                 c.start()
-        for c in own:
-            c.start()
+        for c in own + near:
+            c.start()
+        dw1[...] = jnp.zeros_like(dw1)
+        dw2[...] = jnp.zeros_like(dw2)
+        dwa1[...] = jnp.zeros_like(dwa1)
+        dwa2[...] = jnp.zeros_like(dwa2)
+        dvec_ref[...] = jnp.zeros_like(dvec_ref)
+        db1_ref[...] = jnp.zeros_like(db1_ref)
         for n in range(3):
             small[n][0].wait_recv()
             small[n][2].start()
-        large[1].start()
-        large[3].start()
         for c in own:
             c.wait()
         for n in range(3):
             small[n][1].wait_recv()
             small[n][2].wait_recv()
-        for c in biases:
+        for c in biases + near:
             c.wait_recv()
         for s in range(3):
             for k in range(TP):
@@ -152,22 +193,23 @@
         for c in flush:
             c.start()
 
-    @pl.when(step + AHEAD < STEPS)
-    def _():
-        for c in group_sends(patches, xbuf, x_send, x_recv, others, step + AHEAD):
-            c.start()
-
-    @pl.when(step == STEPS - AHEAD)
-    def _():
-        large[0].start()
+    @pl.when(step + AHEAD < FRONT_STEPS)
+    def _():
+        for c in arrivals(step + AHEAD):
+            c.start()
+
+    @pl.when(step == FRONT_STEPS - AHEAD)
+    def _():
+        far[0].start()
+        far[1].start()
 
     for c in group_sends(patches, xbuf, x_send, x_recv, others, step):
         c.wait_recv()
     x = slot_rows(xbuf, step)
     posb = jnp.concatenate([wop[k, 192:192 + PART] for k in range(TP)], axis=0).astype(WIDE) + row(patch_b)
-    emb = dot_nn(x, wp[...]) + jnp.concatenate([posb] * GROUP, axis=0)
+    emb = dot_nn(x, wp[...]) + jnp.concatenate([posb] * FRONT, axis=0)
     e_h = emb.astype(HALF)
-    for g in range(GROUP):
+    for g in range(FRONT):
         x_ref[g] = x[TOK * g:TOK * g + TOK]
         e_ref[g] = e_h[TOK * g:TOK * g + TOK]
     e_f = e_h.astype(WIDE)
@@ -175,9 +217,9 @@
     h1 = (xhat * ln_scale[0:1].astype(WIDE) + ln_bias[0:1].astype(WIDE)).astype(HALF)
     for s in range(3):
         part = (dot_nt(h1, jnp.concatenate([wq[k, s] for k in range(TP)], axis=0)) + bqkv[s:s + 1]).astype(HALF)
-        for g in range(GROUP):
+        for g in range(FRONT):
             qkv_ref[g, :, DIM * s:DIM * s + DIM] = part[TOK * g:TOK * g + TOK]
-    for g in range(GROUP):
+    for g in range(FRONT):
         for pr in range(PAIRS):
             q = qkv_ref[g, :, 128 * pr:128 * pr + 128]
             k = qkv_ref[g, :, DIM + 128 * pr:DIM + 128 * pr + 128]
@@ -191,127 +233,13 @@
                 probs.append((e * (1.0 / l)).astype(HALF))
             pv = dot_nn(jnp.concatenate(probs, axis=1), jnp.concatenate([mask_half(v, 0), mask_half(v, 1)], axis=0))
             o_ref[g, :, 128 * pr:128 * pr + 128] = pv.astype(HALF)
-    o = jnp.concatenate([o_ref[g] for g in range(GROUP)], axis=0)
-    e_f = jnp.concatenate([e_ref[g] for g in range(GROUP)], axis=0).astype(WIDE)
+    o = jnp.concatenate([o_ref[g] for g in range(FRONT)], axis=0)
+    e_f = jnp.concatenate([e_ref[g] for g in range(FRONT)], axis=0).astype(WIDE)
     x1 = (e_f + (dot_nn(o, jnp.concatenate([wop[k, 0:192] for k in range(TP)], axis=0)) + row(out_b))).astype(HALF)
-    for g in range(GROUP):
+    for g in range(FRONT):
         x1_ref[g] = x1[TOK * g:TOK * g + TOK]
 
-    @pl.when(step == STEPS - 1)
-    def _():
-        large[0].wait_recv()
-        large[2].start()
-        for c in large[1:]:
-            c.wait_recv()
-        for c in small[0] + small[1] + small[2] + large:
-            c.wait_send()
-        for c in biases:
-            c.wait_send()
-        for c in flush:
-            c.wait()
-        for g in range(STEPS):
-            for c in group_sends(patches, xbuf, x_send, x_recv, others, g):
-                c.wait_send()
-
-
-def fixed(shape):
-    return pl.BlockSpec(shape, lambda i: (0,) * len(shape), pipeline_mode=pl.Buffered(1))
-
-
-def image_spec(width):
-    return pl.BlockSpec((GROUP, TOK, width), lambda i: (i, 0, 0))
-
-
-def any_spec():
-    return pl.BlockSpec(memory_space=pl.ANY)
-
-
-def params(cid):
-    return pltpu.CompilerParams(dimension_semantics=('arbitrary',), vmem_limit_bytes=67043328, collective_id=cid, has_side_effects=True)
-
-
-def image_shape(width):
-    return jax.ShapeDtypeStruct((IMAGES, TOK, width), HALF)
-
-
-def half_shape(*shape):
-    return jax.ShapeDtypeStruct(shape, HALF)
-
-
-def wide_shape(*shape):
-    return jax.ShapeDtypeStruct(shape, WIDE)
-
-
-def vec_spec(*shape):
-    return pl.BlockSpec(shape, lambda i: (0,) * len(shape))
-
-
-def attn_fwd(patches, wq, wo, pos, w1, w2, wp, patch_b, qkv_b, fc1_b, out_b, ln_scale, ln_bias):
-    dma = pltpu.SemaphoreType.DMA
-    return pl.pallas_call(
-        attn_fwd_kernel,
-        grid=(STEPS,),
-        in_specs=[any_spec()] * 6 + [fixed((DIM, DIM)), vec_spec(DIM), vec_spec(3, 3, 64), vec_spec(DIM), vec_spec(DIM), vec_spec(2, DIM), vec_spec(2, DIM)],
-        out_specs=[image_spec(DIM), image_spec(3 * DIM), image_spec(DIM), image_spec(DIM), image_spec(DIM)] + [any_spec()] * 5,
-        out_shape=[image_shape(DIM), image_shape(3 * DIM), image_shape(DIM), image_shape(DIM), image_shape(DIM), half_shape(TP, 3, 192, DIM), half_shape(TP, 256, DIM), half_shape(TP, 16, DIM), half_shape(3, DIM, DIM), half_shape(DIM, DIM)],
-        scratch_shapes=[pltpu.VMEM((TP, IMAGES, PART, DIM), HALF), pltpu.VMEM((TP, 3, 192, DIM), HALF), pltpu.VMEM((TP, 256, DIM), HALF), pltpu.VMEM((TP, 16, DIM), HALF), pltpu.VMEM((16, DIM), HALF), pltpu.VMEM((8, DIM), WIDE), dma((3, STEPS)), dma((3, STEPS)), dma((6, 3)), dma((6, 3)), dma((7,))],
-        compiler_params=params(0),
-        cost_estimate=pl.CostEstimate(flops=60_000_000_000, bytes_accessed=50_000_000, transcendentals=12_000_000),
-        name='attn_fwd',
-    )(patches, wq, wo, pos, w1, w2, wp, patch_b, qkv_b, fc1_b, out_b, ln_scale, ln_bias)
-
-
-def mlp_slot(n, f, h2, dout, w1, w2, b1, y, dh2, dw1, dw2, db1_ref):
-    pre = dot_nn(h2, w1) + b1
-    sq = pre * pre
-    t = jnp.tanh(pre * (GELU_C + (GELU_C * GELU_A) * sq))
-    half_pre = 0.5 * pre
-    hid = (half_pre + half_pre * t).astype(HALF)
-    slope = (0.5 + 0.5 * t) + (half_pre * (1.0 - t * t)) * (GELU_C + (3.0 * GELU_C * GELU_A) * sq)
-    dhid = dot_nt(dout, w2).astype(HALF).astype(WIDE)
-    dpre = dhid * slope
-    db1_ref[f:f + 1] += col_sum(dpre)
-    dpre_h = dpre.astype(HALF)
-    part_y = dot_nn(hid, w2)
-    part_h = dot_nt(dpre_h, w1)
-    y = part_y if y is None else y + part_y
-    dh2 = part_h if dh2 is None else dh2 + part_h
-    dw1[n] += dot_tn(h2, dpre_h)
-    dw2[n] += dot_tn(dout, hid)
-    return y, dh2
-
-
-def mlp_near_kernel(d_out, w2_push, x1_ref, w1_own, w1_near, w2_own, w2_near, bias, ln_scale, ln_bias, dout_ref, y_ref, dh_ref, w2_far, keep_out, give_out, dvec_ref, db1_ref, dbuf, dw1, dw2, d_send, d_recv, w_send, w_recv, local):
-    step = pl.program_id(0)
-    me, core, others = peers()
-    own = pltpu.make_async_copy(d_out.at[pl.ds(me * IMAGES, IMAGES)], dbuf.at[0], local.at[4])
-    far = push(w2_push, w2_far.at[0], w_send.at[0], w_recv.at[0], others[2])
-    relay = push(w2_far.at[0], w2_far.at[1], w_send.at[1], w_recv.at[1], others[1])
-
-    @pl.when(step == 0)
-    def _():
-        meet(others)
-        for g in range(AHEAD):
-            for c in group_sends(d_out, dbuf, d_send, d_recv, others, g):
-                c.start()
-        own.start()
-        dw1[...] = jnp.zeros_like(dw1)
-        dw2[...] = jnp.zeros_like(dw2)
-        dvec_ref[...] = jnp.zeros_like(dvec_ref)
-        db1_ref[...] = jnp.zeros_like(db1_ref)
-        own.wait()
-
-    @pl.when(step + AHEAD < STEPS)
-    def _():
-        for c in group_sends(d_out, dbuf, d_send, d_recv, others, step + AHEAD):
-            c.start()
-
-    @pl.when(step == STEPS - AHEAD)
-    def _():
-        far.start()
-
-    x1 = jnp.concatenate([x1_ref[g] for g in range(GROUP)], axis=0)
-    xhat, inv = normalize(x1.astype(WIDE))
+    xhat, _ = normalize(x1.astype(WIDE))
     h2 = (xhat * ln_scale[1:2].astype(WIDE) + ln_bias[1:2].astype(WIDE)).astype(HALF)
     for c in group_sends(d_out, dbuf, d_send, d_recv, others, step):
         c.wait_recv()
@@ -319,59 +247,107 @@
     dvec_ref[2:3] += col_sum(dout.astype(WIDE))
     y = None
     dh2 = None
-    for f, (w1, w2) in enumerate(((w1_own, w2_own), (w1_near, w2_near))):
-        y, dh2 = mlp_slot(f, f, h2, dout, w1[...], w2[...], bias[f, 3:4].astype(WIDE), y, dh2, dw1, dw2, db1_ref)
-    for g in range(GROUP):
+    for f in range(2):
+        y, dh2 = mlp_slot(f, 0, h2, dout, w1[f], w2[f], bias, y, dh2, dw1.at[f], dw2.at[f], db1_ref)
+
+    @pl.when(step == 0)
+    def _():
+        for n in range(2):
+            early[n].wait_recv()
+            early_relay[n].start()
+        for c in early_relay:
+            c.wait_recv()
+
+    for f in range(2):
+        y, dh2 = mlp_slot(f + 2, 0, h2, dout, wa1[f], wa2[f], bias, y, dh2, dwa1.at[f], dwa2.at[f], db1_ref)
+    for g in range(FRONT):
         rows = slice(TOK * g, TOK * g + TOK)
         dout_ref[g] = dout[rows]
         y_ref[g] = y[rows]
         dh_ref[g] = dh2[rows]
 
-    @pl.when(step == STEPS - 1)
+    @pl.when(step == FRONT_STEPS - 1)
     def _():
         copies = []
         for n, out in enumerate((keep_out, give_out)):
-            copies.append(pltpu.make_async_copy(dw1.at[n], out.at[0:DIM], local.at[2 * n]))
-            copies.append(pltpu.make_async_copy(dw2.at[n], out.at[DIM:2 * DIM], local.at[2 * n + 1]))
+            copies.append(pltpu.make_async_copy(dw1.at[n], out.at[0:DIM], done.at[2 * n]))
+            copies.append(pltpu.make_async_copy(dw2.at[n], out.at[DIM:2 * DIM], done.at[2 * n + 1]))
+        copies.append(pltpu.make_async_copy(dwa1, part1_out, done.at[4]))
+        copies.append(pltpu.make_async_copy(dwa2, part2_out, done.at[5]))
         for c in copies:
             c.start()
-        far.wait_recv()
-        relay.start()
-        for g in range(STEPS):
-            for c in group_sends(d_out, dbuf, d_send, d_recv, others, g):
+        for n in range(2):
+            far[n].wait_recv()
+            relay[n].start()
+        for c in relay:
+            c.wait_recv()
+        for c in small[0] + small[1] + small[2] + tuple(near + early + early_relay + far + relay + biases):
+            c.wait_send()
+        for c in copies + flush:
+            c.wait()
+        for g in range(FRONT_STEPS):
+            for c in arrivals(g):
                 c.wait_send()
-        for c in copies:
-            c.wait()
-        far.wait_send()
-        relay.wait()
-
-
-def mlp_near(d_out, x1, w1, w1_near, w2, w2_near, bias, ln_scale, ln_bias):
+
+
+def fixed(shape):
+    return pl.BlockSpec(shape, lambda i: (0,) * len(shape), pipeline_mode=pl.Buffered(1))
+
+
+def image_spec(width, size=GROUP):
+    return pl.BlockSpec((size, TOK, width), lambda i: (i, 0, 0))
+
+
+def any_spec():
+    return pl.BlockSpec(memory_space=pl.ANY)
+
+
+def params(cid):
+    return pltpu.CompilerParams(dimension_semantics=('arbitrary',), vmem_limit_bytes=67043328, collective_id=cid, has_side_effects=True)
+
+
+def image_shape(width):
+    return jax.ShapeDtypeStruct((IMAGES, TOK, width), HALF)
+
+
+def half_shape(*shape):
+    return jax.ShapeDtypeStruct(shape, HALF)
+
+
+def wide_shape(*shape):
+    return jax.ShapeDtypeStruct(shape, WIDE)
+
+
+def vec_spec(*shape):
+    return pl.BlockSpec(shape, lambda i: (0,) * len(shape))
+
+
+def front(patches, d_out, wq, wo, pos, w1, w2, wp, patch_b, qkv_b, fc1_b, out_b, ln_scale, ln_bias):
     dma = pltpu.SemaphoreType.DMA
     wide_image = jax.ShapeDtypeStruct((IMAGES, TOK, DIM), WIDE)
     return pl.pallas_call(
-        mlp_near_kernel,
-        grid=(STEPS,),
-        in_specs=[any_spec(), any_spec(), image_spec(DIM), fixed((DIM, DIM)), pl.BlockSpec((None, DIM, DIM), lambda i: (0, 0, 0), pipeline_mode=pl.Buffered(1)), fixed((DIM, DIM)), fixed((DIM, DIM)), fixed((TP, 16, DIM)), vec_spec(2, DIM), vec_spec(2, DIM)],
-        out_specs=[image_spec(DIM)] * 3 + [any_spec()] * 3 + [vec_spec(8, DIM), vec_spec(8, DIM)],
-        out_shape=[image_shape(DIM), wide_image, wide_image, half_shape(2, DIM, DIM), wide_shape(2 * DIM, DIM), wide_shape(2 * DIM, DIM), wide_shape(8, DIM), wide_shape(8, DIM)],
-        scratch_shapes=[pltpu.VMEM((TP, IMAGES, PART, DIM), HALF), pltpu.VMEM((2, DIM, DIM), WIDE), pltpu.VMEM((2, DIM, DIM), WIDE), dma((3, STEPS)), dma((3, STEPS)), dma((2,)), dma((2,)), dma((5,))],
-        compiler_params=params(1),
-        cost_estimate=pl.CostEstimate(flops=60_000_000_000, bytes_accessed=80_000_000, transcendentals=6_000_000),
-        name='mlp_near',
-    )(d_out, w2, x1, w1, w1_near, w2, w2_near, bias, ln_scale, ln_bias)
-
-
-def mlp_far_kernel(give, x1_ref, o_ref, dout_ref, y_ref, dh_ref, w1_rest, w2_far, wop, bias, ln_scale, ln_bias, fc2_b, dvec_near, db1_near, x2_out, dx1_ref, do_ref, near_a, keep_o, near_o, keep_b, near_b, dvec_ref, db1_ref, ybuf, dw1, dw2, dwo, y_send, y_recv, y_own, g_send, g_recv, local):
+        front_kernel,
+        grid=(FRONT_STEPS,),
+        in_specs=[any_spec()] * 7 + [fixed((DIM, DIM)), vec_spec(DIM), vec_spec(3, 3, 64), vec_spec(DIM), vec_spec(DIM), vec_spec(2, DIM), vec_spec(2, DIM)],
+        out_specs=[image_spec(DIM, FRONT), image_spec(3 * DIM, FRONT)] + [image_spec(DIM, FRONT)] * 6 + [any_spec()] * 9 + [vec_spec(8, DIM), vec_spec(8, DIM)],
+        out_shape=[image_shape(DIM), image_shape(3 * DIM), image_shape(DIM), image_shape(DIM), image_shape(DIM), image_shape(DIM), wide_image, wide_image, half_shape(TP, 3, 192, DIM), half_shape(TP, 256, DIM), half_shape(TP, 16, DIM), half_shape(2, DIM, LATE), half_shape(2, LATE, DIM), wide_shape(2 * DIM, DIM), wide_shape(2 * DIM, DIM), wide_shape(2, DIM, EARLY), wide_shape(2, DIM, EARLY), wide_shape(8, DIM), wide_shape(8, DIM)],
+        scratch_shapes=[pltpu.VMEM((TP, IMAGES, PART, DIM), HALF), pltpu.VMEM((TP, IMAGES, PART, DIM), HALF), pltpu.VMEM((TP, 3, 192, DIM), HALF), pltpu.VMEM((TP, 256, DIM), HALF), pltpu.VMEM((2, DIM, DIM), HALF), pltpu.VMEM((2, DIM, DIM), HALF), pltpu.VMEM((2, DIM, EARLY), HALF), pltpu.VMEM((2, EARLY, DIM), HALF), pltpu.VMEM((TP, 16, DIM), HALF), pltpu.VMEM((16, DIM), HALF), pltpu.VMEM((8, DIM), WIDE), pltpu.VMEM((2, DIM, DIM), WIDE), pltpu.VMEM((2, DIM, DIM), WIDE), pltpu.VMEM((2, DIM, EARLY), WIDE), pltpu.VMEM((2, DIM, EARLY), WIDE), dma((3, FRONT_STEPS)), dma((3, FRONT_STEPS)), dma((3, FRONT_STEPS)), dma((3, FRONT_STEPS)), dma((8, 3)), dma((8, 3)), dma((10,)), dma((6,))],
+        compiler_params=params(0),
+        cost_estimate=pl.CostEstimate(flops=120_000_000_000, bytes_accessed=120_000_000, transcendentals=18_000_000),
+        name='front',
+    )(patches, d_out, wq, wo, pos, w1, w2, wp, patch_b, qkv_b, fc1_b, out_b, ln_scale, ln_bias)
+
+
+def mlp_far_kernel(give, part1, part2, x1_ref, o_ref, dout_ref, y_ref, dh_ref, w1_far, w2_far, wop, bias, ln_scale, ln_bias, fc2_b, dvec_near, db1_near, x2_out, dx1_ref, do_ref, near_a, keep_o, near_o, keep_b, near_b, dvec_ref, db1_ref, ybuf, dw1, dw2, dwo, y_send, y_recv, y_own, g_send, g_recv, local):
     step = pl.program_id(0)
     me, core, others = peers()
     slot = lax.rem(step, 2)
 
     def y_sends(at, group):
-        return [push(ybuf.at[at, k], x2_out.at[image_rows(me, group)], y_send.at[k - 1, at], y_recv.at[k - 1, group], others[k]) for k in (2, 3, 1)]
+        return [push(ybuf.at[at, k], x2_out.at[image_rows(me, group, GROUP)], y_send.at[k - 1, at], y_recv.at[k - 1, group], others[k]) for k in (2, 3, 1)]
 
     def y_keep(at, group):
-        return pltpu.make_async_copy(ybuf.at[at, 0], x2_out.at[image_rows(me, group)], y_own.at[at])
+        return pltpu.make_async_copy(ybuf.at[at, 0], x2_out.at[image_rows(me, group, GROUP)], y_own.at[at])
 
     def y_wait(at, group):
         for c in y_sends(at, group):
@@ -386,8 +362,14 @@
     def _():
         meet(others)
         early.start()
-        dw1[...] = jnp.zeros_like(dw1)
-        dw2[...] = jnp.zeros_like(dw2)
+        loads = [pltpu.make_async_copy(part1, dw1.at[:, :, 0:EARLY], local.at[4]), pltpu.make_async_copy(part2, dw2.at[:, :, 0:EARLY], local.at[5])]
+        for c in loads:
+            c.start()
+        for acc in (dw1, dw2):
+            for n in range(2):
+                acc[n, :, EARLY:DIM] = jnp.zeros((DIM, LATE), WIDE)
+        for c in loads:
+            c.wait()
         dwo[...] = jnp.zeros_like(dwo)
         dvec_ref[...] = dvec_near[...]
         db1_ref[...] = db1_near[...]
@@ -399,7 +381,7 @@
     y = jnp.concatenate([y_ref[g] for g in range(GROUP)], axis=0)
     dh2 = jnp.concatenate([dh_ref[g] for g in range(GROUP)], axis=0)
     for f in range(2):
-        y, dh2 = mlp_slot(f, f + 2, h2, dout, w1_rest[f + 1], w2_far[f], bias[f + 2, 3:4].astype(WIDE), y, dh2, dw1, dw2, db1_ref)
+        y, dh2 = mlp_slot(f + 2, EARLY, h2, dout, w1_far[f], w2_far[f], bias, y, dh2, dw1.at[f, :, EARLY:DIM], dw2.at[f, :, EARLY:DIM], db1_ref)
     x2 = (x1.astype(WIDE) + (y + row(fc2_b))).astype(HALF)
 
     @pl.when(step >= 2)
@@ -443,19 +425,19 @@
             y_wait(g % 2, g)
 
 
-def mlp_far(give, x1, o, dout, y, dh, w1_rest, w2_far, wop, bias, ln_scale, ln_bias, fc2_b, dvec_near, db1_near):
+def mlp_far(give, part1, part2, x1, o, dout, y, dh, w1_far, w2_far, wop, bias, ln_scale, ln_bias, fc2_b, dvec_near, db1_near):
     dma = pltpu.SemaphoreType.DMA
     return pl.pallas_call(
         mlp_far_kernel,
         grid=(STEPS,),
-        in_specs=[any_spec()] + [image_spec(DIM)] * 5 + [fixed((3, DIM, DIM)), fixed((2, DIM, DIM)), fixed((TP, 256, DIM)), fixed((TP, 16, DIM)), vec_spec(2, DIM), vec_spec(2, DIM), vec_spec(DIM), vec_spec(8, DIM), vec_spec(8, DIM)],
+        in_specs=[any_spec()] * 3 + [image_spec(DIM)] * 5 + [fixed((2, DIM, LATE)), fixed((2, LATE, DIM)), fixed((TP, 256, DIM)), fixed((TP, 16, DIM)), vec_spec(2, DIM), vec_spec(2, DIM), vec_spec(DIM), vec_spec(8, DIM), vec_spec(8, DIM)],
         out_specs=[any_spec(), image_spec(DIM), image_spec(DIM)] + [any_spec()] * 5 + [vec_spec(8, DIM), vec_spec(8, DIM)],
         out_shape=[half_shape(TP * IMAGES, PART, DIM), image_shape(DIM), image_shape(DIM), wide_shape(2 * DIM, DIM), wide_shape(192, DIM), wide_shape(192, DIM), wide_shape(PACK, DIM), wide_shape(PACK, DIM), wide_shape(8, DIM), wide_shape(8, DIM)],
-        scratch_shapes=[pltpu.VMEM((2, TP, GROUP, PART, DIM), HALF), pltpu.VMEM((2, DIM, DIM), WIDE), pltpu.VMEM((2, DIM, DIM), WIDE), pltpu.VMEM((DIM, DIM), WIDE), dma((3, 2)), dma((3, STEPS)), dma((2,)), dma((5,)), dma((5,)), dma((4,))],
+        scratch_shapes=[pltpu.VMEM((2, TP, GROUP, PART, DIM), HALF), pltpu.VMEM((2, DIM, DIM), WIDE), pltpu.VMEM((2, DIM, DIM), WIDE), pltpu.VMEM((DIM, DIM), WIDE), dma((3, 2)), dma((3, STEPS)), dma((2,)), dma((5,)), dma((5,)), dma((6,))],
         compiler_params=params(2),
         cost_estimate=pl.CostEstimate(flops=70_000_000_000, bytes_accessed=80_000_000, transcendentals=6_000_000),
         name='mlp_far',
-    )(give, x1, o, dout, y, dh, w1_rest, w2_far, wop, bias, ln_scale, ln_bias, fc2_b, dvec_near, db1_near)
+    )(give, part1, part2, x1, o, dout, y, dh, w1_far, w2_far, wop, bias, ln_scale, ln_bias, fc2_b, dvec_near, db1_near)
 
 
 def attn_bwd_kernel(keep_b, near_b, keep_a, near_a, keep_o, near_o, e_ref, qkv_ref, do_ref, dx1_ref, x_ref, wq, ln_scale, ln_bias, dvec2_ref, db1_ref, cross_out, dfc1_out, dfc2_out, dwo_out, dqkv_out, dwp_out, dpos_out, tiny_out, fetch_k, fetch_n, sums, dqkv, dwq, dwp, dpos, tiny, near_q, near_p, near_pos, far_q, far_p, far_pos, half_q, half_p, half_pos, p_send, p_recv, t_send, t_recv, n_send, n_recv, f_send, f_recv, h_send, h_recv, c_sem, o_sem, total1, total2, total3, local):
@@ -693,9 +675,8 @@
 def group_step(patches, patch_w, patch_b, pos_emb, ln_scale, ln_bias, qkv_w, qkv_b, out_w, out_b, fc1_w, fc1_b, fc2_w, fc2_b, d_out):
     wq = qkv_w.transpose(0, 2, 3, 1).reshape(3, 192, DIM)
     wo = out_w.reshape(192, DIM)
-    e, qkv, o, x1, x, wq_all, wop_all, bias_all, w1_rest, w2_near = attn_fwd(patches, wq, wo, pos_emb, fc1_w, fc2_w, patch_w, patch_b, qkv_b, fc1_b, out_b, ln_scale, ln_bias)
-    dout, y, dh, w2_far, keep_a, give_a, dvec_n, db1_n = mlp_near(d_out, x1, fc1_w, w1_rest, fc2_w, w2_near, bias_all, ln_scale, ln_bias)
-    x_two, dx1, d_o, near_a, keep_o, near_o, keep_b, near_b, dvec2, db1 = mlp_far(give_a, x1, o, dout, y, dh, w1_rest, w2_far, wop_all, bias_all, ln_scale, ln_bias, fc2_b, dvec_n, db1_n)
+    e, qkv, o, x1, x, dout, y, dh, wq_all, wop_all, bias_all, w1_far, w2_far, keep_a, give_a, part1, part2, dvec_n, db1_n = front(patches, d_out, wq, wo, pos_emb, fc1_w, fc2_w, patch_w, patch_b, qkv_b, fc1_b, out_b, ln_scale, ln_bias)
+    x_two, dx1, d_o, near_a, keep_o, near_o, keep_b, near_b, dvec2, db1 = mlp_far(give_a, part1, part2, x1, o, dout, y, dh, w1_far, w2_far, wop_all, bias_all, ln_scale, ln_bias, fc2_b, dvec_n, db1_n)
     _, d_fc1_w, d_fc2_w, d_out_w, d_qkv, d_patch_w, d_pos, tiny = attn_bwd(keep_b, near_b, keep_a, near_a, keep_o, near_o, e, qkv, d_o, dx1, x, wq_all, ln_scale, ln_bias, dvec2, db1)
     x_two, d_fc1_w, d_fc2_w, d_out_w, d_qkv, d_patch_w, d_pos, d_patch_b, d_ln_scale, d_ln_bias, d_qkv_b, d_out_b, d_fc1_b, d_fc2_b = finish(x_two, d_fc1_w, d_fc2_w, d_out_w, d_qkv.reshape(576, DIM), d_patch_w, d_pos, tiny)
     d_qkv_w = d_qkv.reshape(3, 3, 64, DIM).transpose(0, 3, 1, 2)

time: 547 us -> 519 us (0.949); the launches traced: 540 us -> 519 us
  Pallas kernels: 539 us -> 518 us
    pallas_call x3 -> x2, Pallas kernels: 341 us -> 321 us  [the longest x1 233 us: front(): pl.pallas_call(front_kernel, grid=(FRONT_STEPS,), in_specs=[any_spec()] *...]
where the time goes in v5:
time: 519 us
  Pallas kernels  518 us (100%)
    pallas_call x1, Pallas kernels, front(): pl.pallas_call(front_kernel, grid=(FRONT_STEPS,), in_specs=[any_spec()] *...  233 us
    pallas_call x1, Pallas kernels, attn_bwd(): pl.pallas_call(attn_bwd_kernel, grid=(STEPS,), in_specs=[any_spec()] * 6...  188 us
    pallas_call x1, Pallas kernels, mlp_far(): pl.pallas_call(mlp_far_kernel, grid=(STEPS,), in_specs=[any_spec()] * 3 +...  88.5 us

profile of v5, /device:TPU:0, one launch (start us, length us, event | category | flops | bytes accessed | tf_op | source)
XLA Modules:
  0.0 518.6 jit_solution(5249477083430853207)
XLA Ops:
  0.6 232.8 %front.1 = (bf16[16,256,768]{2,1,0:T(8,128)(2,1)}, bf16[16,256,2304]{2,1,0:T(8,128)(2,1)}, bf16[16,256,768]{2,1,0:T(8,128)(2,1)}, bf16[16,256,768]{2,1,0:T(8,128...) custom-call(bf16[64,64,768]{2,1,0:T(8,128)(2,1)} %patches.1, ...), custom_call_target="tpu_custom_call" | custom-call | flops 120000004096 | bytes 120000000 | tf_op jit(solution)/shard_map/front/pallas_call | solution.py:328
  233.5 88.5 %mlp_far.1 = (bf16[64,64,768]{2,1,0:T(8,128)(2,1)}, bf16[16,256,768]{2,1,0:T(8,128)(2,1)}, bf16[16,256,768]{2,1,0:T(8,128)(2,1)}, f32[1536,768]{1,0:T(8,128)}, f...) custom-call(f32[1536,768]{1,0:T(8,128)} %get-tuple-element.64.give, ...), custom_call_target="tpu_custom_call" | custom-call | flops 70000001024 | bytes 80000000 | tf_op jit(solution)/shard_map/mlp_far/pallas_call | solution.py:430
  322.0 187.6 %attn_bwd.1 = (f32[1728,768]{1,0:T(8,128)}, bf16[768,768]{1,0:T(8,128)(2,1)}, bf16[768,768]{1,0:T(8,128)(2,1)}, bf16[192,768]{1,0:T(8,128)(2,1)}, bf16[3,192,768...) custom-call(f32[1728,768]{1,0:T(8,128)} %get-tuple-element.79.keep_b, ...), custom_call_target="tpu_custom_call" | custom-call | flops 99999997952 | bytes 80000000 | tf_op jit(solution)/shard_map/attn_bwd/pallas_call | solution.py:626
  509.7 8.8 %finish.1 = (bf16[64,64,768]{2,1,0:T(8,128)(2,1)}, bf16[768,768]{1,0:T(8,128)(2,1)}, bf16[768,768]{1,0:T(8,128)(2,1)}, bf16[192,768]{1,0:T(8,128)(2,1)}, bf16[57...) custom-call(bf16[64,64,768]{2,1,0:T(8,128)(2,1)} %get-tuple-element., ...), custom_call_target="tpu_custom_call" | custom-call | tf_op jit(solution)/shard_map/finish/pallas_call | solution.py:664

commit v6 on v5

--- a/solution.py
+++ b/solution.py
@@ -127,12 +127,15 @@
     part_h = dot_nt(dpre_h, w1)
     y = part_y if y is None else y + part_y
     dh2 = part_h if dh2 is None else dh2 + part_h
-    dw1[...] += dot_tn(h2, dpre_h)
-    dw2[...] += dot_tn(dout, hid)
-    return y, dh2
-
-
-def front_kernel(patches, d_out, wq_own, wo_own, pos_own, w1_own, w2_own, wp, patch_b, qkv_b, fc1_b, out_b, ln_scale, ln_bias, e_ref, qkv_ref, o_ref, x1_ref, x_ref, dout_ref, y_ref, dh_ref, wq_out, wop_out, bias_out, w1_far, w2_far, keep_out, give_out, part1_out, part2_out, dvec_ref, db1_ref, xbuf, dbuf, wq, wop, w1, w2, wa1, wa2, bias, bias_own, bqkv, dw1, dw2, dwa1, dwa2, x_send, x_recv, d_send, d_recv, w_send, w_recv, local, done):
+
+    def grads():
+        dw1[...] += dot_tn(h2, dpre_h)
+        dw2[...] += dot_tn(dout, hid)
+
+    return y, dh2, grads
+
+
+def front_kernel(patches, d_out, wq_own, wo_own, pos_own, w1_own, w2_own, wp, patch_b, qkv_b, fc1_b, out_b, ln_scale, ln_bias, e_ref, qkv_ref, o_ref, x1_ref, x_ref, lse_ref, dout_ref, y_ref, dh_ref, wq_out, wop_out, bias_out, w1_far, w2_far, keep_out, give_out, part1_out, part2_out, dvec_ref, db1_ref, xbuf, dbuf, wq, wop, w1, w2, wa1, wa2, bias, bias_own, bqkv, dw1, dw2, dwa1, dwa2, x_send, x_recv, d_send, d_recv, w_send, w_recv, local, done):
     step = pl.program_id(0)
     me, core, others = peers()
     small = []
@@ -142,8 +145,8 @@
     near = [push(w1_own, w1.at[1], w_send.at[3, 0], w_recv.at[3, 0], others[1]), push(w2_own, w2.at[1], w_send.at[4, 0], w_recv.at[4, 0], others[1])]
     early = [push(w1_own.at[:, 0:EARLY], wa1.at[0], w_send.at[6, 0], w_recv.at[6, 0], others[2]), push(w2_own.at[0:EARLY], wa2.at[0], w_send.at[7, 0], w_recv.at[7, 0], others[2])]
     early_relay = [push(wa1.at[0], wa1.at[1], w_send.at[6, 1], w_recv.at[6, 1], others[1]), push(wa2.at[0], wa2.at[1], w_send.at[7, 1], w_recv.at[7, 1], others[1])]
-    far = [push(w1_own.at[:, EARLY:DIM], w1_far.at[0], w_send.at[3, 1], w_recv.at[3, 1], others[2]), push(w2_own.at[EARLY:DIM], w2_far.at[0], w_send.at[4, 1], w_recv.at[4, 1], others[2])]
-    relay = [push(w1_far.at[0], w1_far.at[1], w_send.at[3, 2], w_recv.at[3, 2], others[1]), push(w2_far.at[0], w2_far.at[1], w_send.at[4, 2], w_recv.at[4, 2], others[1])]
+    far = [push(w1_own.at[:, EARLY:DIM], w1_far.at[0], w_send.at[3, 1], w_recv.at[3, 1], others[2]), push(w2_own.at[EARLY:DIM - 256], w2_far.at[0, 0:256], w_send.at[4, 1], w_recv.at[4, 1], others[2]), push(w2_own.at[DIM - 256:DIM], w2_far.at[0, 256:512], w_send.at[8, 0], w_recv.at[8, 0], others[2])]
+    relay = [push(w1_far.at[0], w1_far.at[1], w_send.at[3, 2], w_recv.at[3, 2], others[1]), push(w2_far.at[0, 0:256], w2_far.at[1, 0:256], w_send.at[4, 2], w_recv.at[4, 2], others[1]), push(w2_far.at[0, 256:512], w2_far.at[1, 256:512], w_send.at[8, 1], w_recv.at[8, 1], others[1])]
     biases = [push(bias_own, bias.at[k], w_send.at[5, k - 1], w_recv.at[5, k - 1], others[k]) for k in range(1, TP)]
     own = [pltpu.make_async_copy(wq_own, wq.at[0], local.at[0]), pltpu.make_async_copy(wo_own, wop.at[0, 0:192], local.at[1]), pltpu.make_async_copy(pos_own, wop.at[0, 192:256], local.at[2]), pltpu.make_async_copy(patches.at[pl.ds(me * IMAGES, IMAGES)], xbuf.at[0], local.at[3]), pltpu.make_async_copy(d_out.at[pl.ds(me * IMAGES, IMAGES)], dbuf.at[0], local.at[7]), pltpu.make_async_copy(w1_own, w1.at[0], local.at[8]), pltpu.make_async_copy(w2_own, w2.at[0], local.at[9])]
     flush = [pltpu.make_async_copy(wq, wq_out, local.at[4]), pltpu.make_async_copy(wop, wop_out, local.at[5]), pltpu.make_async_copy(bias, bias_out, local.at[6])]
@@ -200,8 +203,8 @@
 
     @pl.when(step == FRONT_STEPS - AHEAD)
     def _():
-        far[0].start()
-        far[1].start()
+        for c in far:
+            c.start()
 
     for c in group_sends(patches, xbuf, x_send, x_recv, others, step):
         c.wait_recv()
@@ -226,12 +229,13 @@
             v = qkv_ref[g, :, 2 * DIM + 128 * pr:2 * DIM + 128 * pr + 128]
             probs = []
             for j in range(2):
-                s = dot_nt(mask_half(q, j), k)
-                m = jnp.max(s, axis=-1, keepdims=True)
+                s = dot_nt(k, mask_half(q, j))
+                m = jnp.max(s, axis=0, keepdims=True)
                 e = jnp.exp2((s - m) * EXP_SCALE)
-                l = jnp.sum(e, axis=-1, keepdims=True)
+                l = jnp.sum(e, axis=0, keepdims=True)
+                lse_ref[g, 2 * pr + j:2 * pr + j + 1] = m * EXP_SCALE + jnp.log2(l)
                 probs.append((e * (1.0 / l)).astype(HALF))
-            pv = dot_nn(jnp.concatenate(probs, axis=1), jnp.concatenate([mask_half(v, 0), mask_half(v, 1)], axis=0))
+            pv = dot_tn(jnp.concatenate(probs, axis=0), jnp.concatenate([mask_half(v, 0), mask_half(v, 1)], axis=0))
             o_ref[g, :, 128 * pr:128 * pr + 128] = pv.astype(HALF)
     o = jnp.concatenate([o_ref[g] for g in range(FRONT)], axis=0)
     e_f = jnp.concatenate([e_ref[g] for g in range(FRONT)], axis=0).astype(WIDE)
@@ -248,7 +252,8 @@
     y = None
     dh2 = None
     for f in range(2):
-        y, dh2 = mlp_slot(f, 0, h2, dout, w1[f], w2[f], bias, y, dh2, dw1.at[f], dw2.at[f], db1_ref)
+        y, dh2, grads = mlp_slot(f, 0, h2, dout, w1[f], w2[f], bias, y, dh2, dw1.at[f], dw2.at[f], db1_ref)
+        grads()
 
     @pl.when(step == 0)
     def _():
@@ -259,7 +264,8 @@
             c.wait_recv()
 
     for f in range(2):
-        y, dh2 = mlp_slot(f + 2, 0, h2, dout, wa1[f], wa2[f], bias, y, dh2, dwa1.at[f], dwa2.at[f], db1_ref)
+        y, dh2, grads = mlp_slot(f + 2, 0, h2, dout, wa1[f], wa2[f], bias, y, dh2, dwa1.at[f], dwa2.at[f], db1_ref)
+        grads()
     for g in range(FRONT):
         rows = slice(TOK * g, TOK * g + TOK)
         dout_ref[g] = dout[rows]
@@ -276,7 +282,7 @@
         copies.append(pltpu.make_async_copy(dwa2, part2_out, done.at[5]))
         for c in copies:
             c.start()
-        for n in range(2):
+        for n in range(3):
             far[n].wait_recv()
             relay[n].start()
         for c in relay:
@@ -298,6 +304,10 @@
     return pl.BlockSpec((size, TOK, width), lambda i: (i, 0, 0))
 
 
+def lse_spec(size=GROUP):
+    return pl.BlockSpec((size, 16, TOK), lambda i: (i, 0, 0))
+
+
 def any_spec():
     return pl.BlockSpec(memory_space=pl.ANY)
 
@@ -329,16 +339,16 @@
         front_kernel,
         grid=(FRONT_STEPS,),
         in_specs=[any_spec()] * 7 + [fixed((DIM, DIM)), vec_spec(DIM), vec_spec(3, 3, 64), vec_spec(DIM), vec_spec(DIM), vec_spec(2, DIM), vec_spec(2, DIM)],
-        out_specs=[image_spec(DIM, FRONT), image_spec(3 * DIM, FRONT)] + [image_spec(DIM, FRONT)] * 6 + [any_spec()] * 9 + [vec_spec(8, DIM), vec_spec(8, DIM)],
-        out_shape=[image_shape(DIM), image_shape(3 * DIM), image_shape(DIM), image_shape(DIM), image_shape(DIM), image_shape(DIM), wide_image, wide_image, half_shape(TP, 3, 192, DIM), half_shape(TP, 256, DIM), half_shape(TP, 16, DIM), half_shape(2, DIM, LATE), half_shape(2, LATE, DIM), wide_shape(2 * DIM, DIM), wide_shape(2 * DIM, DIM), wide_shape(2, DIM, EARLY), wide_shape(2, DIM, EARLY), wide_shape(8, DIM), wide_shape(8, DIM)],
-        scratch_shapes=[pltpu.VMEM((TP, IMAGES, PART, DIM), HALF), pltpu.VMEM((TP, IMAGES, PART, DIM), HALF), pltpu.VMEM((TP, 3, 192, DIM), HALF), pltpu.VMEM((TP, 256, DIM), HALF), pltpu.VMEM((2, DIM, DIM), HALF), pltpu.VMEM((2, DIM, DIM), HALF), pltpu.VMEM((2, DIM, EARLY), HALF), pltpu.VMEM((2, EARLY, DIM), HALF), pltpu.VMEM((TP, 16, DIM), HALF), pltpu.VMEM((16, DIM), HALF), pltpu.VMEM((8, DIM), WIDE), pltpu.VMEM((2, DIM, DIM), WIDE), pltpu.VMEM((2, DIM, DIM), WIDE), pltpu.VMEM((2, DIM, EARLY), WIDE), pltpu.VMEM((2, DIM, EARLY), WIDE), dma((3, FRONT_STEPS)), dma((3, FRONT_STEPS)), dma((3, FRONT_STEPS)), dma((3, FRONT_STEPS)), dma((8, 3)), dma((8, 3)), dma((10,)), dma((6,))],
+        out_specs=[image_spec(DIM, FRONT), image_spec(3 * DIM, FRONT)] + [image_spec(DIM, FRONT)] * 3 + [lse_spec(FRONT)] + [image_spec(DIM, FRONT)] * 3 + [any_spec()] * 9 + [vec_spec(8, DIM), vec_spec(8, DIM)],
+        out_shape=[image_shape(DIM), image_shape(3 * DIM), image_shape(DIM), image_shape(DIM), image_shape(DIM), wide_shape(IMAGES, 16, TOK), image_shape(DIM), wide_image, wide_image, half_shape(TP, 3, 192, DIM), half_shape(TP, 256, DIM), half_shape(TP, 16, DIM), half_shape(2, DIM, LATE), half_shape(2, LATE, DIM), wide_shape(2 * DIM, DIM), wide_shape(2 * DIM, DIM), wide_shape(2, DIM, EARLY), wide_shape(2, DIM, EARLY), wide_shape(8, DIM), wide_shape(8, DIM)],
+        scratch_shapes=[pltpu.VMEM((TP, IMAGES, PART, DIM), HALF), pltpu.VMEM((TP, IMAGES, PART, DIM), HALF), pltpu.VMEM((TP, 3, 192, DIM), HALF), pltpu.VMEM((TP, 256, DIM), HALF), pltpu.VMEM((2, DIM, DIM), HALF), pltpu.VMEM((2, DIM, DIM), HALF), pltpu.VMEM((2, DIM, EARLY), HALF), pltpu.VMEM((2, EARLY, DIM), HALF), pltpu.VMEM((TP, 16, DIM), HALF), pltpu.VMEM((16, DIM), HALF), pltpu.VMEM((8, DIM), WIDE), pltpu.VMEM((2, DIM, DIM), WIDE), pltpu.VMEM((2, DIM, DIM), WIDE), pltpu.VMEM((2, DIM, EARLY), WIDE), pltpu.VMEM((2, DIM, EARLY), WIDE), dma((3, FRONT_STEPS)), dma((3, FRONT_STEPS)), dma((3, FRONT_STEPS)), dma((3, FRONT_STEPS)), dma((9, 3)), dma((9, 3)), dma((10,)), dma((6,))],
         compiler_params=params(0),
         cost_estimate=pl.CostEstimate(flops=120_000_000_000, bytes_accessed=120_000_000, transcendentals=18_000_000),
         name='front',
     )(patches, d_out, wq, wo, pos, w1, w2, wp, patch_b, qkv_b, fc1_b, out_b, ln_scale, ln_bias)
 
 
-def mlp_far_kernel(give, part1, part2, x1_ref, o_ref, dout_ref, y_ref, dh_ref, w1_far, w2_far, wop, bias, ln_scale, ln_bias, fc2_b, dvec_near, db1_near, x2_out, dx1_ref, do_ref, near_a, keep_o, near_o, keep_b, near_b, dvec_ref, db1_ref, ybuf, dw1, dw2, dwo, y_send, y_recv, y_own, g_send, g_recv, local):
+def mlp_far_kernel(give, part1, part2, x1_ref, o_ref, dout_ref, y_ref, dh_ref, w1_far, w2_far, bias, ln_scale, ln_bias, fc2_b, dvec_near, db1_near, x2_out, dx1_ref, near_a, keep_o, near_o, keep_b, near_b, dvec_ref, db1_ref, ybuf, stage, dw1, dw2, dwo, y_send, y_recv, y_own, g_send, g_recv, local):
     step = pl.program_id(0)
     me, core, others = peers()
     slot = lax.rem(step, 2)
@@ -354,22 +364,25 @@
             c.wait_send()
         y_keep(at, group).wait()
 
-    early = push(give, near_a, g_send.at[0], g_recv.at[0], others[1])
-    grads = [push(dw1.at[1], near_b.at[0:DIM], g_send.at[1], g_recv.at[1], others[1]), push(dw2.at[1], near_b.at[DIM:2 * DIM], g_send.at[2], g_recv.at[2], others[1]), push(dwo.at[576:768], near_b.at[2 * DIM:PACK], g_send.at[3], g_recv.at[3], others[1]), push(dwo.at[192:384], near_o, g_send.at[4], g_recv.at[4], others[1])]
-    keeps = [pltpu.make_async_copy(dw1.at[0], keep_b.at[0:DIM], local.at[0]), pltpu.make_async_copy(dw2.at[0], keep_b.at[DIM:2 * DIM], local.at[1]), pltpu.make_async_copy(dwo.at[384:576], keep_b.at[2 * DIM:PACK], local.at[2]), pltpu.make_async_copy(dwo.at[0:192], keep_o, local.at[3])]
+    early = [push(give, near_a, g_send.at[0], g_recv.at[0], others[1]), push(part1.at[1], near_b.at[0:DIM, 0:EARLY], g_send.at[5], g_recv.at[5], others[1]), push(part2.at[1], near_b.at[DIM:2 * DIM, 0:EARLY], g_send.at[6], g_recv.at[6], others[1])]
+    grads = [push(dw1.at[1], near_b.at[0:DIM, EARLY:DIM], g_send.at[1], g_recv.at[1], others[1]), push(dw2.at[1], near_b.at[DIM:2 * DIM, EARLY:DIM], g_send.at[2], g_recv.at[2], others[1]), push(dwo.at[576:768], near_b.at[2 * DIM:PACK], g_send.at[3], g_recv.at[3], others[1]), push(dwo.at[192:384], near_o, g_send.at[4], g_recv.at[4], others[1])]
+    keeps = [pltpu.make_async_copy(dw1.at[0], keep_b.at[0:DIM, EARLY:DIM], local.at[0]), pltpu.make_async_copy(dw2.at[0], keep_b.at[DIM:2 * DIM, EARLY:DIM], local.at[1]), pltpu.make_async_copy(dwo.at[384:576], keep_b.at[2 * DIM:PACK], local.at[2]), pltpu.make_async_copy(dwo.at[0:192], keep_o, local.at[3])]
+    moves = [pltpu.make_async_copy(stage.at[0], keep_b.at[0:DIM, 0:EARLY], local.at[6]), pltpu.make_async_copy(stage.at[1], keep_b.at[DIM:2 * DIM, 0:EARLY], local.at[7])]
 
     @pl.when(step == 0)
     def _():
         meet(others)
-        early.start()
-        loads = [pltpu.make_async_copy(part1, dw1.at[:, :, 0:EARLY], local.at[4]), pltpu.make_async_copy(part2, dw2.at[:, :, 0:EARLY], local.at[5])]
+        for c in early:
+            c.start()
+        loads = [pltpu.make_async_copy(part1.at[0], stage.at[0], local.at[4]), pltpu.make_async_copy(part2.at[0], stage.at[1], local.at[5])]
         for c in loads:
             c.start()
-        for acc in (dw1, dw2):
-            for n in range(2):
-                acc[n, :, EARLY:DIM] = jnp.zeros((DIM, LATE), WIDE)
+        dw1[...] = jnp.zeros_like(dw1)
+        dw2[...] = jnp.zeros_like(dw2)
         for c in loads:
             c.wait()
+        for c in moves:
+            c.start()
         dwo[...] = jnp.zeros_like(dwo)
         dvec_ref[...] = dvec_near[...]
         db1_ref[...] = db1_near[...]
@@ -380,8 +393,10 @@
     h2 = (xhat * ln_scale[1:2].astype(WIDE) + ln_bias[1:2].astype(WIDE)).astype(HALF)
     y = jnp.concatenate([y_ref[g] for g in range(GROUP)], axis=0)
     dh2 = jnp.concatenate([dh_ref[g] for g in range(GROUP)], axis=0)
+    weight_grads = []
     for f in range(2):
-        y, dh2 = mlp_slot(f + 2, EARLY, h2, dout, w1_far[f], w2_far[f], bias, y, dh2, dw1.at[f, :, EARLY:DIM], dw2.at[f, :, EARLY:DIM], db1_ref)
+        y, dh2, late = mlp_slot(f + 2, EARLY, h2, dout, w1_far[f], w2_far[f], bias, y, dh2, dw1.at[f], dw2.at[f], db1_ref)
+        weight_grads.append(late)
     x2 = (x1.astype(WIDE) + (y + row(fc2_b))).astype(HALF)
 
     @pl.when(step >= 2)
@@ -391,6 +406,18 @@
     for g in range(GROUP):
         for k in range(TP):
             ybuf[slot, k, g] = x2[TOK * g + PART * k:TOK * g + PART * k + PART]
+    weight_grads[1]()
+
+    for c in y_sends(slot, step):
+        c.start()
+    y_keep(slot, step).start()
+
+    @pl.when(step == STEPS - 1)
+    def _():
+        grads[0].start()
+        grads[1].start()
+
+    weight_grads[0]()
     dh2 = dh2.astype(HALF).astype(WIDE)
     xhat, inv = normalize(x1.astype(WIDE))
     dout_f = dout.astype(WIDE)
@@ -398,25 +425,19 @@
     dvec_ref[0:1] += col_sum(dh2 * xhat)
     dvec_ref[1:2] += col_sum(dh2)
     dvec_ref[3:4] += col_sum(dx1.astype(WIDE))
-    d_o = dot_nt(dx1, jnp.concatenate([wop[k, 0:192] for k in range(TP)], axis=0)).astype(HALF)
     for g in range(GROUP):
         dx1_ref[g] = dx1[TOK * g:TOK * g + TOK]
-        do_ref[g] = d_o[TOK * g:TOK * g + TOK]
     o = jnp.concatenate([o_ref[g] for g in range(GROUP)], axis=0)
     dwo[...] += dot_tn(o, dx1)
 
-    for c in y_sends(slot, step):
-        c.start()
-    y_keep(slot, step).start()
 
     @pl.when(step == STEPS - 1)
     def _():
-        for c in grads + keeps:
-            c.start()
-        for c in keeps:
-            c.wait()
-        early.wait()
-        for c in grads:
+        for c in grads[2:] + keeps:
+            c.start()
+        for c in keeps + moves:
+            c.wait()
+        for c in early + grads:
             c.wait()
         for g in range(STEPS):
             for c in y_sends(g % 2, g):
@@ -425,22 +446,22 @@
             y_wait(g % 2, g)
 
 
-def mlp_far(give, part1, part2, x1, o, dout, y, dh, w1_far, w2_far, wop, bias, ln_scale, ln_bias, fc2_b, dvec_near, db1_near):
+def mlp_far(give, part1, part2, x1, o, dout, y, dh, w1_far, w2_far, bias, ln_scale, ln_bias, fc2_b, dvec_near, db1_near):
     dma = pltpu.SemaphoreType.DMA
     return pl.pallas_call(
         mlp_far_kernel,
         grid=(STEPS,),
-        in_specs=[any_spec()] * 3 + [image_spec(DIM)] * 5 + [fixed((2, DIM, LATE)), fixed((2, LATE, DIM)), fixed((TP, 256, DIM)), fixed((TP, 16, DIM)), vec_spec(2, DIM), vec_spec(2, DIM), vec_spec(DIM), vec_spec(8, DIM), vec_spec(8, DIM)],
-        out_specs=[any_spec(), image_spec(DIM), image_spec(DIM)] + [any_spec()] * 5 + [vec_spec(8, DIM), vec_spec(8, DIM)],
-        out_shape=[half_shape(TP * IMAGES, PART, DIM), image_shape(DIM), image_shape(DIM), wide_shape(2 * DIM, DIM), wide_shape(192, DIM), wide_shape(192, DIM), wide_shape(PACK, DIM), wide_shape(PACK, DIM), wide_shape(8, DIM), wide_shape(8, DIM)],
-        scratch_shapes=[pltpu.VMEM((2, TP, GROUP, PART, DIM), HALF), pltpu.VMEM((2, DIM, DIM), WIDE), pltpu.VMEM((2, DIM, DIM), WIDE), pltpu.VMEM((DIM, DIM), WIDE), dma((3, 2)), dma((3, STEPS)), dma((2,)), dma((5,)), dma((5,)), dma((6,))],
+        in_specs=[any_spec()] * 3 + [image_spec(DIM)] * 5 + [fixed((2, DIM, LATE)), fixed((2, LATE, DIM)), fixed((TP, 16, DIM)), vec_spec(2, DIM), vec_spec(2, DIM), vec_spec(DIM), vec_spec(8, DIM), vec_spec(8, DIM)],
+        out_specs=[any_spec(), image_spec(DIM)] + [any_spec()] * 5 + [vec_spec(8, DIM), vec_spec(8, DIM)],
+        out_shape=[half_shape(TP * IMAGES, PART, DIM), image_shape(DIM), wide_shape(2 * DIM, DIM), wide_shape(192, DIM), wide_shape(192, DIM), wide_shape(PACK, DIM), wide_shape(PACK, DIM), wide_shape(8, DIM), wide_shape(8, DIM)],
+        scratch_shapes=[pltpu.VMEM((2, TP, GROUP, PART, DIM), HALF), pltpu.VMEM((2, DIM, EARLY), WIDE), pltpu.VMEM((2, DIM, LATE), WIDE), pltpu.VMEM((2, DIM, LATE), WIDE), pltpu.VMEM((DIM, DIM), WIDE), dma((3, 2)), dma((3, STEPS)), dma((2,)), dma((7,)), dma((7,)), dma((8,))],
         compiler_params=params(2),
         cost_estimate=pl.CostEstimate(flops=70_000_000_000, bytes_accessed=80_000_000, transcendentals=6_000_000),
         name='mlp_far',
-    )(give, part1, part2, x1, o, dout, y, dh, w1_far, w2_far, wop, bias, ln_scale, ln_bias, fc2_b, dvec_near, db1_near)
-
-
-def attn_bwd_kernel(keep_b, near_b, keep_a, near_a, keep_o, near_o, e_ref, qkv_ref, do_ref, dx1_ref, x_ref, wq, ln_scale, ln_bias, dvec2_ref, db1_ref, cross_out, dfc1_out, dfc2_out, dwo_out, dqkv_out, dwp_out, dpos_out, tiny_out, fetch_k, fetch_n, sums, dqkv, dwq, dwp, dpos, tiny, near_q, near_p, near_pos, far_q, far_p, far_pos, half_q, half_p, half_pos, p_send, p_recv, t_send, t_recv, n_send, n_recv, f_send, f_recv, h_send, h_recv, c_sem, o_sem, total1, total2, total3, local):
+    )(give, part1, part2, x1, o, dout, y, dh, w1_far, w2_far, bias, ln_scale, ln_bias, fc2_b, dvec_near, db1_near)
+
+
+def attn_bwd_kernel(keep_b, near_b, keep_a, near_a, keep_o, near_o, e_ref, qkv_ref, lse_ref, dx1_ref, x_ref, wq_all, wop, ln_scale, ln_bias, dvec2_ref, db1_ref, cross_out, dfc1_out, dfc2_out, dwo_out, dqkv_out, dwp_out, dpos_out, tiny_out, fetch_k, fetch_n, sums, do_buf, wq, dqkv, dwq, dwp, dpos, tiny, near_q, near_p, near_pos, far_q, far_p, far_pos, half_q, half_p, half_pos, p_send, p_recv, t_send, t_recv, n_send, n_recv, f_send, f_recv, h_send, h_recv, c_sem, o_sem, total1, total2, total3, fq_send, fq_recv, local):
     step = pl.program_id(0)
     me, core, others = peers()
     pairs = [push(sums.at[n], cross_out.at[CHUNK * n:CHUNK * n + CHUNK], p_send.at[n], p_recv.at[n], others[2]) for n in range(CHUNKS)]
@@ -478,6 +499,15 @@
     def _():
         push(sums.at[step], cross_out.at[pl.ds(step * CHUNK, CHUNK)], p_send.at[step], p_recv.at[step], others[2]).start()
 
+    @pl.when(step == 0)
+    def _():
+        wq_copy = pltpu.make_async_copy(wq_all, wq, local.at[4])
+        wq_copy.start()
+        wq_copy.wait()
+
+    wo = jnp.concatenate([wop[k, 0:192] for k in range(TP)], axis=0)
+    for g in range(GROUP):
+        do_buf[g] = dot_nt(dx1_ref[g], wo).astype(HALF)
     for g in range(GROUP):
         rows = slice(TOK * g, TOK * g + TOK)
         for pr in range(PAIRS):
@@ -485,15 +515,12 @@
             q = qkv_ref[g, :, 128 * pr:128 * pr + 128]
             k = qkv_ref[g, :, DIM + 128 * pr:DIM + 128 * pr + 128]
             v = qkv_ref[g, :, 2 * DIM + 128 * pr:2 * DIM + 128 * pr + 128]
-            d_o = do_ref[g, :, 128 * pr:128 * pr + 128]
+            d_o = do_buf[g, :, 128 * pr:128 * pr + 128]
             probs = []
             dscores = []
             for j in range(2):
                 s = dot_nt(k, mask_half(q, j))
-                m = jnp.max(s, axis=0, keepdims=True)
-                e = jnp.exp2((s - m) * EXP_SCALE)
-                l = jnp.sum(e, axis=0, keepdims=True)
-                p = e * (1.0 / l)
+                p = jnp.exp2(s * EXP_SCALE - lse_ref[g, 2 * pr + j:2 * pr + j + 1])
                 dp = dot_nt(v, mask_half(d_o, j)).astype(HALF).astype(WIDE)
                 delta = jnp.sum(dp * p, axis=0, keepdims=True)
                 ds = (p * ((dp - delta) * 0.125)).astype(HALF)
@@ -543,7 +570,8 @@
         my_half = pl.ds(384 * core, 384)
         near = [push(dwq.at[3], near_q.at[1], n_send.at[0], n_recv.at[0], others[1]), push(dwq.at[1], near_q.at[0], n_send.at[1], n_recv.at[1], others[1]), push(dpos.at[3 * PART:4 * PART], near_pos.at[1], n_send.at[2], n_recv.at[2], others[1]), push(dpos.at[PART:2 * PART], near_pos.at[0], n_send.at[3], n_recv.at[3], others[1]), push(dwp.at[other_half], near_p, n_send.at[4], n_recv.at[4], others[1])]
         tinies = [push(tiny, tiny_out.at[k - 1], t_send.at[k - 1], t_recv.at[k - 1], others[k]) for k in range(1, TP)]
-        far = [push(dwq.at[2], far_q, f_send.at[0], f_recv.at[0], others[2]), push(dwp.at[far_quarter], far_p, f_send.at[1], f_recv.at[1], others[2]), push(dpos.at[2 * PART:3 * PART], far_pos, f_send.at[2], f_recv.at[2], others[2])]
+        far = [None, push(dwp.at[far_quarter], far_p, f_send.at[1], f_recv.at[1], others[2]), push(dpos.at[2 * PART:3 * PART], far_pos, f_send.at[2], f_recv.at[2], others[2])]
+        far_qs = [push(dwq.at[2, s], far_q.at[s], fq_send.at[s], fq_recv.at[s], others[2]) for s in range(3)]
         near[4].start()
         near[0].start()
         for c in near[1:4] + tinies:
@@ -554,7 +582,8 @@
         near[0].wait_recv()
         for s in range(3):
             dwq[2, s] += near_q[1, s]
-        far[0].start()
+        for c in far_qs:
+            c.start()
         near[2].wait_recv()
         dpos[2 * PART:3 * PART] += near_pos[1]
         far[2].start()
@@ -590,8 +619,8 @@
         total3[...] = total(keep_o, near_o, cross_out.at[2 * DIM:PACK], 192).astype(HALF)
         outs.append(pltpu.make_async_copy(total3, dwo_out, o_sem.at[2]))
         outs[2].start()
-        far[0].wait_recv()
         for s in range(3):
+            far_qs[s].wait_recv()
             half_q[s] = ((dwq[0, s] + near_q[0, s]) + far_q[s]).astype(HALF)
         q_copy = pltpu.make_async_copy(half_q, dqkv_out, local.at[0])
         q_copy.start()
@@ -608,7 +637,8 @@
             c.wait_send()
         for c in tinies:
             c.wait()
-        far[0].wait_send()
+        for c in far_qs:
+            c.wait_send()
         far[2].wait_send()
         tiny_copy = pltpu.make_async_copy(tiny, tiny_out.at[3], local.at[3])
         tiny_copy.start()
@@ -621,19 +651,19 @@
         swap.wait()
 
 
-def attn_bwd(keep_b, near_b, keep_a, near_a, keep_o, near_o, e, qkv, d_o, dx1, x, wq, ln_scale, ln_bias, dvec2, db1):
+def attn_bwd(keep_b, near_b, keep_a, near_a, keep_o, near_o, e, qkv, lse, dx1, x, wq, wop, ln_scale, ln_bias, dvec2, db1):
     dma = pltpu.SemaphoreType.DMA
     return pl.pallas_call(
         attn_bwd_kernel,
         grid=(STEPS,),
-        in_specs=[any_spec()] * 6 + [image_spec(DIM), image_spec(3 * DIM), image_spec(DIM), image_spec(DIM), image_spec(DIM), fixed((TP, 3, 192, DIM)), vec_spec(2, DIM), vec_spec(2, DIM), vec_spec(8, DIM), vec_spec(8, DIM)],
+        in_specs=[any_spec()] * 6 + [image_spec(DIM), image_spec(3 * DIM), lse_spec(), image_spec(DIM), image_spec(DIM), any_spec(), fixed((TP, 256, DIM)), vec_spec(2, DIM), vec_spec(2, DIM), vec_spec(8, DIM), vec_spec(8, DIM)],
         out_specs=[any_spec()] * 8,
         out_shape=[wide_shape(PACK, DIM), half_shape(DIM, DIM), half_shape(DIM, DIM), half_shape(192, DIM), half_shape(3, 192, DIM), half_shape(DIM, DIM), half_shape(PART, DIM), wide_shape(TP, 16, DIM)],
-        scratch_shapes=[pltpu.VMEM((2, CHUNK, DIM), WIDE), pltpu.VMEM((2, CHUNK, DIM), WIDE), pltpu.VMEM((CHUNKS, CHUNK, DIM), WIDE), pltpu.VMEM((ROWS, 3 * DIM), HALF), pltpu.VMEM((TP, 3, 192, DIM), WIDE), pltpu.VMEM((DIM, DIM), WIDE), pltpu.VMEM((TOK, DIM), WIDE), pltpu.VMEM((16, DIM), WIDE), pltpu.VMEM((2, 3, 192, DIM), WIDE), pltpu.VMEM((384, DIM), WIDE), pltpu.VMEM((2, PART, DIM), WIDE), pltpu.VMEM((3, 192, DIM), WIDE), pltpu.VMEM((192, DIM), WIDE), pltpu.VMEM((PART, DIM), WIDE), pltpu.VMEM((3, 192, DIM), HALF), pltpu.VMEM((384, DIM), HALF), pltpu.VMEM((PART, DIM), HALF), dma((CHUNKS,)), dma((CHUNKS,)), dma((3,)), dma((3,)), dma((5,)), dma((5,)), dma((3,)), dma((3,)), dma((2,)), dma((2,)), dma((3, 2)), dma((3,)), pltpu.VMEM((DIM, DIM), HALF), pltpu.VMEM((DIM, DIM), HALF), pltpu.VMEM((192, DIM), HALF), dma((4,))],
+        scratch_shapes=[pltpu.VMEM((2, CHUNK, DIM), WIDE), pltpu.VMEM((2, CHUNK, DIM), WIDE), pltpu.VMEM((CHUNKS, CHUNK, DIM), WIDE), pltpu.VMEM((GROUP, TOK, DIM), HALF), pltpu.VMEM((TP, 3, 192, DIM), HALF), pltpu.VMEM((ROWS, 3 * DIM), HALF), pltpu.VMEM((TP, 3, 192, DIM), WIDE), pltpu.VMEM((DIM, DIM), WIDE), pltpu.VMEM((TOK, DIM), WIDE), pltpu.VMEM((16, DIM), WIDE), pltpu.VMEM((2, 3, 192, DIM), WIDE), pltpu.VMEM((384, DIM), WIDE), pltpu.VMEM((2, PART, DIM), WIDE), pltpu.VMEM((3, 192, DIM), WIDE), pltpu.VMEM((192, DIM), WIDE), pltpu.VMEM((PART, DIM), WIDE), pltpu.VMEM((3, 192, DIM), HALF), pltpu.VMEM((384, DIM), HALF), pltpu.VMEM((PART, DIM), HALF), dma((CHUNKS,)), dma((CHUNKS,)), dma((3,)), dma((3,)), dma((5,)), dma((5,)), dma((3,)), dma((3,)), dma((2,)), dma((2,)), dma((3, 2)), dma((3,)), pltpu.VMEM((DIM, DIM), HALF), pltpu.VMEM((DIM, DIM), HALF), pltpu.VMEM((192, DIM), HALF), dma((3,)), dma((3,)), dma((5,))],
         compiler_params=params(3),
         cost_estimate=pl.CostEstimate(flops=100_000_000_000, bytes_accessed=80_000_000, transcendentals=12_000_000),
         name='attn_bwd',
-    )(keep_b, near_b, keep_a, near_a, keep_o, near_o, e, qkv, d_o, dx1, x, wq, ln_scale, ln_bias, dvec2, db1)
+    )(keep_b, near_b, keep_a, near_a, keep_o, near_o, e, qkv, lse, dx1, x, wq, wop, ln_scale, ln_bias, dvec2, db1)
 
 
 def finish_kernel(x2, fc1, fc2, wo, qkv, wp, pos, tiny, x2_out, fc1_out, fc2_out, wo_out, qkv_out, wp_out, pos_out, patch_b, ln_scale, ln_bias, qkv_b, out_b, fc1_b, fc2_b):
@@ -675,9 +705,9 @@
 def group_step(patches, patch_w, patch_b, pos_emb, ln_scale, ln_bias, qkv_w, qkv_b, out_w, out_b, fc1_w, fc1_b, fc2_w, fc2_b, d_out):
     wq = qkv_w.transpose(0, 2, 3, 1).reshape(3, 192, DIM)
     wo = out_w.reshape(192, DIM)
-    e, qkv, o, x1, x, dout, y, dh, wq_all, wop_all, bias_all, w1_far, w2_far, keep_a, give_a, part1, part2, dvec_n, db1_n = front(patches, d_out, wq, wo, pos_emb, fc1_w, fc2_w, patch_w, patch_b, qkv_b, fc1_b, out_b, ln_scale, ln_bias)
-    x_two, dx1, d_o, near_a, keep_o, near_o, keep_b, near_b, dvec2, db1 = mlp_far(give_a, part1, part2, x1, o, dout, y, dh, w1_far, w2_far, wop_all, bias_all, ln_scale, ln_bias, fc2_b, dvec_n, db1_n)
-    _, d_fc1_w, d_fc2_w, d_out_w, d_qkv, d_patch_w, d_pos, tiny = attn_bwd(keep_b, near_b, keep_a, near_a, keep_o, near_o, e, qkv, d_o, dx1, x, wq_all, ln_scale, ln_bias, dvec2, db1)
+    e, qkv, o, x1, x, lse, dout, y, dh, wq_all, wop_all, bias_all, w1_far, w2_far, keep_a, give_a, part1, part2, dvec_n, db1_n = front(patches, d_out, wq, wo, pos_emb, fc1_w, fc2_w, patch_w, patch_b, qkv_b, fc1_b, out_b, ln_scale, ln_bias)
+    x_two, dx1, near_a, keep_o, near_o, keep_b, near_b, dvec2, db1 = mlp_far(give_a, part1, part2, x1, o, dout, y, dh, w1_far, w2_far, bias_all, ln_scale, ln_bias, fc2_b, dvec_n, db1_n)
+    _, d_fc1_w, d_fc2_w, d_out_w, d_qkv, d_patch_w, d_pos, tiny = attn_bwd(keep_b, near_b, keep_a, near_a, keep_o, near_o, e, qkv, lse, dx1, x, wq_all, wop_all, ln_scale, ln_bias, dvec2, db1)
     x_two, d_fc1_w, d_fc2_w, d_out_w, d_qkv, d_patch_w, d_pos, d_patch_b, d_ln_scale, d_ln_bias, d_qkv_b, d_out_b, d_fc1_b, d_fc2_b = finish(x_two, d_fc1_w, d_fc2_w, d_out_w, d_qkv.reshape(576, DIM), d_patch_w, d_pos, tiny)
     d_qkv_w = d_qkv.reshape(3, 3, 64, DIM).transpose(0, 3, 1, 2)
     return (x_two, d_patch_w, d_patch_b, d_pos, d_ln_scale, d_ln_bias, d_qkv_w, d_qkv_b, d_out_w.reshape(3, 64, DIM), d_out_b, d_fc1_w, d_fc1_b, d_fc2_w, d_fc2_b)

time: 519 us -> 512 us (0.987)
  Pallas kernels: 518 us -> 511 us
where the time goes in v6:
time: 512 us
  Pallas kernels  511 us (100%)
    pallas_call x1, Pallas kernels, front(): pl.pallas_call(front_kernel, grid=(FRONT_STEPS,), in_specs=[any_spec()] *...  230 us
    pallas_call x1, Pallas kernels, attn_bwd(): pl.pallas_call(attn_bwd_kernel, grid=(STEPS,), in_specs=[any_spec()] * 6...  187 us
    pallas_call x1, Pallas kernels, mlp_far(): pl.pallas_call(mlp_far_kernel, grid=(STEPS,), in_specs=[any_spec()] * 3 +...  84.7 us

profile of v6, /device:TPU:0, one launch (start us, length us, event | category | flops | bytes accessed | tf_op | source)
XLA Modules:
  0.0 511.6 jit_solution(2896825002109134595)
XLA Ops:
  0.6 230.3 %front.1 = (bf16[16,256,768]{2,1,0:T(8,128)(2,1)}, bf16[16,256,2304]{2,1,0:T(8,128)(2,1)}, bf16[16,256,768]{2,1,0:T(8,128)(2,1)}, bf16[16,256,768]{2,1,0:T(8,128...) custom-call(bf16[64,64,768]{2,1,0:T(8,128)(2,1)} %patches.1, ...), custom_call_target="tpu_custom_call" | custom-call | flops 120000004096 | bytes 120000000 | tf_op jit(solution)/shard_map/front/pallas_call | solution.py:338
  230.9 84.7 %mlp_far.1 = (bf16[64,64,768]{2,1,0:T(8,128)(2,1)}, bf16[16,256,768]{2,1,0:T(8,128)(2,1)}, f32[1536,768]{1,0:T(8,128)}, f32[192,768]{1,0:T(8,128)}, f32[192,768]...) custom-call(f32[1536,768]{1,0:T(8,128)} %get-tuple-element.64.give, ...), custom_call_target="tpu_custom_call" | custom-call | flops 70000001024 | bytes 80000000 | tf_op jit(solution)/shard_map/mlp_far/pallas_call | solution.py:451
  315.6 187.0 %attn_bwd.1 = (f32[1728,768]{1,0:T(8,128)}, bf16[768,768]{1,0:T(8,128)(2,1)}, bf16[768,768]{1,0:T(8,128)(2,1)}, bf16[192,768]{1,0:T(8,128)(2,1)}, bf16[3,192,768...) custom-call(f32[1728,768]{1,0:T(8,128)} %get-tuple-element.78.keep_b, ...), custom_call_target="tpu_custom_call" | custom-call | flops 99999997952 | bytes 80000000 | tf_op jit(solution)/shard_map/attn_bwd/pallas_call | solution.py:656
  502.6 8.8 %finish.1 = (bf16[64,64,768]{2,1,0:T(8,128)(2,1)}, bf16[768,768]{1,0:T(8,128)(2,1)}, bf16[768,768]{1,0:T(8,128)(2,1)}, bf16[192,768]{1,0:T(8,128)(2,1)}, bf16[57...) custom-call(bf16[64,64,768]{2,1,0:T(8,128)(2,1)} %get-tuple-element., ...), custom_call_target="tpu_custom_call" | custom-call | tf_op jit(solution)/shard_map/finish/pallas_call | solution.py:694

commit v7 on v6

--- a/solution.py
+++ b/solution.py
@@ -490,7 +490,6 @@
 
     @pl.when(step == 0)
     def _():
-        dwq[...] = jnp.zeros_like(dwq)
         dwp[...] = jnp.zeros_like(dwp)
         dpos[...] = jnp.zeros_like(dpos)
         tiny[...] = jnp.zeros_like(tiny)
@@ -503,6 +502,7 @@
     def _():
         wq_copy = pltpu.make_async_copy(wq_all, wq, local.at[4])
         wq_copy.start()
+        dwq[...] = jnp.zeros_like(dwq)
         wq_copy.wait()
 
     wo = jnp.concatenate([wop[k, 0:192] for k in range(TP)], axis=0)
@@ -689,11 +689,11 @@
 
 def finish(x2, fc1, fc2, wo, qkv, wp, pos, tiny):
     arrays = (x2, fc1, fc2, wo, qkv, wp, pos)
-    specs = [pl.BlockSpec((a.shape[0] // 4,) + a.shape[1:], lambda i, n=a.ndim: (i,) + (0,) * (n - 1)) for a in arrays]
+    specs = [pl.BlockSpec((a.shape[0] // 2,) + a.shape[1:], lambda i, n=a.ndim: (i,) + (0,) * (n - 1)) for a in arrays]
     smalls = [(DIM,), (2, DIM), (2, DIM), (3, 3, 64), (DIM,), (DIM,), (DIM,)]
     return pl.pallas_call(
         finish_kernel,
-        grid=(4,),
+        grid=(2,),
         in_specs=specs + [vec_spec(TP, 16, DIM)],
         out_specs=specs + [vec_spec(*shape) for shape in smalls],
         out_shape=[jax.ShapeDtypeStruct(a.shape, a.dtype) for a in arrays] + [half_shape(*shape) for shape in smalls],

time: 512 us -> 510 us (level)
  no operation moved by 1% of the time
where the time goes in v7:
time: 510 us
  Pallas kernels  509 us (100%)
    pallas_call x1, Pallas kernels, front(): pl.pallas_call(front_kernel, grid=(FRONT_STEPS,), in_specs=[any_spec()] *...  230 us
    pallas_call x1, Pallas kernels, attn_bwd(): pl.pallas_call(attn_bwd_kernel, grid=(STEPS,), in_specs=[any_spec()] * 6...  187 us
    pallas_call x1, Pallas kernels, mlp_far(): pl.pallas_call(mlp_far_kernel, grid=(STEPS,), in_specs=[any_spec()] * 3 +...  84.7 us

profile of v7, /device:TPU:0, one launch (start us, length us, event | category | flops | bytes accessed | tf_op | source)
XLA Modules:
  0.0 510.0 jit_solution(5810589967858656554)
XLA Ops:
  0.6 230.3 %front.1 = (bf16[16,256,768]{2,1,0:T(8,128)(2,1)}, bf16[16,256,2304]{2,1,0:T(8,128)(2,1)}, bf16[16,256,768]{2,1,0:T(8,128)(2,1)}, bf16[16,256,768]{2,1,0:T(8,128...) custom-call(bf16[64,64,768]{2,1,0:T(8,128)(2,1)} %patches.1, ...), custom_call_target="tpu_custom_call" | custom-call | flops 120000004096 | bytes 120000000 | tf_op jit(solution)/shard_map/front/pallas_call | solution.py:338
  230.9 84.7 %mlp_far.1 = (bf16[64,64,768]{2,1,0:T(8,128)(2,1)}, bf16[16,256,768]{2,1,0:T(8,128)(2,1)}, f32[1536,768]{1,0:T(8,128)}, f32[192,768]{1,0:T(8,128)}, f32[192,768]...) custom-call(f32[1536,768]{1,0:T(8,128)} %get-tuple-element.64.give, ...), custom_call_target="tpu_custom_call" | custom-call | flops 70000001024 | bytes 80000000 | tf_op jit(solution)/shard_map/mlp_far/pallas_call | solution.py:451
  315.6 186.5 %attn_bwd.1 = (f32[1728,768]{1,0:T(8,128)}, bf16[768,768]{1,0:T(8,128)(2,1)}, bf16[768,768]{1,0:T(8,128)(2,1)}, bf16[192,768]{1,0:T(8,128)(2,1)}, bf16[3,192,768...) custom-call(f32[1728,768]{1,0:T(8,128)} %get-tuple-element.78.keep_b, ...), custom_call_target="tpu_custom_call" | custom-call | flops 99999997952 | bytes 80000000 | tf_op jit(solution)/shard_map/attn_bwd/pallas_call | solution.py:656
  502.2 7.6 %finish.1 = (bf16[64,64,768]{2,1,0:T(8,128)(2,1)}, bf16[768,768]{1,0:T(8,128)(2,1)}, bf16[768,768]{1,0:T(8,128)(2,1)}, bf16[192,768]{1,0:T(8,128)(2,1)}, bf16[57...) custom-call(bf16[64,64,768]{2,1,0:T(8,128)(2,1)} %get-tuple-element., ...), custom_call_target="tpu_custom_call" | custom-call | tf_op jit(solution)/shard_map/finish/pallas_call | solution.py:694

commit v8 on v7

--- a/solution.py
+++ b/solution.py
@@ -340,8 +340,8 @@
         grid=(FRONT_STEPS,),
         in_specs=[any_spec()] * 7 + [fixed((DIM, DIM)), vec_spec(DIM), vec_spec(3, 3, 64), vec_spec(DIM), vec_spec(DIM), vec_spec(2, DIM), vec_spec(2, DIM)],
         out_specs=[image_spec(DIM, FRONT), image_spec(3 * DIM, FRONT)] + [image_spec(DIM, FRONT)] * 3 + [lse_spec(FRONT)] + [image_spec(DIM, FRONT)] * 3 + [any_spec()] * 9 + [vec_spec(8, DIM), vec_spec(8, DIM)],
-        out_shape=[image_shape(DIM), image_shape(3 * DIM), image_shape(DIM), image_shape(DIM), image_shape(DIM), wide_shape(IMAGES, 16, TOK), image_shape(DIM), wide_image, wide_image, half_shape(TP, 3, 192, DIM), half_shape(TP, 256, DIM), half_shape(TP, 16, DIM), half_shape(2, DIM, LATE), half_shape(2, LATE, DIM), wide_shape(2 * DIM, DIM), wide_shape(2 * DIM, DIM), wide_shape(2, DIM, EARLY), wide_shape(2, DIM, EARLY), wide_shape(8, DIM), wide_shape(8, DIM)],
-        scratch_shapes=[pltpu.VMEM((TP, IMAGES, PART, DIM), HALF), pltpu.VMEM((TP, IMAGES, PART, DIM), HALF), pltpu.VMEM((TP, 3, 192, DIM), HALF), pltpu.VMEM((TP, 256, DIM), HALF), pltpu.VMEM((2, DIM, DIM), HALF), pltpu.VMEM((2, DIM, DIM), HALF), pltpu.VMEM((2, DIM, EARLY), HALF), pltpu.VMEM((2, EARLY, DIM), HALF), pltpu.VMEM((TP, 16, DIM), HALF), pltpu.VMEM((16, DIM), HALF), pltpu.VMEM((8, DIM), WIDE), pltpu.VMEM((2, DIM, DIM), WIDE), pltpu.VMEM((2, DIM, DIM), WIDE), pltpu.VMEM((2, DIM, EARLY), WIDE), pltpu.VMEM((2, DIM, EARLY), WIDE), dma((3, FRONT_STEPS)), dma((3, FRONT_STEPS)), dma((3, FRONT_STEPS)), dma((3, FRONT_STEPS)), dma((9, 3)), dma((9, 3)), dma((10,)), dma((6,))],
+        out_shape=[image_shape(DIM), image_shape(3 * DIM), image_shape(DIM), image_shape(DIM), image_shape(DIM), wide_shape(IMAGES, 16, TOK), image_shape(DIM), wide_image, wide_image, half_shape(TP, 3, 192, DIM), half_shape(TP, 256, DIM), half_shape(TP, 8, DIM), half_shape(2, DIM, LATE), half_shape(2, LATE, DIM), wide_shape(2 * DIM, DIM), wide_shape(2 * DIM, DIM), wide_shape(2, DIM, EARLY), wide_shape(2, DIM, EARLY), wide_shape(8, DIM), wide_shape(8, DIM)],
+        scratch_shapes=[pltpu.VMEM((TP, IMAGES, PART, DIM), HALF), pltpu.VMEM((TP, IMAGES, PART, DIM), HALF), pltpu.VMEM((TP, 3, 192, DIM), HALF), pltpu.VMEM((TP, 256, DIM), HALF), pltpu.VMEM((2, DIM, DIM), HALF), pltpu.VMEM((2, DIM, DIM), HALF), pltpu.VMEM((2, DIM, EARLY), HALF), pltpu.VMEM((2, EARLY, DIM), HALF), pltpu.VMEM((TP, 8, DIM), HALF), pltpu.VMEM((8, DIM), HALF), pltpu.VMEM((8, DIM), WIDE), pltpu.VMEM((2, DIM, DIM), WIDE), pltpu.VMEM((2, DIM, DIM), WIDE), pltpu.VMEM((2, DIM, EARLY), WIDE), pltpu.VMEM((2, DIM, EARLY), WIDE), dma((3, FRONT_STEPS)), dma((3, FRONT_STEPS)), dma((3, FRONT_STEPS)), dma((3, FRONT_STEPS)), dma((9, 3)), dma((9, 3)), dma((10,)), dma((6,))],
         compiler_params=params(0),
         cost_estimate=pl.CostEstimate(flops=120_000_000_000, bytes_accessed=120_000_000, transcendentals=18_000_000),
         name='front',
@@ -451,7 +451,7 @@
     return pl.pallas_call(
         mlp_far_kernel,
         grid=(STEPS,),
-        in_specs=[any_spec()] * 3 + [image_spec(DIM)] * 5 + [fixed((2, DIM, LATE)), fixed((2, LATE, DIM)), fixed((TP, 16, DIM)), vec_spec(2, DIM), vec_spec(2, DIM), vec_spec(DIM), vec_spec(8, DIM), vec_spec(8, DIM)],
+        in_specs=[any_spec()] * 3 + [image_spec(DIM)] * 5 + [fixed((2, DIM, LATE)), fixed((2, LATE, DIM)), fixed((TP, 8, DIM)), vec_spec(2, DIM), vec_spec(2, DIM), vec_spec(DIM), vec_spec(8, DIM), vec_spec(8, DIM)],
         out_specs=[any_spec(), image_spec(DIM)] + [any_spec()] * 5 + [vec_spec(8, DIM), vec_spec(8, DIM)],
         out_shape=[half_shape(TP * IMAGES, PART, DIM), image_shape(DIM), wide_shape(2 * DIM, DIM), wide_shape(192, DIM), wide_shape(192, DIM), wide_shape(PACK, DIM), wide_shape(PACK, DIM), wide_shape(8, DIM), wide_shape(8, DIM)],
         scratch_shapes=[pltpu.VMEM((2, TP, GROUP, PART, DIM), HALF), pltpu.VMEM((2, DIM, EARLY), WIDE), pltpu.VMEM((2, DIM, LATE), WIDE), pltpu.VMEM((2, DIM, LATE), WIDE), pltpu.VMEM((DIM, DIM), WIDE), dma((3, 2)), dma((3, STEPS)), dma((2,)), dma((7,)), dma((7,)), dma((8,))],

time: 510 us -> 510 us (level)
  no operation moved by 1% of the time
where the time goes in v8:
time: 510 us
  Pallas kernels  509 us (100%)
    pallas_call x1, Pallas kernels, front(): pl.pallas_call(front_kernel, grid=(FRONT_STEPS,), in_specs=[any_spec()] *...  230 us
    pallas_call x1, Pallas kernels, attn_bwd(): pl.pallas_call(attn_bwd_kernel, grid=(STEPS,), in_specs=[any_spec()] * 6...  187 us
    pallas_call x1, Pallas kernels, mlp_far(): pl.pallas_call(mlp_far_kernel, grid=(STEPS,), in_specs=[any_spec()] * 3 +...  84.7 us

profile of v8, /device:TPU:0, one launch (start us, length us, event | category | flops | bytes accessed | tf_op | source)
XLA Modules:
  0.0 509.6 jit_solution(7962027566624828037)
XLA Ops:
  0.6 229.9 %front.1 = (bf16[16,256,768]{2,1,0:T(8,128)(2,1)}, bf16[16,256,2304]{2,1,0:T(8,128)(2,1)}, bf16[16,256,768]{2,1,0:T(8,128)(2,1)}, bf16[16,256,768]{2,1,0:T(8,128...) custom-call(bf16[64,64,768]{2,1,0:T(8,128)(2,1)} %patches.1, ...), custom_call_target="tpu_custom_call" | custom-call | flops 120000004096 | bytes 120000000 | tf_op jit(solution)/shard_map/front/pallas_call | solution.py:338
  230.6 84.7 %mlp_far.1 = (bf16[64,64,768]{2,1,0:T(8,128)(2,1)}, bf16[16,256,768]{2,1,0:T(8,128)(2,1)}, f32[1536,768]{1,0:T(8,128)}, f32[192,768]{1,0:T(8,128)}, f32[192,768]...) custom-call(f32[1536,768]{1,0:T(8,128)} %get-tuple-element.64.give, ...), custom_call_target="tpu_custom_call" | custom-call | flops 70000001024 | bytes 80000000 | tf_op jit(solution)/shard_map/mlp_far/pallas_call | solution.py:451
  315.3 186.5 %attn_bwd.1 = (f32[1728,768]{1,0:T(8,128)}, bf16[768,768]{1,0:T(8,128)(2,1)}, bf16[768,768]{1,0:T(8,128)(2,1)}, bf16[192,768]{1,0:T(8,128)(2,1)}, bf16[3,192,768...) custom-call(f32[1728,768]{1,0:T(8,128)} %get-tuple-element.78.keep_b, ...), custom_call_target="tpu_custom_call" | custom-call | flops 99999997952 | bytes 80000000 | tf_op jit(solution)/shard_map/attn_bwd/pallas_call | solution.py:656
  501.8 7.6 %finish.1 = (bf16[64,64,768]{2,1,0:T(8,128)(2,1)}, bf16[768,768]{1,0:T(8,128)(2,1)}, bf16[768,768]{1,0:T(8,128)(2,1)}, bf16[192,768]{1,0:T(8,128)(2,1)}, bf16[57...) custom-call(bf16[64,64,768]{2,1,0:T(8,128)(2,1)} %get-tuple-element., ...), custom_call_target="tpu_custom_call" | custom-call | tf_op jit(solution)/shard_map/finish/pallas_call | solution.py:694
